TPU v7x, 32 devices: a whole 2x2x4 slice. The times are simulated.
32 devices in a mesh: rep: 2 (over x), kv2: 4 (over z), kv: 4 (over y, core).
Axes of the slice: x: 2, y: 2, z: 4, core: 2. Of those that a mesh axis runs over, the one named last changes fastest.
Arguments:
- x_embed: bfloat16 [2, 384, 3072], P(None, ('rep', 'kv2', 'kv')), parts along dimension 1
- w_query: bfloat16 [2, 3072, 3072], replicated
- w_key: bfloat16 [2, 3072, 1024], replicated
- w_value: bfloat16 [2, 3072, 1024], replicated
- w_out: bfloat16 [2, 3072, 3072], replicated
- w_up: bfloat16 [2, 3072, 8192], replicated
- w_down: bfloat16 [2, 8192, 3072], replicated
- k_pool: bfloat16 [1920, 2, 32, 8, 128], P(('rep', 'kv2', 'kv')), parts along dimension 0
- v_pool: bfloat16 [1920, 2, 32, 8, 128], P(('rep', 'kv2', 'kv')), parts along dimension 0
- old_table: int32 [384, 2], P(('rep', 'kv2', 'kv')), parts along dimension 0
- seq_len: int32 [384], P(('rep', 'kv2', 'kv')), parts along dimension 0
- src_slot: int32 [384], P(('rep', 'kv2', 'kv')), parts along dimension 0
- dst_slot: int32 [384], P(('rep', 'kv2', 'kv')), parts along dimension 0
Outputs:
- output 1: bfloat16 [2, 384, 3072], P(None, ('rep', 'kv2', 'kv')), parts along dimension 1
- output 2: bfloat16 [1920, 2, 32, 8, 128], P(('rep', 'kv2', 'kv')), parts along dimension 0
- output 3: bfloat16 [1920, 2, 32, 8, 128], P(('rep', 'kv2', 'kv')), parts along dimension 0
There are 2 independent parts. A program takes and returns all parts, laid end to end along the dimension named above; an argument that names none is the same for every part.
All inputs are finite; a program needn't handle non-finite values.
Results may differ from a plain program's by a relative error of at most 0.0137214.
Values are sent between devices in bfloat16 or wider.
A program may use at most 1.25 GiB of HBM per device.

v0:
```python
import jax
import jax.numpy as jnp
from jax import lax
from jax.sharding import PartitionSpec as P


def solution(mesh):
    n_rows = mesh.shape['kv2']
    n_cols = mesh.shape['kv']
    dev_axes = ('rep', 'kv2', 'kv')
    seq_spec = P(None, dev_axes, None)
    pool_spec = P(dev_axes, None, None, None, None)
    table_spec = P(dev_axes, None)
    vec_spec = P(dev_axes)
    full_spec = P()

    def per_device(x_embed, w_query, w_key, w_value, w_out, w_up, w_down, k_pool, v_pool, old_table, seq_len, src_slot, dst_slot):
        n_slots, layers, page, kv_heads, head_dim = k_pool.shape
        heads = w_query.shape[2] // head_dim
        q_group = heads // kv_heads
        seq_dev = x_embed.shape[1]
        n_pages = old_table.shape[1]
        row_seqs = seq_dev * n_cols
        slot_base = (lax.axis_index('kv2') * n_cols + lax.axis_index('kv')) * n_slots
        src_all = lax.all_gather(src_slot, ('kv2', 'kv'), tiled=True)
        dst_all = lax.all_gather(dst_slot, ('kv2', 'kv'), tiled=True)
        src_local = src_slot - slot_base
        out_pages = jnp.stack([k_pool[src_local], v_pool[src_local]], axis=1)
        in_pages = lax.all_gather(out_pages, ('kv2', 'kv'), tiled=True)
        dst_local = dst_all - slot_base
        dst_local = jnp.where((dst_local >= 0) & (dst_local < n_slots), dst_local, n_slots)
        k_pool = k_pool.at[dst_local].set(in_pages[:, 0], mode='drop')
        v_pool = v_pool.at[dst_local].set(in_pages[:, 1], mode='drop')
        row_table = lax.all_gather(old_table, 'kv', tiled=True)
        row_len = lax.all_gather(seq_len, 'kv', tiled=True)
        slot_move = jnp.full((n_rows * n_cols * n_slots,), -1, jnp.int32).at[src_all].set(jnp.arange(src_all.shape[0], dtype=jnp.int32))
        move_idx = slot_move[jnp.maximum(row_table, 0)]
        new_table = jnp.where((row_table >= 0) & (move_idx >= 0), dst_all[jnp.maximum(move_idx, 0)], row_table)
        table_local = new_table - slot_base
        owned = (new_table >= 0) & (table_local >= 0) & (table_local < n_slots)
        cell_ids = jnp.arange(row_seqs * n_pages, dtype=jnp.int32).reshape(row_seqs, n_pages)
        slot_cell = jnp.full((n_slots,), -1, jnp.int32).at[jnp.where(owned, table_local, n_slots)].set(cell_ids, mode='drop')
        slot_used = slot_cell >= 0
        seq_of_slot = jnp.where(slot_used, slot_cell // n_pages, 0)
        seg_ids = jnp.where(slot_used, seq_of_slot, row_seqs)
        slot_first = jnp.where(slot_used, slot_cell % n_pages, 0) * page
        tok_off = jnp.arange(page)
        row_ids = jnp.arange(row_seqs)
        q_scale = head_dim ** -0.5
        step_outs = []
        for step_idx in range(2):
            cur_pos = row_len + step_idx
            w_slot = new_table[row_ids, cur_pos // page] - slot_base
            w_slot = jnp.where((w_slot >= 0) & (w_slot < n_slots), w_slot, n_slots)
            w_off = cur_pos % page
            visible = slot_used[:, None] & (tok_off[None, :] <= (cur_pos[seq_of_slot] - slot_first)[:, None])
            hidden = x_embed[step_idx]
            for layer_idx in range(layers):
                query = jnp.dot(hidden, w_query[layer_idx], preferred_element_type=jnp.float32).astype(jnp.bfloat16)
                k_new = jnp.dot(hidden, w_key[layer_idx], preferred_element_type=jnp.float32).astype(jnp.bfloat16)
                v_new = jnp.dot(hidden, w_value[layer_idx], preferred_element_type=jnp.float32).astype(jnp.bfloat16)
                q_row = lax.all_gather(query, 'kv', tiled=True)
                kv_row = lax.all_gather(jnp.stack([k_new, v_new]), 'kv', axis=1, tiled=True).reshape(2, row_seqs, kv_heads, head_dim)
                k_pool = k_pool.at[w_slot, layer_idx, w_off].set(kv_row[0], mode='drop')
                v_pool = v_pool.at[w_slot, layer_idx, w_off].set(kv_row[1], mode='drop')
                q_slot = q_row[seq_of_slot].reshape(n_slots, kv_heads, q_group, head_dim)
                scores = jnp.einsum('sgrd,spgd->sgrp', q_slot, k_pool[:, layer_idx], preferred_element_type=jnp.float32) * q_scale
                scores = jnp.where(visible[:, None, None, :], scores, -1e30)
                slot_max = scores.max(axis=-1)
                expo = jnp.exp(scores - slot_max[..., None])
                slot_out = jnp.einsum('sgrp,spgd->sgrd', expo.astype(jnp.bfloat16), v_pool[:, layer_idx], preferred_element_type=jnp.float32)
                seq_max = jnp.full((row_seqs, kv_heads, q_group), -1e30, jnp.float32).at[seg_ids].max(slot_max, mode='drop')
                slot_w = jnp.exp(jnp.where(slot_used[:, None, None], slot_max - seq_max[seq_of_slot], -1e30))
                seq_sum = jax.ops.segment_sum(slot_w * expo.sum(axis=-1), seg_ids, num_segments=row_seqs)
                seq_out = jax.ops.segment_sum(slot_w[..., None] * slot_out, seg_ids, num_segments=row_seqs)
                partial_res = jnp.concatenate([seq_max[..., None], seq_sum[..., None], seq_out], axis=-1)
                home = lax.all_to_all(partial_res, 'kv', 0, 0, tiled=True).reshape(n_cols, seq_dev, kv_heads, q_group, head_dim + 2)
                scale_w = jnp.exp(home[..., 0] - home[..., 0].max(axis=0))
                total = (scale_w * home[..., 1]).sum(axis=0)
                attn_out = ((scale_w[..., None] * home[..., 2:]).sum(axis=0) / total[..., None]).astype(jnp.bfloat16).reshape(seq_dev, heads * head_dim)
                hidden = (hidden.astype(jnp.float32) + jnp.dot(attn_out, w_out[layer_idx], preferred_element_type=jnp.float32)).astype(jnp.bfloat16)
                up_act = jax.nn.gelu(jnp.dot(hidden, w_up[layer_idx], preferred_element_type=jnp.float32)).astype(jnp.bfloat16)
                hidden = (hidden.astype(jnp.float32) + jnp.dot(up_act, w_down[layer_idx], preferred_element_type=jnp.float32)).astype(jnp.bfloat16)
            step_outs.append(hidden)
        return jnp.stack(step_outs), k_pool, v_pool

    return jax.shard_map(per_device, mesh=mesh, in_specs=(seq_spec, full_spec, full_spec, full_spec, full_spec, full_spec, full_spec, pool_spec, pool_spec, table_spec, vec_spec, vec_spec, vec_spec), out_specs=(seq_spec, pool_spec, pool_spec), check_vma=False)
```

profile of v0, /device:TPU:0, one launch (start us, length us, event | category | flops | bytes accessed | tf_op | source)
XLA Modules:
  0.0 875.9 jit_solution(10043571265814189860)
XLA Ops:
  7.2 7.6 copy.503
  28.3 6.1 all-gather
  36.4 13.1 %all-reduce.3 = (s32[192]{0:T(256)S(1)}, s32[192]{0:T(256)S(1)}) all-reduce(s32[192]{0:T(256)S(1)} %dynamic-update-slice.1, s32[192]{0:T(256)S(1)} %dynamic-update-slice), channel_id=1, replica_groups=mesh['rep'=2,'kv2'=4,'kv'=4] {'kv2','kv'}, use_global_device_ids=true, to_apply=%add.1 | all-reduce | flops 384 | bytes 3072
  72.1 6.8 all_gather.45
  79.8 7.7 fusion.155
  87.5 9.3 %all-gather.1 = bf16[4,12,3072]{2,1,0:T(8,128)(2,1)S(1)} all-gather(bf16[1,12,3072]{2,1,0:T(8,128)(2,1)S(1)} %fusion.155), channel_id=1, replica_groups=mesh['rep'=2,'kv2'=4,'kv'=4] {'kv'}, dimensions={0}, use_global_device_ids=true | all-gather | bytes 368640 | tf_op jit(solution)/shard_map/all_gather | solution.py:62
  107.1 7.7 fusion.152
  114.8 166.1 %all-gather.7.cloned.1.call-done = bf16[192,2,2,32,8,128]{5,4,3,2,0,1:T(8,128)(2,1)} async-done(((bf16[12,2,2,32,8,128]{5,4,3,2,0,1:T(8,128)(2,1)}), bf16[192,2,2,32,8,128]{5,4,3,2,0,1:T(8,128)(2,1)}) %all-gather.7.cloned.1.call-update) | async-done | bytes 50331664 | tf_op jit(solution)/shard_map/all_gather | solution.py:29
  280.9 33.3 %slice_bitcast_fusion.1 = (bf16[192,2,32,8,128]{4,3,2,1,0:T(8,128)(2,1)}, bf16[192,2,32,8,128]{4,3,2,1,0:T(8,128)(2,1)}) fusion(bf16[192,2,2,32,8,128]{5,4,3,2,0,1:T(8,128)(2,1)} %all-gather.7.cloned.1.call-done), kind=kLoop, calls=%fused_computation.65 | loop fusion | bytes 100663296 | tf_op jit(solution)/shard_map/squeeze | solution.py:32
  314.2 56.6 %scatter_fusion = bf16[60,2,32,8,128]{4,3,2,1,0:T(8,128)(2,1)} fusion(bf16[60,2,32,8,128]{4,3,2,1,0:T(8,128)(2,1)} %copy.503, s32[192]{0:T(256)S(1)} %compare_select_fusion, bf16[192,2,32,8,128]{4,3,2,1,0:T(8,128)(2,1)} %get-tuple-element.50), kind=kCustom, calls=%fused_computation.18 | custom fusion | bytes 75498240 | tf_op jit(solution)/shard_map/scatter | solution.py:32
  370.7 5.8 scatter_fusion.1
  387.0 56.4 %scatter_fusion.4 = bf16[60,2,32,8,128]{4,3,2,1,0:T(8,128)(2,1)} fusion(bf16[60,2,32,8,128]{4,3,2,1,0:T(8,128)(2,1)} %copy.504, s32[192]{0:T(256)S(1)} %compare_select_fusion, bf16[192,2,32,8,128]{4,3,2,1,0:T(8,128)(2,1)} %get-tuple-element.51), kind=kCustom, calls=%fused_computation.22 | custom fusion | bytes 75498240 | tf_op jit(solution)/shard_map/scatter | solution.py:33
  466.8 17.4 %all_gather.49 = bf16[2,48,1024]{2,0,1:T(2,128)(2,1)S(1)} all-gather(bf16[2,12,1024]{2,0,1:T(2,128)(2,1)S(1)} %copy.351), channel_id=1, replica_groups=mesh['rep'=2,'kv2'=4,'kv'=4] {'kv'}, dimensions={1}, use_global_device_ids=true | all-gather | bytes 245760 | tf_op jit(solution)/shard_map/all_gather | solution.py:63
  485.1 6.6 all-gather.3
  496.6 7.8 fusion.125
  504.3 32.8 %fusion.113 = bf16[12,3072]{1,0:T(8,128)(2,1)S(1)} fusion(bf16[2,8192,3072]{2,1,0:T(8,128)(2,1)} %param.19, bf16[12,3072]{1,0:T(8,128)(2,1)S(1)} %fusion.125, bf16[2,3072,8192]{2,1,0:T(8,128)(2,1)} %param.18), kind=kOutput, calls=%fused_computation.141 | convolution fusion | flops 1208954880 | bytes 100933632 | tf_op jit(solution)/shard_map/dot_general | solution.py:83
  544.5 7.7 fusion.149
  558.8 5.8 scatter_fusion.7
  569.1 6.6 all-gather.2
  582.1 6.3 scatter_fusion.12
  605.9 5.8 scatter_fusion.10
  665.4 7.7 fusion.122
  673.2 32.8 %fusion.110 = bf16[12,3072]{1,0:T(8,128)(2,1)S(1)} fusion(bf16[2,8192,3072]{2,1,0:T(8,128)(2,1)} %param.19, bf16[12,3072]{1,0:T(8,128)(2,1)S(1)} %fusion.122, bf16[2,3072,8192]{2,1,0:T(8,128)(2,1)} %param.18), kind=kOutput, calls=%fused_computation.140 | convolution fusion | flops 1208954880 | bytes 100933632 | tf_op jit(solution)/shard_map/dot_general | solution.py:83
  713.4 7.7 fusion.146
  721.2 5.9 all_gather.51
  728.0 5.8 scatter_fusion.17
  738.2 6.8 all-gather.4
  755.1 7.8 fusion.119
  768.1 5.8 scatter_fusion.20
  791.7 32.8 %fusion.140 = bf16[1,12,3072]{2,1,0:T(8,128)(2,1)S(1)} fusion(bf16[2,8192,3072]{2,1,0:T(8,128)(2,1)} %param.19, bf16[12,3072]{1,0:T(8,128)(2,1)S(1)} %fusion.119, bf16[2,3072,8192]{2,1,0:T(8,128)(2,1)} %param.18), kind=kOutput, calls=%fused_computation.150 | convolution fusion | flops 1208954880 | bytes 100933632 | tf_op jit(solution)/shard_map/dot_general | solution.py:83
  827.2 7.7 fusion.116
  834.9 32.8 %fusion.143 = bf16[1,12,3072]{2,1,0:T(8,128)(2,1)S(1)} fusion(bf16[2,8192,3072]{2,1,0:T(8,128)(2,1)} %param.19, bf16[12,3072]{1,0:T(8,128)(2,1)S(1)} %fusion.116, bf16[2,3072,8192]{2,1,0:T(8,128)(2,1)} %param.18), kind=kOutput, calls=%fused_computation.151 | convolution fusion | flops 1208954880 | bytes 100933632 | tf_op jit(solution)/shard_map/dot_general | solution.py:83
  (283 shorter events, 231.7 us)
Async XLA Ops:
  7.2 273.7 %all-gather.7.cloned.1.call-start = ((), (), s32[]{:S(2)}) async-start(), calls=%async_computation.4 | async-start | bytes 53477376 | tf_op jit(solution)/shard_map/all_gather | solution.py:29
  7.2 7.6 copy-start
  14.9 3.2 copy-start.12
  18.1 10.2 %copy-start.11 = (s32[12,2]{0,1:T(2,128)S(1)}, s32[12,2]{0,1:T(2,128)}, u32[]{:S(2)}) copy-start(s32[12,2]{0,1:T(2,128)} %param.22) | copy-start | bytes 292
  18.1 16.5 %copy-start.16 = (u32[32]{0:T(128)S(1)}, u32[32]{0:T(128)}, u32[]{:S(2)}) copy-start(u32[32]{0:T(128)} %constant.358) | copy-start | bytes 388
  18.1 18.0 %copy-start.13 = (s32[12]{0:T(128)S(1)}, s32[12]{0:T(128)}, u32[]{:S(2)}) copy-start(s32[12]{0:T(128)} %param.25) | copy-start | bytes 148
  51.7 2.1 copy-start.15
  51.7 4.3 copy-start.14
  51.7 12.6 %copy-start.6 = (bf16[2,12,3072]{2,0,1:T(2,128)(2,1)S(1)}, bf16[2,12,3072]{2,0,1:T(2,128)(2,1)}, u32[]{:S(2)}) copy-start(bf16[2,12,3072]{2,0,1:T(2,128)(2,1)} %param.13) | copy-start | bytes 442372
  64.5 42.6 %copy-start.8 = (bf16[1,12,3072]{2,0,1:T(2,128)(2,1)}, bf16[1,12,3072]{2,0,1:T(2,128)(2,1)S(1)}, u32[]{:S(2)}) copy-start(bf16[1,12,3072]{2,0,1:T(2,128)(2,1)S(1)} %get-tuple-element.64) | copy-start | bytes 221188
  463.2 30.7 %all-to-all-start = ((f32[48,8,3,130]{3,1,2,0:T(8,128)}), f32[48,8,3,130]{3,1,2,0:T(8,128)S(1)}, u32[]{:S(2)}, u32[]{:S(2)}) async-start(f32[48,8,3,130]{3,1,2,0:T(8,128)} %pad_maximum_fusion.1), calls=%async_computation | async-start | bytes 2359296 | tf_op jit(solution)/shard_map/all_to_all | solution.py:77
  569.1 13.0 %copy-start.2 = (s32[48]{0:T(128)S(1)}, s32[48]{0:T(128)}, u32[]{:S(2)}) copy-start(s32[48]{0:T(128)} %get-tuple-element.67) | copy-start | bytes 580
  577.1 13.7 %copy-start.7 = (bf16[60,8,3,128]{3,2,1,0:T(4,128)(2,1)S(1)}, bf16[60,8,3,128]{3,2,1,0:T(4,128)(2,1)}, u32[]{:S(2)}) copy-start(bf16[60,8,3,128]{3,2,1,0:T(4,128)(2,1)} %reshape.282) | copy-start | bytes 1105924
  577.1 13.7 %copy-start.10 = (pred[60,32]{1,0:T(8,128)(4,1)S(1)}, pred[60,32]{1,0:T(8,128)(4,1)}, u32[]{:S(2)}) copy-start(pred[60,32]{1,0:T(8,128)(4,1)} %get-tuple-element.72) | copy-start | bytes 5764
  581.5 19.1 %copy-start.3 = (f32[60,8,3,32]{3,2,1,0:T(4,128)}, f32[60,8,3,32]{3,2,1,0:T(4,128)S(1)}, u32[]{:S(2)}) copy-start(f32[60,8,3,32]{3,2,1,0:T(4,128)S(1)} %get-tuple-element.79) | copy-start | bytes 552964
  611.7 13.6 %copy-start.5 = (f32[60,8,3,32]{3,2,1,0:T(4,128)S(1)}, f32[60,8,3,32]{3,2,1,0:T(4,128)}, u32[]{:S(2)}) copy-start(f32[60,8,3,32]{3,2,1,0:T(4,128)} %get-tuple-element.81) | copy-start | bytes 552964
  638.3 19.1 %all-to-all-start.2 = ((f32[48,8,3,130]{3,1,2,0:T(8,128)}), f32[48,8,3,130]{3,1,2,0:T(8,128)S(1)}, u32[]{:S(2)}, u32[]{:S(2)}) async-start(f32[48,8,3,130]{3,1,2,0:T(8,128)} %pad_maximum_fusion.3), calls=%async_computation.2 | async-start | bytes 2359296 | tf_op jit(solution)/shard_map/all_to_all | solution.py:77
  648.6 16.8 %copy-start.9 = (bf16[1,12,3072]{2,0,1:T(2,128)(2,1)S(1)}, bf16[1,12,3072]{2,0,1:T(2,128)(2,1)}, u32[]{:S(2)}) copy-start(bf16[1,12,3072]{2,0,1:T(2,128)(2,1)} %copy-done.8) | copy-start | bytes 221188
  657.5 94.9 %all-to-all-start.1 = ((f32[48,8,3,130]{3,1,2,0:T(8,128)}), f32[48,8,3,130]{3,1,2,0:T(8,128)S(1)}, u32[]{:S(2)}, u32[]{:S(2)}) async-start(f32[48,8,3,130]{3,1,2,0:T(8,128)} %pad_maximum_fusion.2), calls=%async_computation.1 | async-start | bytes 2359296 | tf_op jit(solution)/shard_map/all_to_all | solution.py:77
  713.4 14.6 %copy-start.1 = (s32[48]{0:T(128)S(1)}, s32[48]{0:T(128)}, u32[]{:S(2)}) copy-start(s32[48]{0:T(128)} %get-tuple-element.66) | copy-start | bytes 580
  755.1 11.5 %copy-start.4 = (f32[60,8,3,32]{3,2,1,0:T(4,128)S(1)}, f32[60,8,3,32]{3,2,1,0:T(4,128)}, u32[]{:S(2)}) copy-start(f32[60,8,3,32]{3,2,1,0:T(4,128)} %get-tuple-element.83) | copy-start | bytes 552964
  787.9 36.6 %all-to-all-start.3 = ((f32[48,8,3,130]{3,1,2,0:T(8,128)}), f32[48,8,3,130]{3,1,2,0:T(8,128)S(1)}, u32[]{:S(2)}, u32[]{:S(2)}) async-start(f32[48,8,3,130]{3,1,2,0:T(8,128)} %pad_maximum_fusion.4), calls=%async_computation.3 | async-start | bytes 2359296 | tf_op jit(solution)/shard_map/all_to_all | solution.py:77
Sparse Core Ops, SparseCore 0:
  28.4 252.4 all-gather.6
where the time goes:
time: 887 us; the launch traced here: 876 us
  local copies, waits for them, and re-layouts  285 us (32%)
  matrix products  248 us (28%)
  waiting for transfers between devices  166 us (19%)
  blocking collectives  88.6 us (10%)
  other arithmetic  57.4 us (6%)
  between operations  17 us (2%)
  starting transfers between devices  14.4 us (2%)
    all_gather x1, waiting for transfers between devices, per_device(): in_pages = lax.all_gather(out_pages, ('kv2', 'kv'), tiled=True)  166 us
    dot_general x4, matrix products, per_device(): jnp.dot(up_act, w_down[layer_idx], preferred_element_type=jnp.float32)  131 us
    scatter x1, local copies, waits for them, and re-layouts, per_device(): k_pool = k_pool.at[dst_local].set(in_pages[:, 0], mode='drop')  56.6 us
    scatter x1, local copies, waits for them, and re-layouts, per_device(): v_pool = v_pool.at[dst_local].set(in_pages[:, 1], mode='drop')  56.4 us
    all_gather x4, blocking collectives, per_device(): lax.all_gather(jnp.stack([k_new, v_new]), 'kv', axis=1, tiled=True)  35.7 us
    squeeze x1, local copies, waits for them, and re-layouts, per_device(): k_pool = k_pool.at[dst_local].set(in_pages[:, 0], mode='drop')  33.3 us
    dot_general x4, matrix products, per_device(): jnp.dot(attn_out, w_out[layer_idx], preferred_element_type=jnp.float32)  31.1 us
    dot_general x4, matrix products, per_device(): jnp.dot(hidden, w_query[layer_idx], preferred_element_type=jnp.float32)  30.9 us
  transfers between devices with their start and end apart: 5, of which 2 were waited for; matrix products, arithmetic and copies ran while one was open for 20% of the time, Pallas kernels for 0%

commit v1 on v0

v1 whole, which is shorter than its diff:
```python
import functools

import jax
import jax.numpy as jnp
from jax import lax
from jax.experimental import pallas as pl
from jax.experimental.pallas import tpu as pltpu
from jax.sharding import PartitionSpec as P

MESH_ID = pl.DeviceIdType.MESH
NEG = -1e30
UNROLL = 4


def take_pages(rows, k_rows, v_rows, layers):
    m = rows.shape[0]
    tail = k_rows.shape[1:]

    def body(rows_ref, k_in, v_in, *rest):
        outs, (buf, isem, osem) = rest[:layers], rest[layers:]
        ins, puts = [], []
        for layer in range(layers):
            for i in range(m):
                for which, ref in enumerate((k_in, v_in)):
                    j = 2 * i + which
                    cp = pltpu.make_async_copy(ref.at[rows_ref[i] + layer], buf.at[layer, j], isem.at[layer, j])
                    cp.start()
                    ins.append(cp)
        for layer in range(layers):
            for cp in ins[layer * 2 * m:(layer + 1) * 2 * m]:
                cp.wait()
            cp = pltpu.make_async_copy(buf.at[layer], outs[layer], osem.at[layer])
            cp.start()
            puts.append(cp)
        for cp in puts:
            cp.wait()

    any_spec = pl.BlockSpec(memory_space=pl.ANY)
    return pl.pallas_call(
        body,
        out_shape=[jax.ShapeDtypeStruct((2 * m,) + tail, k_rows.dtype)] * layers,
        in_specs=[pl.BlockSpec(memory_space=pltpu.SMEM), any_spec, any_spec],
        out_specs=[any_spec] * layers,
        scratch_shapes=[pltpu.VMEM((layers, 2 * m) + tail, k_rows.dtype),
                        pltpu.SemaphoreType.DMA((layers, 2 * m)), pltpu.SemaphoreType.DMA((layers,))],
        name="take_pages",
    )(rows, k_rows, v_rows)


def enter(axis, n, me):
    barrier = pltpu.get_barrier_semaphore()
    for d in range(1, n):
        pl.semaphore_signal(barrier, inc=1, device_id={axis: lax.rem(me + d, n)}, device_id_type=MESH_ID)
    pl.semaphore_wait(barrier, n - 1)


def gather_rows(x, axis, n, cid):
    def body(x_ref, o_ref, send_sem, recv_sem):
        me = lax.axis_index(axis)
        enter(axis, n, me)
        copies = []
        for d in range(1, n):
            cp = pltpu.make_async_remote_copy(
                src_ref=x_ref, dst_ref=o_ref.at[me], send_sem=send_sem.at[d], recv_sem=recv_sem.at[d],
                device_id={axis: lax.rem(me + d, n)}, device_id_type=MESH_ID)
            cp.start()
            copies.append(cp)
        o_ref[me] = x_ref[...]
        for cp in copies:
            cp.wait()

    return pl.pallas_call(
        body,
        out_shape=jax.ShapeDtypeStruct((n,) + x.shape, x.dtype),
        in_specs=[pl.BlockSpec(memory_space=pltpu.VMEM)],
        out_specs=pl.BlockSpec(memory_space=pltpu.VMEM),
        scratch_shapes=[pltpu.SemaphoreType.DMA((n,)), pltpu.SemaphoreType.DMA((n,))],
        compiler_params=pltpu.CompilerParams(collective_id=cid, has_side_effects=True),
        name="gather_rows",
    )(x)


def combine(acc, ml, axis, n, cid):
    rows, r, hd = acc.shape
    b = rows // n

    def body(acc_ref, ml_ref, o_ref, acc_in, ml_in, send_sem, recv_sem, send_ml, recv_ml):
        me = lax.axis_index(axis)
        enter(axis, n, me)
        copies = []
        for d in range(1, n):
            peer = lax.rem(me + d, n)
            for src, dst, ss, rs in (
                (acc_ref.at[pl.ds(peer * b, b)], acc_in.at[d], send_sem, recv_sem),
                (ml_ref, ml_in.at[d], send_ml, recv_ml),
            ):
                cp = pltpu.make_async_remote_copy(
                    src_ref=src, dst_ref=dst, send_sem=ss.at[d], recv_sem=rs.at[d],
                    device_id={axis: peer}, device_id_type=MESH_ID)
                cp.start()
                copies.append(cp)
        for cp in copies:
            cp.wait()
        lane = lax.broadcasted_iota(jnp.int32, (r, ml_ref.shape[2]), 1)
        for i in range(b):
            sel = lane == me * b + i
            pick = lambda t: jnp.sum(jnp.where(sel, t, 0.0), axis=1, keepdims=True)
            ms = [pick(ml_ref[0])] + [pick(ml_in[d, 0]) for d in range(1, n)]
            ls = [pick(ml_ref[1])] + [pick(ml_in[d, 1]) for d in range(1, n)]
            top = functools.reduce(jnp.maximum, ms)
            ws = [jnp.exp(m - top) for m in ms]
            den = sum(w * l for w, l in zip(ws, ls))
            num = ws[0] * acc_ref[me * b + i]
            for d in range(1, n):
                num += ws[d] * acc_in[d, i]
            o_ref[i] = (num / den).astype(o_ref.dtype)

    return pl.pallas_call(
        body,
        out_shape=jax.ShapeDtypeStruct((b, r, hd), jnp.bfloat16),
        in_specs=[pl.BlockSpec(memory_space=pltpu.VMEM)] * 2,
        out_specs=pl.BlockSpec(memory_space=pltpu.VMEM),
        scratch_shapes=[
            pltpu.VMEM((n, b, r, hd), jnp.float32),
            pltpu.VMEM((n,) + ml.shape, jnp.float32),
            pltpu.SemaphoreType.DMA((n,)), pltpu.SemaphoreType.DMA((n,)),
            pltpu.SemaphoreType.DMA((n,)), pltpu.SemaphoreType.DMA((n,)),
        ],
        compiler_params=pltpu.CompilerParams(collective_id=cid, has_side_effects=True),
        name="combine",
    )(acc, ml)


def attend(info, counts, qkv, k_src, v_src, prev_pools, state, layer, part, n_slots, layers, page, kvh, q_group, hd):
    prow = page * kvh
    qr = 2 * kvh * q_group
    n_seq = qkv.shape[0]
    scale = hd ** -0.5
    aliased = prev_pools is not None
    carried = state is not None

    def body(info_ref, cnt_ref, qkv_ref, k_in, v_in, *rest):
        if aliased:
            rest = rest[2:]
        if carried:
            acc_prev, ml_prev = rest[:2]
            rest = rest[2:]
        k_out, v_out, acc_ref, ml_ref, kbuf, vbuf, isem, osem = rest
        lo = cnt_ref[2 * part - 1] if part else 0
        mid = cnt_ref[2 * part]
        hi = cnt_ref[2 * part + 1]

        def loads(i):
            if part:
                k_at, v_at = info_ref[3, i] * 2, info_ref[3, i] * 2 + 1
            else:
                k_at = v_at = info_ref[0, i] * layers + layer
            return (pltpu.make_async_copy(k_in.at[k_at], kbuf.at[i], isem.at[0, i]),
                    pltpu.make_async_copy(v_in.at[v_at], vbuf.at[i], isem.at[1, i]))

        def stores(i):
            slot = info_ref[0, i]
            return (pltpu.make_async_copy(kbuf.at[i], k_out.at[slot * layers + layer], osem.at[0, i]),
                    pltpu.make_async_copy(vbuf.at[i], v_out.at[slot * layers + layer], osem.at[1, i]))

        @pl.loop(lo, hi)
        def _(i):
            for cp in loads(i):
                cp.start()

        if carried:
            acc_ref[...] = acc_prev[...]
            ml_ref[...] = ml_prev[...]
        else:
            acc_ref[...] = jnp.zeros_like(acc_ref)
            ml_ref[0] = jnp.full(ml_ref.shape[1:], NEG, jnp.float32)
            ml_ref[1] = jnp.zeros(ml_ref.shape[1:], jnp.float32)

        col = lax.broadcasted_iota(jnp.int32, (qr, prow), 1)
        row = lax.broadcasted_iota(jnp.int32, (qr, prow), 0)
        late = (row >= kvh * q_group).astype(jnp.int32)
        head_ok = lax.rem(col, kvh) == (row - late * (kvh * q_group)) // q_group
        need = col // kvh - late
        need = jnp.where(head_ok, need, 1 << 20)
        lane = lax.broadcasted_iota(jnp.int32, ml_ref.shape[1:], 1)
        wrow = lax.broadcasted_iota(jnp.int32, (4 * kvh, hd), 0) // kvh

        @pl.loop(0, (mid - lo + UNROLL - 1) // UNROLL)
        def _(g):
            base = lo + g * UNROLL
            idx, seqs, offs = [], [], []
            for u in range(UNROLL):
                i = base + u
                live = i < mid
                j = jnp.minimum(i, mid - 1)
                idx.append(j)
                seqs.append(jnp.where(live, info_ref[1, j], n_seq))
                offs.append(info_ref[2, j])

                @pl.when(live)
                def _():
                    for cp in loads(j):
                        cp.wait()

                    @pl.when(info_ref[2, j] < page)
                    def _():
                        off = info_ref[2, j]
                        w = jnp.minimum(off // 2, page // 2 - 2)
                        at = pl.ds(pl.multiple_of(w * (2 * kvh), 2 * kvh), 4 * kvh)
                        for buf, r0 in ((kbuf, qr), (vbuf, qr + 2 * kvh)):
                            new = qkv_ref[info_ref[1, j], r0:r0 + 2 * kvh, :].astype(jnp.float32)
                            first = jnp.concatenate([new[:kvh]] * 4, axis=0)
                            second = jnp.concatenate([new[kvh:]] * 4, axis=0)
                            old = buf[j, at, :].astype(jnp.float32)
                            tok = wrow + 2 * w
                            old = jnp.where(tok == off, first, jnp.where(tok == off + 1, second, old))
                            buf[j, at, :] = old.astype(jnp.bfloat16)

            res = []
            for u in range(UNROLL):
                q = qkv_ref[jnp.minimum(seqs[u], n_seq - 1), :qr, :]
                s = lax.dot_general(q, kbuf[idx[u]], (((1,), (1,)), ((), ())), preferred_element_type=jnp.float32) * scale
                s = jnp.where(need <= offs[u], s, NEG)
                m = jnp.max(s, axis=1, keepdims=True)
                p = jnp.exp(s - m)
                l = jnp.sum(p, axis=1, keepdims=True)
                o = jnp.dot(p.astype(jnp.bfloat16), vbuf[idx[u]], preferred_element_type=jnp.float32)
                res.append((m, l, o))
            for u in range(UNROLL):
                m, l, o = res[u]
                sel = lane == seqs[u]
                m_all, l_all = ml_ref[0], ml_ref[1]
                m_old = jnp.max(jnp.where(sel, m_all, NEG), axis=1, keepdims=True)
                m_new = jnp.maximum(m_old, m)
                alpha = jnp.exp(m_old - m_new)
                beta = jnp.exp(m - m_new)
                acc_ref[seqs[u]] = acc_ref[seqs[u]] * alpha + o * beta
                ml_ref[0] = jnp.where(sel, m_new, m_all)
                ml_ref[1] = jnp.where(sel, l_all * alpha + l * beta, l_all)
            for u in range(UNROLL):
                @pl.when(base + u < mid)
                def _():
                    for cp in stores(base + u):
                        cp.start()

        @pl.loop(mid, hi)
        def _(i):
            for cp in loads(i):
                cp.wait()
            for cp in stores(i):
                cp.start()

        @pl.loop(lo, hi)
        def _(i):
            for cp in stores(i):
                cp.wait()

    any_spec = pl.BlockSpec(memory_space=pl.ANY)
    vmem = pl.BlockSpec(memory_space=pltpu.VMEM)
    smem = pl.BlockSpec(memory_space=pltpu.SMEM)
    operands = [info, counts, qkv, k_src, v_src]
    specs = [smem, smem, vmem, any_spec, any_spec]
    alias = {}
    if aliased:
        alias = {5: 0, 6: 1}
        operands += list(prev_pools)
        specs += [any_spec, any_spec]
    if carried:
        operands += list(state)
        specs += [vmem, vmem]
    pool = jax.ShapeDtypeStruct((n_slots * layers, prow, hd), jnp.bfloat16)
    return pl.pallas_call(
        body,
        out_shape=[pool, pool,
                   jax.ShapeDtypeStruct((n_seq + 1, qr, hd), jnp.float32),
                   jax.ShapeDtypeStruct((2, qr, 128), jnp.float32)],
        in_specs=specs,
        out_specs=[any_spec, any_spec, vmem, vmem],
        scratch_shapes=[
            pltpu.VMEM((n_slots, prow, hd), jnp.bfloat16),
            pltpu.VMEM((n_slots, prow, hd), jnp.bfloat16),
            pltpu.SemaphoreType.DMA((2, n_slots)),
            pltpu.SemaphoreType.DMA((2, n_slots)),
        ],
        input_output_aliases=alias,
        cost_estimate=pl.CostEstimate(flops=400_000_000, bytes_accessed=16_000_000, transcendentals=0),
        name=f"attend_{layer}_{part}",
    )(*operands)


def solution(mesh):
    n_rows = mesh.shape['kv2']
    n_cols = mesh.shape['kv']
    dev_axes = ('rep', 'kv2', 'kv')
    seq_spec = P(None, dev_axes, None)
    pool_spec = P(dev_axes, None, None, None, None)
    table_spec = P(dev_axes, None)
    vec_spec = P(dev_axes)
    full_spec = P()

    def per_device(x_embed, w_query, w_key, w_value, w_out, w_up, w_down, k_pool, v_pool, old_table, seq_len, src_slot, dst_slot):
        n_slots, layers, page, kv_heads, head_dim = k_pool.shape
        heads = w_query.shape[2] // head_dim
        q_group = heads // kv_heads
        seq_dev = x_embed.shape[1]
        n_pages = old_table.shape[1]
        n_mig = src_slot.shape[0]
        n_dev = n_rows * n_cols
        row_seqs = seq_dev * n_cols
        prow = page * kv_heads
        width = x_embed.shape[2]
        me_row, me_col = lax.axis_index('kv2'), lax.axis_index('kv')
        me = me_row * n_cols + me_col
        base = me * n_slots

        meta = jnp.concatenate([src_slot, dst_slot, old_table.reshape(-1), seq_len])
        meta = lax.all_gather(meta, ('kv2', 'kv'))
        src_all = meta[:, :n_mig].reshape(-1)
        dst_all = meta[:, n_mig:2 * n_mig].reshape(-1)
        row_meta = lax.dynamic_slice_in_dim(meta, me_row * n_cols, n_cols, axis=0)
        row_table = row_meta[:, 2 * n_mig:2 * n_mig + seq_dev * n_pages].reshape(-1)
        row_len = row_meta[:, 2 * n_mig + seq_dev * n_pages:].reshape(-1)

        k_rows = k_pool.reshape(n_slots * layers, prow, head_dim)
        v_rows = v_pool.reshape(n_slots * layers, prow, head_dim)
        leaving = take_pages((src_slot - base) * layers, k_rows, v_rows, layers)
        moved = [lax.all_gather(t, ('kv2', 'kv'), tiled=True) for t in leaving]

        same = row_table[:, None] == src_all[None, :]
        new_table = jnp.where(same.any(axis=1), jnp.sum(jnp.where(same, dst_all[None, :], 0), axis=1), row_table)
        slots = jnp.arange(n_slots, dtype=jnp.int32)
        cells = jnp.arange(row_seqs * n_pages, dtype=jnp.int32)
        slot_cell = jnp.max(jnp.where(new_table[None, :] == (slots + base)[:, None], cells[None, :], -1), axis=1)
        moves = jnp.arange(n_dev * n_mig, dtype=jnp.int32)
        move_of = jnp.max(jnp.where(dst_all[None, :] == (slots + base)[:, None], moves[None, :], -1), axis=1)
        is_mig = move_of >= 0
        used = slot_cell >= 0
        seq_of = jnp.where(used, slot_cell // n_pages, row_seqs)
        seq_one = seq_of[:, None] == jnp.arange(row_seqs, dtype=jnp.int32)[None, :]
        len_of = jnp.sum(jnp.where(seq_one, row_len[None, :], 0), axis=1)
        off_of = len_of - (slot_cell % n_pages) * page
        off_of = jnp.where(used & (off_of >= 0) & (off_of < page), off_of, 2 * page)
        key = is_mig.astype(jnp.int32) * 2 + (~used).astype(jnp.int32)
        order = key * n_slots + slots
        pos = jnp.sum((order[None, :] < order[:, None]).astype(jnp.int32), axis=1)
        place = pos[None, :] == jnp.arange(64, dtype=jnp.int32)[:, None]
        info = jnp.stack([jnp.sum(jnp.where(place, t[None, :], 0), axis=1) for t in (slots, seq_of, off_of, move_of)])
        counts = jnp.sum((key[None, :] <= jnp.arange(4, dtype=jnp.int32)[:, None]).astype(jnp.int32), axis=1)

        hidden = x_embed.reshape(2 * seq_dev, width)
        pools = None
        for layer in range(layers):
            dot = lambda a, w: jnp.dot(a, w[layer], preferred_element_type=jnp.float32)
            query = dot(hidden, w_query).astype(jnp.bfloat16).reshape(2, seq_dev, heads, head_dim)
            k_new = dot(hidden, w_key).astype(jnp.bfloat16).reshape(2, seq_dev, kv_heads, head_dim)
            v_new = dot(hidden, w_value).astype(jnp.bfloat16).reshape(2, seq_dev, kv_heads, head_dim)
            per_seq = lambda t: jnp.swapaxes(t, 0, 1).reshape(seq_dev, -1, head_dim)
            qkv = jnp.concatenate([per_seq(query), per_seq(k_new), per_seq(v_new)], axis=1)
            qkv = gather_rows(qkv, 'kv', n_cols, 0).reshape(row_seqs, -1, head_dim)
            dims = dict(layer=layer, n_slots=n_slots, layers=layers, page=page, kvh=kv_heads, q_group=q_group, hd=head_dim)
            *pools, acc, ml = attend(info, counts, qkv, k_rows, v_rows, pools, None, part=0, **dims)
            *pools, acc, ml = attend(info, counts, qkv, moved[layer], moved[layer], pools, (acc, ml), part=1, **dims)
            o = combine(acc[:row_seqs], ml, 'kv', n_cols, 1)
            attn_out = jnp.swapaxes(o.reshape(seq_dev, 2, heads * head_dim), 0, 1).reshape(2 * seq_dev, heads * head_dim)
            hidden = (hidden.astype(jnp.float32) + dot(attn_out, w_out)).astype(jnp.bfloat16)
            up_act = jax.nn.gelu(dot(hidden, w_up)).astype(jnp.bfloat16)
            hidden = (hidden.astype(jnp.float32) + dot(up_act, w_down)).astype(jnp.bfloat16)
        k_out, v_out = (p.reshape(k_pool.shape) for p in pools)
        return hidden.reshape(2, seq_dev, width), k_out, v_out

    return jax.shard_map(per_device, mesh=mesh, in_specs=(seq_spec, full_spec, full_spec, full_spec, full_spec, full_spec, full_spec, pool_spec, pool_spec, table_spec, vec_spec, vec_spec, vec_spec), out_specs=(seq_spec, pool_spec, pool_spec), check_vma=False)
```

time: 887 us -> 396 us (0.45); the launches traced: 876 us -> 394 us
  local copies, waits for them, and re-layouts: 285 us -> 9.39 us
  Pallas kernels: 0 us -> 161 us
  matrix products: 248 us -> 111 us
  waiting for transfers between devices: 166 us -> 77.3 us
  blocking collectives: 88.6 us -> 14 us
  other arithmetic: 57.4 us -> 5.3 us
  starting transfers between devices: 14.4 us -> 0.08 us
    scatter x12 -> x0, local copies, waits for them, and re-layouts: 162 us -> none  [the longest x1 56.6 us: per_device(): k_pool = k_pool.at[dst_local].set(in_pages[:, 0], mode='drop')]
    pallas_call x0 -> x9, Pallas kernels: none -> 161 us  [the longest x4 53.6 us: attend(): pl.pallas_call(body, out_shape=[pool, pool, jax.ShapeDtypeStruct((n_seq +...]
    dot_general x28 -> x10, matrix products: 248 us -> 111 us  [per_device(): dot = lambda a, w: jnp.dot(a, w[layer], preferred_element_type=jnp.float32)]
    all_gather x1 -> x2, waiting for transfers between devices: 166 us -> 76.6 us  [per_device(): moved = [lax.all_gather(t, ('kv2', 'kv'), tiled=True) for t in leaving]]
    all_gather x9 -> x0, blocking collectives: 71.2 us -> none  [the longest x4 35.7 us: per_device(): lax.all_gather(jnp.stack([k_new, v_new]), 'kv', axis=1, tiled=True)]
    squeeze x1 -> x0, local copies, waits for them, and re-layouts: 33.3 us -> none  [per_device(): k_pool = k_pool.at[dst_local].set(in_pages[:, 0], mode='drop')]
    scatter-add x8 -> x0, other arithmetic: 24.8 us -> none  [the longest x4 13.3 us: per_device(): jax.ops.segment_sum(slot_w[..., None] * slot_out, seg_ids, num_segments=r...]
    slice x13 -> x5, local copies, waits for them, and re-layouts: 28.9 us -> 5.02 us  [the longest x2 4.81 us: per_device(): o = combine(acc[:row_seqs], ml, 'kv', n_cols, 1)]
  transfers between devices with their start and end apart: 5 -> 2, of which waited for: 2 -> 2; matrix products, arithmetic and copies ran while one was open for 20% -> 20% of each run, Pallas kernels for 0% -> 32%
where the time goes in v1:
time: 396 us; the launch traced here: 394 us
  Pallas kernels  161 us (41%)
  matrix products  111 us (28%)
  waiting for transfers between devices  77.3 us (20%)
  between operations  15.1 us (4%)
  blocking collectives  14 us (4%)
  local copies, waits for them, and re-layouts  9.39 us (2%)
  other arithmetic  5.3 us (1%)
    dot_general x10, matrix products, per_device(): dot = lambda a, w: jnp.dot(a, w[layer], preferred_element_type=jnp.float32)  111 us
    all_gather x2, waiting for transfers between devices, per_device(): moved = [lax.all_gather(t, ('kv2', 'kv'), tiled=True) for t in leaving]  76.6 us
    pallas_call x4, Pallas kernels, attend(): pl.pallas_call(body, out_shape=[pool, pool, jax.ShapeDtypeStruct((n_seq +...  53.6 us
    pallas_call x2, Pallas kernels, combine(): pl.pallas_call(body, out_shape=jax.ShapeDtypeStruct((b, r, hd), jnp.bfloa...  52.5 us
    pallas_call x2, Pallas kernels, gather_rows(): pl.pallas_call(body, out_shape=jax.ShapeDtypeStruct((n,) + x.shape, x.dty...  51 us
    unnamed x1, blocking collectives  14 us
  transfers between devices with their start and end apart: 2, of which 2 were waited for; matrix products, arithmetic and copies ran while one was open for 20% of the time, Pallas kernels for 32%

profile of v1, /device:TPU:0, one launch (start us, length us, event | category | flops | bytes accessed | tf_op | source)
XLA Modules:
  0.0 393.9 jit_solution(10249228222675681642)
XLA Ops:
  7.3 1.2 subtract_multiply_fusion.rows_ref
  8.5 4.1 %take_pages.1 = (bf16[24,256,128]{2,1,0:T(8,128)(2,1)}, bf16[24,256,128]{2,1,0:T(8,128)(2,1)}) custom-call(s32[12]{0:T(128)} %subtract_multiply_fusion.rows_ref, bf16[120,256,128]{2,1,0:T(8,128)(2,1)} %bitcast.163, bf16[120,256,128]{2,1,0:T(8,128)(2,1)} %bitcast.166), custom_call_target="tpu_custom_call" | custom-call | tf_op jit(solution)/shard_map/take_pages/pallas_call | solution.py:39
  12.7 0.7 all-gather.6.cloned.1.call-update
  15.1 14.0 %all-reduce = s32[960]{0:T(1024)S(1)} all-reduce(s32[960]{0:T(1024)S(1)} %add_dynamic-update-slice_fusion), channel_id=2, replica_groups=mesh['rep'=2,'kv2'=4,'kv'=4] {'kv2','kv'}, use_global_device_ids=true, to_apply=%add | all-reduce | flops 960 | bytes 7680
  29.9 3.7 fusion.93
  33.6 3.7 fusion.90
  37.3 7.7 %fusion.69 = bf16[3,8,24,128]{3,1,2,0:T(8,128)(2,1)S(1)} fusion(bf16[24,3072]{1,0:T(8,128)(2,1)S(1)} %reshape.193, bf16[2,3072,3072]{2,1,0:T(8,128)(2,1)} %param.14), kind=kOutput, calls=%fused_computation.49 | convolution fusion | flops 453058560 | bytes 19169280 | tf_op jit(solution)/shard_map/dot_general | solution.py:353
  45.2 0.7 pad_maximum_fusion.x_ref
  45.9 24.7 %gather_rows.2 = bf16[4,12,80,128]{3,2,1,0:T(8,128)(2,1)} custom-call(bf16[12,80,128]{2,1,0:T(8,128)(2,1)} %pad_maximum_fusion.x_ref), custom_call_target="tpu_custom_call" | custom-call | tf_op jit(solution)/shard_map/gather_rows/pallas_call | solution.py:72
  72.4 0.7 convert_reduce_fusion.1.cnt_ref
  73.1 12.9 %attend_0_0.1 = (bf16[120,256,128]{2,1,0:T(8,128)(2,1)}, bf16[120,256,128]{2,1,0:T(8,128)(2,1)}, f32[49,48,128]{2,1,0:T(8,128)}, f32[2,48,128]{2,1,0:T(8,128)}) custom-call(s32[4,64]{1,0:T(4,128)} %pad_add_fusion.info_ref, s32[4]{0:T(128)} %convert_reduce_fusion.1.cnt_ref, bf16[48,80,128]{2,1,0:T(8,128)(2,1)} %bitcast.171, bf16[120,256,128]{2,1,0:T(8,128)(2,1)} %bitcast.164, ...), custom_call_target="tpu_custom_call" | custom-call | flops 400000000 | bytes 16000000 | tf_op jit(solution)/shard_map/attend_0_0/pallas_call | solution.py:272
  86.0 68.3 %all-gather.4.cloned.1.call-done.k_in.v_in = bf16[384,256,128]{2,1,0:T(8,128)(2,1)} async-done(((bf16[24,256,128]{2,1,0:T(8,128)(2,1)}), bf16[384,256,128]{2,1,0:T(8,128)(2,1)}) %all-gather.4.cloned.1.call-update) | async-done | bytes 25165840 | tf_op jit(solution)/shard_map/all_gather | solution.py:327
  154.3 13.8 %attend_0_1.1 = (bf16[120,256,128]{2,1,0:T(8,128)(2,1)}, bf16[120,256,128]{2,1,0:T(8,128)(2,1)}, f32[49,48,128]{2,1,0:T(8,128)}, f32[2,48,128]{2,1,0:T(8,128)}) custom-call(s32[4,64]{1,0:T(4,128)} %pad_add_fusion.info_ref, s32[4]{0:T(128)} %convert_reduce_fusion.1.cnt_ref, ...), custom_call_target="tpu_custom_call", output_to_operand_aliasing={{0}: (5, {}), {1}: (6, {})} | custom-call | flops 400000000 | bytes 16000000 | tf_op jit(solution)/shard_map/attend_0_1/pallas_call | solution.py:272
  168.1 2.5 slice.61.acc_ref
  170.6 33.8 %combine.2 = bf16[12,48,128]{2,1,0:T(8,128)(2,1)} custom-call(f32[48,48,128]{2,1,0:T(8,128)} %slice.61.acc_ref, f32[2,48,128]{2,1,0:T(8,128)} %get-tuple-element.27.ml_ref), custom_call_target="tpu_custom_call" | custom-call | tf_op jit(solution)/shard_map/combine/pallas_call | solution.py:118
  204.4 0.9 reshape.204
  205.4 7.8 %fusion.57 = bf16[24,3072]{1,0:T(8,128)(2,1)S(1)} fusion(bf16[24,3072]{1,0:T(8,128)(2,1)S(1)} %reshape.205, bf16[2,3072,3072]{2,1,0:T(8,128)(2,1)} %param.17, bf16[24,3072]{1,0:T(8,128)(2,1)S(1)} %reshape.193), kind=kOutput, calls=%fused_computation.43 | convolution fusion | flops 453206016 | bytes 19316736 | tf_op jit(solution)/shard_map/dot_general | solution.py:353
  213.2 32.8 %fusion.51 = bf16[24,3072]{1,0:T(8,128)(2,1)S(1)} fusion(bf16[2,8192,3072]{2,1,0:T(8,128)(2,1)} %param.19, bf16[24,3072]{1,0:T(8,128)(2,1)S(1)} %fusion.57, bf16[2,3072,8192]{2,1,0:T(8,128)(2,1)} %param.18), kind=kOutput, calls=%fused_computation.41 | convolution fusion | flops 2417909760 | bytes 101105664 | tf_op jit(solution)/shard_map/dot_general | solution.py:353
  246.0 7.7 %fusion.66 = bf16[3,8,24,128]{3,1,2,0:T(8,128)(2,1)S(1)} fusion(bf16[24,3072]{1,0:T(8,128)(2,1)S(1)} %fusion.51, bf16[2,3072,3072]{2,1,0:T(8,128)(2,1)} %param.14), kind=kOutput, calls=%fused_computation.48 | convolution fusion | flops 453058560 | bytes 19169280 | tf_op jit(solution)/shard_map/dot_general | solution.py:353
  253.8 3.7 fusion.84
  257.6 3.7 fusion.87
  261.3 0.7 pad_maximum_fusion.1.x_ref
  262.1 26.2 %gather_rows.3 = bf16[4,12,80,128]{3,2,1,0:T(8,128)(2,1)} custom-call(bf16[12,80,128]{2,1,0:T(8,128)(2,1)} %pad_maximum_fusion.1.x_ref), custom_call_target="tpu_custom_call" | custom-call | tf_op jit(solution)/shard_map/gather_rows/pallas_call | solution.py:72
  288.3 12.9 %attend_1_0.1 = (bf16[120,256,128]{2,1,0:T(8,128)(2,1)}, bf16[120,256,128]{2,1,0:T(8,128)(2,1)}, f32[49,48,128]{2,1,0:T(8,128)}, f32[2,48,128]{2,1,0:T(8,128)}) custom-call(s32[4,64]{1,0:T(4,128)} %pad_add_fusion.info_ref, s32[4]{0:T(128)} %convert_reduce_fusion.1.cnt_ref, ...), custom_call_target="tpu_custom_call", output_to_operand_aliasing={{0}: (5, {}), {1}: (6, {})} | custom-call | flops 400000000 | bytes 16000000 | tf_op jit(solution)/shard_map/attend_1_0/pallas_call | solution.py:272
  301.2 8.4 %all-gather.6.cloned.1.call-done.k_in.v_in = bf16[384,256,128]{2,1,0:T(8,128)(2,1)} async-done(((bf16[24,256,128]{2,1,0:T(8,128)(2,1)}), bf16[384,256,128]{2,1,0:T(8,128)(2,1)}) %all-gather.6.cloned.1.call-update) | async-done | bytes 25165840 | tf_op jit(solution)/shard_map/all_gather | solution.py:327
  309.6 13.9 %attend_1_1.1 = (bf16[120,256,128]{2,1,0:T(8,128)(2,1)}, bf16[120,256,128]{2,1,0:T(8,128)(2,1)}, f32[49,48,128]{2,1,0:T(8,128)}, f32[2,48,128]{2,1,0:T(8,128)}) custom-call(s32[4,64]{1,0:T(4,128)} %pad_add_fusion.info_ref, s32[4]{0:T(128)} %convert_reduce_fusion.1.cnt_ref, ...), custom_call_target="tpu_custom_call", output_to_operand_aliasing={{0}: (5, {}), {1}: (6, {})} | custom-call | flops 400000000 | bytes 16000000 | tf_op jit(solution)/shard_map/attend_1_1/pallas_call | solution.py:272
  323.5 2.4 slice.68.acc_ref
  325.9 18.7 %combine.3 = bf16[12,48,128]{2,1,0:T(8,128)(2,1)} custom-call(f32[48,48,128]{2,1,0:T(8,128)} %slice.68.acc_ref, f32[2,48,128]{2,1,0:T(8,128)} %get-tuple-element.36.ml_ref), custom_call_target="tpu_custom_call" | custom-call | tf_op jit(solution)/shard_map/combine/pallas_call | solution.py:118
  344.5 0.9 reshape.213
  345.6 7.8 %fusion.54 = bf16[24,3072]{1,0:T(8,128)(2,1)S(1)} fusion(bf16[24,3072]{1,0:T(8,128)(2,1)S(1)} %reshape.214, bf16[2,3072,3072]{2,1,0:T(8,128)(2,1)} %param.17, bf16[24,3072]{1,0:T(8,128)(2,1)S(1)} %fusion.51), kind=kOutput, calls=%fused_computation.42 | convolution fusion | flops 453206016 | bytes 19316736 | tf_op jit(solution)/shard_map/dot_general | solution.py:353
  353.4 32.8 %fusion.48 = bf16[24,3072]{1,0:T(8,128)(2,1)S(1)} fusion(bf16[2,8192,3072]{2,1,0:T(8,128)(2,1)} %param.19, bf16[24,3072]{1,0:T(8,128)(2,1)S(1)} %fusion.54, bf16[2,3072,8192]{2,1,0:T(8,128)(2,1)} %param.18), kind=kOutput, calls=%fused_computation.40 | convolution fusion | flops 2417909760 | bytes 101105664 | tf_op jit(solution)/shard_map/dot_general | solution.py:353
  386.2 0.8 copy.63
  (59 shorter events, 3.9 us)
Async XLA Ops:
  7.2 6.5 %copy-start.5 = (u32[32]{0:T(128)S(1)}, u32[32]{0:T(128)}, u32[]{:S(2)}) copy-start(u32[32]{0:T(128)} %constant.73) | copy-start | bytes 388
  7.2 7.7 %copy-start.4 = (s32[12]{0:T(128)S(1)}, s32[12]{0:T(128)}, u32[]{:S(2)}) copy-start(s32[12]{0:T(128)} %param.24) | copy-start | bytes 148
  7.2 6.3 %copy-start.1 = (s32[12,2]{0,1:T(2,128)S(1)}, s32[12,2]{0,1:T(2,128)}, u32[]{:S(2)}) copy-start(s32[12,2]{0,1:T(2,128)} %param.22) | copy-start | bytes 292
  7.2 7.7 %copy-start.2 = (s32[12]{0:T(128)S(1)}, s32[12]{0:T(128)}, u32[]{:S(2)}) copy-start(s32[12]{0:T(128)} %param.23) | copy-start | bytes 148
  7.2 7.7 %copy-start.3 = (s32[12]{0:T(128)S(1)}, s32[12]{0:T(128)}, u32[]{:S(2)}) copy-start(s32[12]{0:T(128)} %param.25) | copy-start | bytes 148
  7.2 22.5 %copy-start = (bf16[2,12,3072]{2,0,1:T(2,128)(2,1)S(1)}, bf16[2,12,3072]{2,0,1:T(2,128)(2,1)}, u32[]{:S(2)}) copy-start(bf16[2,12,3072]{2,0,1:T(2,128)(2,1)} %param.13) | copy-start | bytes 442372
  7.2 147.0 %all-gather.4.cloned.1.call-start = ((), (), s32[]{:S(2)}) async-start(), calls=%async_computation | async-start | bytes 26738688 | tf_op jit(solution)/shard_map/all_gather | solution.py:327
  12.7 296.9 %all-gather.6.cloned.1.call-start = ((), (), s32[]{:S(2)}) async-start(), calls=%async_computation.1 | async-start | bytes 26738688 | tf_op jit(solution)/shard_map/all_gather | solution.py:327
Sparse Core Ops, SparseCore 0:
  12.8 141.4 all-gather.3
  155.9 153.6 all-gather.5

commit v2 on v1

--- a/solution.py
+++ b/solution.py
@@ -7,14 +7,25 @@
 from jax.experimental.pallas import tpu as pltpu
 from jax.sharding import PartitionSpec as P
 
+
 MESH_ID = pl.DeviceIdType.MESH
 NEG = -1e30
 UNROLL = 4
+Z_CORE = 6
+Y_CORE = 10
+
+
+def uninit(shape, dtype):
+    def body(o_ref):
+        pass
+
+    return pl.pallas_call(
+        body, out_shape=jax.ShapeDtypeStruct(shape, dtype), out_specs=pl.BlockSpec(memory_space=pl.ANY), name="uninit")()
 
 
 def take_pages(rows, k_rows, v_rows, layers):
     m = rows.shape[0]
-    tail = k_rows.shape[1:]
+    prow, hd = k_rows.shape[1:]
 
     def body(rows_ref, k_in, v_in, *rest):
         outs, (buf, isem, osem) = rest[:layers], rest[layers:]
@@ -22,8 +33,8 @@
         for layer in range(layers):
             for i in range(m):
                 for which, ref in enumerate((k_in, v_in)):
-                    j = 2 * i + which
-                    cp = pltpu.make_async_copy(ref.at[rows_ref[i] + layer], buf.at[layer, j], isem.at[layer, j])
+                    cp = pltpu.make_async_copy(
+                        ref.at[rows_ref[i] + layer], buf.at[layer, i, pl.ds(which * prow, prow)], isem.at[layer, 2 * i + which])
                     cp.start()
                     ins.append(cp)
         for layer in range(layers):
@@ -38,13 +49,159 @@
     any_spec = pl.BlockSpec(memory_space=pl.ANY)
     return pl.pallas_call(
         body,
-        out_shape=[jax.ShapeDtypeStruct((2 * m,) + tail, k_rows.dtype)] * layers,
+        out_shape=[jax.ShapeDtypeStruct((m, 2 * prow, hd), k_rows.dtype)] * layers,
         in_specs=[pl.BlockSpec(memory_space=pltpu.SMEM), any_spec, any_spec],
         out_specs=[any_spec] * layers,
-        scratch_shapes=[pltpu.VMEM((layers, 2 * m) + tail, k_rows.dtype),
+        scratch_shapes=[pltpu.VMEM((layers, m, 2 * prow, hd), k_rows.dtype),
                         pltpu.SemaphoreType.DMA((layers, 2 * m)), pltpu.SemaphoreType.DMA((layers,))],
+        cost_estimate=pl.CostEstimate(flops=100_000_000, bytes_accessed=12_000_000, transcendentals=0),
         name="take_pages",
     )(rows, k_rows, v_rows)
+
+
+def pick(lists, sources, splits):
+    n = sum(splits)
+    tail, dtype = sources[0].shape[1:], sources[0].dtype
+
+    def body(idx_ref, *rest):
+        ins, outs, (buf, isem, osem) = rest[:len(sources)], rest[len(sources):-3], rest[-3:]
+
+        @pl.loop(0, n)
+        def _(i):
+            at, lo = idx_ref[i], 0
+            for ref in ins:
+                hi = lo + ref.shape[0]
+
+                @pl.when((at >= lo) & (at < hi))
+                def _():
+                    pltpu.make_async_copy(ref.at[at - lo], buf.at[i], isem.at[i]).start()
+
+                lo = hi
+
+        @pl.loop(0, n)
+        def _(i):
+            pltpu.make_async_copy(ins[0].at[0], buf.at[i], isem.at[i]).wait()
+
+        puts, lo = [], 0
+        for j, size in enumerate(splits):
+            cp = pltpu.make_async_copy(buf.at[pl.ds(lo, size)], outs[j], osem.at[j])
+            cp.start()
+            puts.append(cp)
+            lo += size
+        for cp in puts:
+            cp.wait()
+
+    any_spec = pl.BlockSpec(memory_space=pl.ANY)
+    return pl.pallas_call(
+        body,
+        out_shape=[jax.ShapeDtypeStruct((size,) + tail, dtype) for size in splits],
+        in_specs=[pl.BlockSpec(memory_space=pltpu.SMEM)] + [any_spec] * len(sources),
+        out_specs=[any_spec] * len(splits),
+        scratch_shapes=[pltpu.VMEM((n,) + tail, dtype), pltpu.SemaphoreType.DMA((n,)), pltpu.SemaphoreType.DMA((len(splits),))],
+        cost_estimate=pl.CostEstimate(flops=100_000_000, bytes_accessed=5_000_000, transcendentals=0),
+    )(lists, *sources)
+
+
+def share_plan(x, mesh_shape, cid):
+    nx, ny, nz = mesh_shape
+    n = nx * ny * nz
+
+    def body(x_ref, o_ref, send_sem, recv_sem):
+        me = (lax.axis_index('rep') * ny + lax.axis_index('kv2')) * nz + lax.axis_index('kv')
+
+        def coords(d):
+            p = lax.rem(me + d, n)
+            return (p // (ny * nz), lax.rem(p // nz, ny), lax.rem(p, nz))
+
+        barrier = pltpu.get_barrier_semaphore()
+        for d in range(1, n):
+            pl.semaphore_signal(barrier, inc=1, device_id=coords(d), device_id_type=MESH_ID)
+        pl.semaphore_wait(barrier, n - 1)
+        copies = []
+        for d in range(1, n):
+            cp = pltpu.make_async_remote_copy(
+                src_ref=x_ref, dst_ref=o_ref.at[me], send_sem=send_sem.at[d], recv_sem=recv_sem.at[d],
+                device_id=coords(d), device_id_type=MESH_ID)
+            cp.start()
+            copies.append(cp)
+        o_ref[me] = x_ref[...]
+        for cp in copies:
+            cp.wait()
+
+    return pl.pallas_call(
+        body,
+        out_shape=jax.ShapeDtypeStruct((n,) + x.shape, x.dtype),
+        in_specs=[pl.BlockSpec(memory_space=pltpu.VMEM)],
+        out_specs=pl.BlockSpec(memory_space=pltpu.VMEM),
+        scratch_shapes=[pltpu.SemaphoreType.DMA((n,)), pltpu.SemaphoreType.DMA((n,))],
+        compiler_params=pltpu.CompilerParams(collective_id=cid, has_side_effects=True),
+        name="share_plan",
+    )(x)
+
+
+def route(dst, dev, pos, n_mig, n_slots):
+    n_dev = dev.shape[0] // n_mig
+    z_at, y_at = 2 * n_mig, 2 * n_mig + 2 * 3 * Z_CORE
+
+    def body(dst_ref, dev_ref, pos_ref, z_ref, y_ref, s_ref, cnt, cnt2):
+        row, colm = pos_ref[0], pos_ref[1]
+        half, core = colm >> 1, colm & 1
+        me = row * 4 + colm
+
+        @pl.loop(0, 64)
+        def _(i):
+            z_ref[i] = 0
+            y_ref[i] = 0
+            s_ref[i] = -1
+            cnt[i] = 0
+
+        @pl.loop(0, 8)
+        def _(i):
+            cnt2[i] = 0
+
+        @pl.loop(0, n_dev)
+        def _(d):
+            si, sy, sc = d >> 2, (d >> 1) & 1, d & 1
+
+            @pl.loop(0, n_mig)
+            def _(e):
+                dd = dev_ref[d * n_mig + e]
+                di, dy = dd >> 2, (dd >> 1) & 1
+                c1 = (d >> 1) * 4 + di
+                k = cnt[c1]
+                cnt[c1] = k + 1
+                cross = (dy != sy).astype(jnp.int32)
+                c2 = di * 2 + sy
+                k2 = cnt2[c2]
+                cnt2[c2] = k2 + cross
+                shift = (di - si) & 3
+                at = jnp.where(sc == core, e, n_mig + e)
+                z_slot = (shift - 1) * Z_CORE + (k >> 1)
+                here = jnp.where(shift == 0, at, z_at + z_slot + jnp.where((k & 1) == core, 0, 3 * Z_CORE))
+
+                @pl.when((si == row) & (sy == half) & (shift != 0) & ((k & 1) == core) & (k < 2 * Z_CORE))
+                def _():
+                    z_ref[z_slot] = at
+
+                @pl.when((di == row) & (sy == half) & (cross == 1) & ((k2 & 1) == core) & (k2 < 2 * Y_CORE))
+                def _():
+                    y_ref[k2 >> 1] = jnp.minimum(here, y_at - 1)
+
+                @pl.when(dd == me)
+                def _():
+                    by_y = y_at + (k2 >> 1) + jnp.where((k2 & 1) == core, 0, Y_CORE)
+                    s_ref[dst_ref[d * n_mig + e] - me * n_slots] = jnp.where(cross == 1, by_y, here)
+
+    smem = pl.BlockSpec(memory_space=pltpu.SMEM)
+    return pl.pallas_call(
+        body,
+        out_shape=[jax.ShapeDtypeStruct((64,), jnp.int32)] * 3,
+        in_specs=[smem] * 3,
+        out_specs=[smem] * 3,
+        scratch_shapes=[pltpu.SMEM((64,), jnp.int32), pltpu.SMEM((8,), jnp.int32)],
+        cost_estimate=pl.CostEstimate(flops=100_000_000, bytes_accessed=1_000_000, transcendentals=0),
+        name="route",
+    )(dst, dev, pos)
 
 
 def enter(axis, n, me):
@@ -131,7 +288,122 @@
     )(acc, ml)
 
 
-def attend(info, counts, qkv, k_src, v_src, prev_pools, state, layer, part, n_slots, layers, page, kvh, q_group, hd):
+def mlp_pair(attn, hidden, w_out, w_up, w_down, layer, cid):
+    rows, d = attn.shape
+    ff = w_up.shape[2]
+    r = -(-rows // 32) * 32
+    tile = 512
+    d_half, f_half = d // 2, ff // 2
+    n_o, n_f = d_half // tile, f_half // tile
+    ring_c, ring_r = min(8, n_o + n_f), min(6, n_f)
+    attn, hidden = (jnp.pad(t, ((0, r - rows), (0, 0))) for t in (attn, hidden))
+
+    def body(attn_ref, hid_ref, wo_ref, wu_ref, wd_ref, o_ref, x_all, h_all, hm, act, acc, rx, wc, wr, csem, rsem, ssem, qsem):
+        me = lax.axis_index('kv')
+        core = lax.rem(me, 2)
+        peer = me + 1 - 2 * core
+        mine, other = pl.ds(core * r, r), pl.ds((1 - core) * r, r)
+
+        def col(c, is_out):
+            if is_out:
+                src = wo_ref.at[layer, :, pl.ds(pl.multiple_of(core * d_half + c * tile, tile), tile)]
+            else:
+                src = wu_ref.at[layer, :, pl.ds(pl.multiple_of(core * f_half + (c - n_o) * tile, tile), tile)]
+            slot = lax.rem(c, ring_c)
+            return pltpu.make_async_copy(src, wc.at[slot], csem.at[slot])
+
+        def row(j):
+            slot = lax.rem(j, ring_r)
+            src = wd_ref.at[layer, pl.ds(pl.multiple_of(core * f_half + j * tile, tile), tile), :]
+            return pltpu.make_async_copy(src, wr.at[slot], rsem.at[slot])
+
+        for c in range(ring_c):
+            col(c, c < n_o).start()
+
+        barrier = pltpu.get_barrier_semaphore()
+        pl.semaphore_signal(barrier, inc=1, device_id={'kv': peer}, device_id_type=MESH_ID)
+        pl.semaphore_wait(barrier, 1)
+
+        def send(src, dst, i):
+            return pltpu.make_async_remote_copy(
+                src_ref=src, dst_ref=dst, send_sem=ssem.at[i], recv_sem=qsem.at[i],
+                device_id={'kv': peer}, device_id_type=MESH_ID)
+
+        swaps = [send(attn_ref, x_all.at[mine], 0), send(hid_ref, h_all.at[mine], 1)]
+        for cp in swaps:
+            cp.start()
+        x_all[mine] = attn_ref[...]
+        h_all[mine] = hid_ref[...]
+        for cp in swaps:
+            cp.wait()
+
+        @pl.loop(0, n_o)
+        def _(c):
+            col(c, True).wait()
+            at = pl.ds(pl.multiple_of(core * d_half + c * tile, tile), tile)
+            part = jnp.dot(x_all[...], wc[lax.rem(c, ring_c)], preferred_element_type=jnp.float32)
+            hm[:, at] = (h_all[:, at].astype(jnp.float32) + part).astype(jnp.bfloat16)
+
+            @pl.when(c + ring_c < n_o + n_f)
+            def _():
+                col(c + ring_c, False).start()
+
+        own_cols = pl.ds(pl.multiple_of(core * d_half, tile), d_half)
+        cp = send(hm.at[:, own_cols], hm.at[:, own_cols], 2)
+        cp.start()
+        acc[...] = jnp.zeros_like(acc)
+        cp.wait()
+
+        @pl.loop(0, n_f)
+        def _(j):
+            c = j + n_o
+            col(c, False).wait()
+            up = jnp.dot(hm[...], wc[lax.rem(c, ring_c)], preferred_element_type=jnp.float32)
+            act[:, pl.ds(pl.multiple_of(j * tile, tile), tile)] = jax.nn.gelu(up).astype(jnp.bfloat16)
+
+            @pl.when(c + ring_c < n_o + n_f)
+            def _():
+                col(c + ring_c, False).start()
+
+            @pl.when(j < ring_r)
+            def _():
+                row(j).start()
+
+        @pl.loop(0, n_f)
+        def _(j):
+            row(j).wait()
+            acc[...] += jnp.dot(act[:, pl.ds(pl.multiple_of(j * tile, tile), tile)], wr[lax.rem(j, ring_r)],
+                                preferred_element_type=jnp.float32)
+
+            @pl.when(j + ring_r < n_f)
+            def _():
+                row(j + ring_r).start()
+
+        cp = send(acc.at[other], rx, 3)
+        cp.start()
+        cp.wait()
+        o_ref[...] = (hm[mine].astype(jnp.float32) + (acc[mine] + rx[...])).astype(o_ref.dtype)
+
+    vmem, any_spec = pl.BlockSpec(memory_space=pltpu.VMEM), pl.BlockSpec(memory_space=pl.ANY)
+    out = pl.pallas_call(
+        body,
+        out_shape=jax.ShapeDtypeStruct((r, d), jnp.bfloat16),
+        in_specs=[vmem, vmem, any_spec, any_spec, any_spec],
+        out_specs=vmem,
+        scratch_shapes=[
+            pltpu.VMEM((2 * r, d), jnp.bfloat16), pltpu.VMEM((2 * r, d), jnp.bfloat16), pltpu.VMEM((2 * r, d), jnp.bfloat16),
+            pltpu.VMEM((2 * r, f_half), jnp.bfloat16), pltpu.VMEM((2 * r, d), jnp.float32), pltpu.VMEM((r, d), jnp.float32),
+            pltpu.VMEM((ring_c, d, tile), jnp.bfloat16), pltpu.VMEM((ring_r, tile, d), jnp.bfloat16),
+            pltpu.SemaphoreType.DMA((ring_c,)), pltpu.SemaphoreType.DMA((ring_r,)),
+            pltpu.SemaphoreType.DMA((4,)), pltpu.SemaphoreType.DMA((4,)),
+        ],
+        compiler_params=pltpu.CompilerParams(collective_id=cid, has_side_effects=True, vmem_limit_bytes=58 * 1024 * 1024),
+        cost_estimate=pl.CostEstimate(flops=6_000_000_000, bytes_accessed=60_000_000, transcendentals=0),
+    )(attn, hidden, w_out, w_up, w_down)
+    return out[:rows]
+
+
+def attend(info, counts, qkv, sources, prev_pools, state, layer, part, n_slots, layers, page, kvh, q_group, hd):
     prow = page * kvh
     qr = 2 * kvh * q_group
     n_seq = qkv.shape[0]
@@ -139,7 +411,8 @@
     aliased = prev_pools is not None
     carried = state is not None
 
-    def body(info_ref, cnt_ref, qkv_ref, k_in, v_in, *rest):
+    def body(info_ref, cnt_ref, qkv_ref, *rest):
+        ins, rest = rest[:len(sources)], rest[len(sources):]
         if aliased:
             rest = rest[2:]
         if carried:
@@ -150,13 +423,32 @@
         mid = cnt_ref[2 * part]
         hi = cnt_ref[2 * part + 1]
 
+        def load_from(k_page, v_page, i):
+            return (pltpu.make_async_copy(k_page, kbuf.at[i], isem.at[0, i]),
+                    pltpu.make_async_copy(v_page, vbuf.at[i], isem.at[1, i]))
+
         def loads(i):
             if part:
-                k_at, v_at = info_ref[3, i] * 2, info_ref[3, i] * 2 + 1
-            else:
-                k_at = v_at = info_ref[0, i] * layers + layer
-            return (pltpu.make_async_copy(k_in.at[k_at], kbuf.at[i], isem.at[0, i]),
-                    pltpu.make_async_copy(v_in.at[v_at], vbuf.at[i], isem.at[1, i]))
+                return load_from(ins[0].at[0, pl.ds(0, prow)], ins[0].at[0, pl.ds(prow, prow)], i)
+            at = info_ref[0, i] * layers + layer
+            return load_from(ins[0].at[at], ins[1].at[at], i)
+
+        def start_loads(i):
+            if not part:
+                for cp in loads(i):
+                    cp.start()
+                return
+            at, first = info_ref[3, i], 0
+            for ref in ins:
+                last = first + ref.shape[0]
+
+                @pl.when((at >= first) & (at < last))
+                def _():
+                    u = at - first
+                    for cp in load_from(ref.at[u, pl.ds(0, prow)], ref.at[u, pl.ds(prow, prow)], i):
+                        cp.start()
+
+                first = last
 
         def stores(i):
             slot = info_ref[0, i]
@@ -165,8 +457,7 @@
 
         @pl.loop(lo, hi)
         def _(i):
-            for cp in loads(i):
-                cp.start()
+            start_loads(i)
 
         if carried:
             acc_ref[...] = acc_prev[...]
@@ -258,11 +549,11 @@
     any_spec = pl.BlockSpec(memory_space=pl.ANY)
     vmem = pl.BlockSpec(memory_space=pltpu.VMEM)
     smem = pl.BlockSpec(memory_space=pltpu.SMEM)
-    operands = [info, counts, qkv, k_src, v_src]
-    specs = [smem, smem, vmem, any_spec, any_spec]
+    operands = [info, counts, qkv, *sources]
+    specs = [smem, smem, vmem] + [any_spec] * len(sources)
     alias = {}
     if aliased:
-        alias = {5: 0, 6: 1}
+        alias = {len(operands): 0, len(operands) + 1: 1}
         operands += list(prev_pools)
         specs += [any_spec, any_spec]
     if carried:
@@ -284,7 +575,6 @@
         ],
         input_output_aliases=alias,
         cost_estimate=pl.CostEstimate(flops=400_000_000, bytes_accessed=16_000_000, transcendentals=0),
-        name=f"attend_{layer}_{part}",
     )(*operands)
 
 
@@ -313,18 +603,55 @@
         me = me_row * n_cols + me_col
         base = me * n_slots
 
-        meta = jnp.concatenate([src_slot, dst_slot, old_table.reshape(-1), seq_len])
-        meta = lax.all_gather(meta, ('kv2', 'kv'))
-        src_all = meta[:, :n_mig].reshape(-1)
-        dst_all = meta[:, n_mig:2 * n_mig].reshape(-1)
+        n_rep = mesh.shape['rep']
+        words = [src_slot, dst_slot, dst_slot // n_slots, old_table.reshape(-1), seq_len]
+        cuts = [0]
+        for w in words:
+            cuts.append(cuts[-1] + w.shape[0])
+        meta = jnp.pad(jnp.concatenate(words), (0, 128 - cuts[-1])).reshape(1, 128)
+        meta_all = share_plan(meta, (n_rep, n_rows, n_cols), 2).reshape(n_rep, n_dev, 128)
+        meta = lax.dynamic_index_in_dim(meta_all, lax.axis_index('rep'), 0, keepdims=False)
+        src_all, dst_all, dev_all = (meta[:, cuts[t]:cuts[t + 1]].reshape(-1) for t in range(3))
         row_meta = lax.dynamic_slice_in_dim(meta, me_row * n_cols, n_cols, axis=0)
-        row_table = row_meta[:, 2 * n_mig:2 * n_mig + seq_dev * n_pages].reshape(-1)
-        row_len = row_meta[:, 2 * n_mig + seq_dev * n_pages:].reshape(-1)
+        row_table = row_meta[:, cuts[3]:cuts[4]].reshape(-1)
+        row_len = row_meta[:, cuts[4]:cuts[5]].reshape(-1)
+
+        dev_by = meta_all[:, :, cuts[2]:cuts[3]]
+        to_row = dev_by // n_cols
+        rows4 = jnp.arange(n_rows, dtype=jnp.int32)
+        goes = (to_row[..., None] == rows4).astype(jnp.int32).sum(axis=2)
+        per_chip = goes.reshape(n_rep, n_rows, n_cols // 2, 2, n_rows).sum(axis=3)
+        leaves = rows4[:, None] != rows4[None, :]
+        z_full = ((per_chip > 2 * Z_CORE) & leaves[None, :, None, :]).any()
+        side = (jnp.arange(n_dev, dtype=jnp.int32) // 2 % 2)[None, :, None]
+        crosses = dev_by // 2 % 2 != side
+        per_side = ((to_row[..., None] == rows4) & crosses[..., None]).astype(jnp.int32).sum(axis=2)
+        y_full = (per_side.reshape(n_rep, n_rows, n_cols // 2, 2, n_rows).sum(axis=(1, 3)) > 2 * Y_CORE).any()
+        full = z_full | y_full
 
         k_rows = k_pool.reshape(n_slots * layers, prow, head_dim)
         v_rows = v_pool.reshape(n_slots * layers, prow, head_dim)
         leaving = take_pages((src_slot - base) * layers, k_rows, v_rows, layers)
-        moved = [lax.all_gather(t, ('kv2', 'kv'), tiled=True) for t in leaving]
+        pos = jnp.stack([me_row, me_col]).astype(jnp.int32)
+        z_list, y_list, unit_of = route(dst_all, dev_all, pos, n_mig, n_slots)
+        pair = [(c, c ^ 1) for c in range(n_cols)]
+        over = [(c, c ^ 2) for c in range(n_cols)]
+        z_hops = [[(r, (r + s) % n_rows) for r in range(n_rows)] for s in range(1, n_rows)]
+
+        def along_z(hops):
+            got = []
+            for h, z in zip(hops, z_hops):
+                got.append(lax.ppermute(h, 'kv2', z))
+            return got
+
+        def to_y(units, got):
+            units = units + got + [lax.ppermute(g, 'kv', pair) for g in got]
+            hop, = pick(y_list, units, [Y_CORE])
+            return units, hop
+
+        def along_y(units, hop):
+            got = lax.ppermute(hop, 'kv', over)
+            return units + [got, lax.ppermute(got, 'kv', pair)]
 
         same = row_table[:, None] == src_all[None, :]
         new_table = jnp.where(same.any(axis=1), jnp.sum(jnp.where(same, dst_all[None, :], 0), axis=1), row_table)
@@ -344,11 +671,24 @@
         order = key * n_slots + slots
         pos = jnp.sum((order[None, :] < order[:, None]).astype(jnp.int32), axis=1)
         place = pos[None, :] == jnp.arange(64, dtype=jnp.int32)[:, None]
-        info = jnp.stack([jnp.sum(jnp.where(place, t[None, :], 0), axis=1) for t in (slots, seq_of, off_of, move_of)])
+        fast_units = 2 * n_mig + 2 * (n_rows - 1) * Z_CORE + 2 * Y_CORE
+        unit = jnp.where(full, slots + fast_units, unit_of[:n_slots])
+        info = jnp.stack([jnp.sum(jnp.where(place, t[None, :], 0), axis=1) for t in (slots, seq_of, off_of, unit)])
         counts = jnp.sum((key[None, :] <= jnp.arange(4, dtype=jnp.int32)[:, None]).astype(jnp.int32), axis=1)
+
+        def all_pages(layer):
+            def collect():
+                every = lax.all_gather(leaving[layer], ('kv2', 'kv'), tiled=True)
+                return pick(jnp.maximum(move_of, 0), [every], [n_slots])[0]
+
+            return lax.cond(full, collect, lambda: uninit((n_slots, 2 * prow, head_dim), jnp.bfloat16))
 
         hidden = x_embed.reshape(2 * seq_dev, width)
         pools = None
+        units = [[own, lax.ppermute(own, 'kv', pair)] for own in leaving]
+        hops = pick(z_list, units[0], [Z_CORE] * (n_rows - 1))
+        *hops, z_list, hidden = lax.optimization_barrier((*hops, z_list, hidden))
+        got = along_z(hops)
         for layer in range(layers):
             dot = lambda a, w: jnp.dot(a, w[layer], preferred_element_type=jnp.float32)
             query = dot(hidden, w_query).astype(jnp.bfloat16).reshape(2, seq_dev, heads, head_dim)
@@ -358,13 +698,20 @@
             qkv = jnp.concatenate([per_seq(query), per_seq(k_new), per_seq(v_new)], axis=1)
             qkv = gather_rows(qkv, 'kv', n_cols, 0).reshape(row_seqs, -1, head_dim)
             dims = dict(layer=layer, n_slots=n_slots, layers=layers, page=page, kvh=kv_heads, q_group=q_group, hd=head_dim)
-            *pools, acc, ml = attend(info, counts, qkv, k_rows, v_rows, pools, None, part=0, **dims)
-            *pools, acc, ml = attend(info, counts, qkv, moved[layer], moved[layer], pools, (acc, ml), part=1, **dims)
-            o = combine(acc[:row_seqs], ml, 'kv', n_cols, 1)
+            *pools, acc, ml = attend(info, counts, qkv, [k_rows, v_rows], pools, None, part=0, **dims)
+            if layer == 0:
+                next_hops = pick(z_list, units[1], [Z_CORE] * (n_rows - 1))
+                got, acc, next_hops = lax.optimization_barrier((got, acc, next_hops))
+                next_got = along_z(next_hops)
+                all_units, hop = to_y(units[0], got)
+            all_units = along_y(all_units, hop)
+            *pools, acc, ml = attend(info, counts, qkv, all_units + [all_pages(layer)], pools, (acc, ml), part=1, **dims)
+            o = combine(acc, ml, 'kv', n_cols, 1)
+            if layer + 1 < layers:
+                next_got, o = lax.optimization_barrier((next_got, o))
+                all_units, hop = to_y(units[1], next_got)
             attn_out = jnp.swapaxes(o.reshape(seq_dev, 2, heads * head_dim), 0, 1).reshape(2 * seq_dev, heads * head_dim)
-            hidden = (hidden.astype(jnp.float32) + dot(attn_out, w_out)).astype(jnp.bfloat16)
-            up_act = jax.nn.gelu(dot(hidden, w_up)).astype(jnp.bfloat16)
-            hidden = (hidden.astype(jnp.float32) + dot(up_act, w_down)).astype(jnp.bfloat16)
+            hidden = mlp_pair(attn_out, hidden, w_out, w_up, w_down, layer, 3 + layer)
         k_out, v_out = (p.reshape(k_pool.shape) for p in pools)
         return hidden.reshape(2, seq_dev, width), k_out, v_out
 

time: 396 us -> 379 us (0.957)
  the two profiles are of different devices: /device:TPU:0 before, /device:TPU:9 now
where the time goes in v2:
time: 379 us; the launch traced here: 378 us
  Pallas kernels  206 us (54%)
  waiting for transfers between devices  92.9 us (25%)
  matrix products  29.3 us (8%)
  between operations  15.9 us (4%)
  starting transfers between devices  13.3 us (4%)
  other arithmetic  10.9 us (3%)
  local copies, waits for them, and re-layouts  9.35 us (2%)
    pallas_call x2, Pallas kernels, combine(): pl.pallas_call(body, out_shape=jax.ShapeDtypeStruct((b, r, hd), jnp.bfloa...  61.5 us
    ppermute x6, waiting for transfers between devices, along_z(): got.append(lax.ppermute(h, 'kv2', z))  57.3 us
    pallas_call x2, Pallas kernels, mlp_pair(): pl.pallas_call(body, out_shape=jax.ShapeDtypeStruct((r, d), jnp.bfloat16)...  45.4 us
    pallas_call x2, Pallas kernels, gather_rows(): pl.pallas_call(body, out_shape=jax.ShapeDtypeStruct((n,) + x.shape, x.dty...  31.9 us
    pallas_call x4, Pallas kernels, attend(): pl.pallas_call(body, out_shape=[pool, pool, jax.ShapeDtypeStruct((n_seq +...  31.1 us
    dot_general x6, matrix products, per_device(): dot = lambda a, w: jnp.dot(a, w[layer], preferred_element_type=jnp.float32)  29.3 us
    ppermute x2, waiting for transfers between devices, along_y(): got = lax.ppermute(hop, 'kv', over)  28.9 us
    pallas_call x4, Pallas kernels, pick(): pl.pallas_call(body, out_shape=[jax.ShapeDtypeStruct((size,) + tail, dtyp...  16.4 us
  transfers between devices with their start and end apart: 18, of which 11 were waited for; matrix products, arithmetic and copies ran while one was open for 12% of the time, Pallas kernels for 37%

profile of v2, /device:TPU:9, one launch (start us, length us, event | category | flops | bytes accessed | tf_op | source)
XLA Modules:
  0.0 377.7 jit_solution(9063251756598141139)
XLA Ops:
  8.4 3.2 take_pages.1
  13.3 9.3 %share_plan.1 = s32[32,1,128]{2,1,0:T(1,128)} custom-call(s32[1,128]{1,0:T(1,128)} %pad_bitcast_fusion.x_ref), custom_call_target="tpu_custom_call" | custom-call | tf_op jit(solution)/shard_map/share_plan/pallas_call | solution.py:131
  31.0 7.3 %route.1 = (s32[64]{0:T(128)}, s32[64]{0:T(128)}, s32[64]{0:T(128)}) custom-call(s32[192]{0:T(256)} %copy-done.11, s32[192]{0:T(256)} %reshape.253.dev_ref, s32[2]{0:T(128)} %pad_add_fusion.1.pos_ref), custom_call_target="tpu_custom_call" | custom-call | flops 100000000 | bytes 1000000 | tf_op jit(solution)/shard_map/route/pallas_call | solution.py:196
  41.9 5.0 %shard_map.148 = (bf16[6,512,128]{2,1,0:T(8,128)(2,1)}, bf16[6,512,128]{2,1,0:T(8,128)(2,1)}, bf16[6,512,128]{2,1,0:T(8,128)(2,1)}) custom-call(s32[64]{0:T(128)} %get-tuple-element.75.idx_ref, bf16[12,512,128]{2,1,0:T(8,128)(2,1)S(1)} %get-tuple-element.66.rest_0_, bf16[12,512,128]{2,1,0:T(8,128)(2,1)} %collective-permute-done.rest_1_), custom_call_target="tpu_custom_call" | custom-call | flops 100000000 | bytes 5000000 | tf_op jit(solution)/shard_map/pallas_call | solution.py:95
  46.9 3.9 %fusion.48 = bf16[3,8,8,128]{3,1,2,0:T(8,128)(2,1)S(1)} fusion(bf16[24,3072]{1,0:T(8,128)(2,1)S(1)} %reshape.256, bf16[2,3072,1024]{2,1,0:T(8,128)(2,1)} %param.20), kind=kOutput, calls=%fused_computation.30 | convolution fusion | flops 151019520 | bytes 6488064 | tf_op jit(solution)/shard_map/dot_general | solution.py:693
  50.9 1.5 collective-permute-start.1
  52.3 1.3 collective-permute-start.2
  54.6 7.7 %fusion.27 = bf16[3,8,24,128]{3,1,2,0:T(8,128)(2,1)S(1)} fusion(bf16[24,3072]{1,0:T(8,128)(2,1)S(1)} %reshape.256, bf16[2,3072,3072]{2,1,0:T(8,128)(2,1)} %param.18), kind=kOutput, calls=%fused_computation.23 | convolution fusion | flops 453058560 | bytes 19169280 | tf_op jit(solution)/shard_map/dot_general | solution.py:693
  64.1 16.9 %gather_rows.2 = bf16[4,12,80,128]{3,2,1,0:T(8,128)(2,1)} custom-call(bf16[12,80,128]{2,1,0:T(8,128)(2,1)} %pad_maximum_fusion.x_ref), custom_call_target="tpu_custom_call" | custom-call | tf_op jit(solution)/shard_map/gather_rows/pallas_call | solution.py:229
  81.1 5.1 %shard_map.150 = (bf16[6,512,128]{2,1,0:T(8,128)(2,1)}, bf16[6,512,128]{2,1,0:T(8,128)(2,1)}, bf16[6,512,128]{2,1,0:T(8,128)(2,1)}) custom-call(s32[64]{0:T(128)} %get-tuple-element.75.idx_ref, bf16[12,512,128]{2,1,0:T(8,128)(2,1)S(1)} %get-tuple-element.76.rest_0_, bf16[12,512,128]{2,1,0:T(8,128)(2,1)} %collective-permute-done.4.rest_1_), custom_call_target="tpu_custom_call" | custom-call | flops 100000000 | bytes 5000000 | tf_op jit(solution)/shard_map/pallas_call | solution.py:95
  86.2 10.6 %shard_map.149 = (bf16[120,256,128]{2,1,0:T(8,128)(2,1)}, bf16[120,256,128]{2,1,0:T(8,128)(2,1)}, f32[49,48,128]{2,1,0:T(8,128)}, f32[2,48,128]{2,1,0:T(8,128)}) custom-call(s32[4,64]{1,0:T(4,128)} %pad_add_fusion.info_ref, s32[4]{0:T(128)} %convert_reduce_fusion.3.cnt_ref, bf16[48,80,128]{2,1,0:T(8,128)(2,1)} %bitcast.128, ...), custom_call_target="tpu_custom_call" | custom-call | flops 400000000 | bytes 16000000 | tf_op jit(solution)/shard_map/pallas_call | solution.py:563
  96.8 22.7 %collective-permute-done.2.rest_3_ = bf16[6,512,128]{2,1,0:T(8,128)(2,1)} collective-permute-done((bf16[6,512,128]{2,1,0:T(8,128)(2,1)}, bf16[6,512,128]{2,1,0:T(8,128)(2,1)}, u32[]{:S(2)}, u32[]{:S(2)}) %collective-permute-start.2) | collective-permute-done | bytes 786464 | tf_op jit(solution)/shard_map/ppermute | solution.py:644
  119.4 2.9 collective-permute-done.3.rest_4_
  123.5 1.7 collective-permute-done.8.rest_5_
  127.5 3.1 shard_map.151
  131.9 28.9 %collective-permute-done.11.rest_8_ = bf16[10,512,128]{2,1,0:T(8,128)(2,1)} collective-permute-done((bf16[10,512,128]{2,1,0:T(8,128)(2,1)}, bf16[10,512,128]{2,1,0:T(8,128)(2,1)}, u32[]{:S(2)}, u32[]{:S(2)}) %collective-permute-start.11) | collective-permute-done | bytes 1310752 | tf_op jit(solution)/shard_map/ppermute | solution.py:653
  160.8 1.4 collective-permute-start.12
  163.2 1.5 collective-permute-start.7
  165.1 4.9 %shard_map.152 = (bf16[120,256,128]{2,1,0:T(8,128)(2,1)}, bf16[120,256,128]{2,1,0:T(8,128)(2,1)}, f32[49,48,128]{2,1,0:T(8,128)}, f32[2,48,128]{2,1,0:T(8,128)}) custom-call(s32[4,64]{1,0:T(4,128)} %pad_add_fusion.info_ref, s32[4]{0:T(128)} %convert_reduce_fusion.3.cnt_ref, ...), custom_call_target="tpu_custom_call", output_to_operand_aliasing={{0}: (14, {}), {1}: (15, {})} | custom-call | flops 400000000 | bytes 16000000 | tf_op jit(solution)/shard_map/pallas_call | solution.py:563
  170.1 30.4 %combine.2 = bf16[12,48,128]{2,1,0:T(8,128)(2,1)} custom-call(f32[49,48,128]{2,1,0:T(8,128)} %get-tuple-element.91.acc_ref, f32[2,48,128]{2,1,0:T(8,128)} %get-tuple-element.92.ml_ref), custom_call_target="tpu_custom_call" | custom-call | tf_op jit(solution)/shard_map/combine/pallas_call | solution.py:275
  200.5 29.7 %collective-permute-done.6.rest_3_ = bf16[6,512,128]{2,1,0:T(8,128)(2,1)} collective-permute-done((bf16[6,512,128]{2,1,0:T(8,128)(2,1)}, bf16[6,512,128]{2,1,0:T(8,128)(2,1)}, u32[]{:S(2)}, u32[]{:S(2)}) %collective-permute-start.6) | collective-permute-done | bytes 786464 | tf_op jit(solution)/shard_map/ppermute | solution.py:644
  230.2 1.9 collective-permute-done.7.rest_4_
  237.1 3.3 shard_map.154
  241.6 23.0 %shard_map.153 = bf16[32,3072]{1,0:T(8,128)(2,1)} custom-call(bf16[32,3072]{1,0:T(8,128)(2,1)} %pad.18.attn_ref, bf16[32,3072]{1,0:T(8,128)(2,1)} %pad.19.hid_ref, bf16[2,3072,3072]{2,1,0:T(8,128)(2,1)} %wo_ref.3, bf16[2,3072,8192]{2,1,0:T(8,128)(2,1)} %wu_ref.3, bf16[2,8192,3072]{2,1,0:T(8,128)(2,1)} %wd_ref.3), custom_call_target="tpu_custom_call" | custom-call | flops 6000000000 | bytes 60000000 | tf_op jit(solution)/shard_map/pallas_call | solution.py:388
  264.6 9.0 %fusion.24 = bf16[3,8,24,128]{3,1,2,0:T(8,128)(2,1)S(1)} fusion(bf16[2,3072,3072]{2,1,0:T(8,128)(2,1)} %param.18, bf16[32,3072]{1,0:T(8,128)(2,1)} %shard_map.153), kind=kOutput, calls=%fused_computation.22 | convolution fusion | flops 453058560 | bytes 19169280 | tf_op jit(solution)/shard_map/dot_general | solution.py:693
  273.9 4.0 %fusion.45 = bf16[3,8,8,128]{3,1,2,0:T(8,128)(2,1)S(1)} fusion(bf16[2,3072,1024]{2,1,0:T(8,128)(2,1)} %param.19, bf16[32,3072]{1,0:T(8,128)(2,1)S(1)} %copy-done.8), kind=kOutput, calls=%fused_computation.29 | convolution fusion | flops 151019520 | bytes 6488064 | tf_op jit(solution)/shard_map/dot_general | solution.py:693
  277.9 3.7 fusion.42
  282.4 14.9 %gather_rows.3 = bf16[4,12,80,128]{3,2,1,0:T(8,128)(2,1)} custom-call(bf16[12,80,128]{2,1,0:T(8,128)(2,1)} %pad_maximum_fusion.1.x_ref), custom_call_target="tpu_custom_call" | custom-call | tf_op jit(solution)/shard_map/gather_rows/pallas_call | solution.py:229
  297.4 10.7 %shard_map.155 = (bf16[120,256,128]{2,1,0:T(8,128)(2,1)}, bf16[120,256,128]{2,1,0:T(8,128)(2,1)}, f32[49,48,128]{2,1,0:T(8,128)}, f32[2,48,128]{2,1,0:T(8,128)}) custom-call(s32[4,64]{1,0:T(4,128)} %pad_add_fusion.info_ref, s32[4]{0:T(128)} %convert_reduce_fusion.3.cnt_ref, ...), custom_call_target="tpu_custom_call", output_to_operand_aliasing={{0}: (5, {}), {1}: (6, {})} | custom-call | flops 400000000 | bytes 16000000 | tf_op jit(solution)/shard_map/pallas_call | solution.py:563
  308.9 4.9 %shard_map.156 = (bf16[120,256,128]{2,1,0:T(8,128)(2,1)}, bf16[120,256,128]{2,1,0:T(8,128)(2,1)}, f32[49,48,128]{2,1,0:T(8,128)}, f32[2,48,128]{2,1,0:T(8,128)}) custom-call(s32[4,64]{1,0:T(4,128)} %pad_add_fusion.info_ref, s32[4]{0:T(128)} %convert_reduce_fusion.3.cnt_ref, ...), custom_call_target="tpu_custom_call", output_to_operand_aliasing={{0}: (14, {}), {1}: (15, {})} | custom-call | flops 400000000 | bytes 16000000 | tf_op jit(solution)/shard_map/pallas_call | solution.py:563
  313.8 31.1 %combine.3 = bf16[12,48,128]{2,1,0:T(8,128)(2,1)} custom-call(f32[49,48,128]{2,1,0:T(8,128)} %get-tuple-element.103.acc_ref, f32[2,48,128]{2,1,0:T(8,128)} %get-tuple-element.104.ml_ref), custom_call_target="tpu_custom_call" | custom-call | tf_op jit(solution)/shard_map/combine/pallas_call | solution.py:275
  346.7 22.5 %shard_map.157 = bf16[32,3072]{1,0:T(8,128)(2,1)} custom-call(bf16[32,3072]{1,0:T(8,128)(2,1)} %pad.20.attn_ref, bf16[32,3072]{1,0:T(8,128)(2,1)} %broadcast_select_fusion.hid_ref, bf16[2,3072,3072]{2,1,0:T(8,128)(2,1)} %wo_ref.3, bf16[2,3072,8192]{2,1,0:T(8,128)(2,1)} %wu_ref.3, bf16[2,8192,3072]{2,1,0:T(8,128)(2,1)} %wd_ref.3), custom_call_target="tpu_custom_call" | custom-call | flops 6000000000 | bytes 60000000 | tf_op jit(solution)/shard_map/pallas_call | solution.py:388
  (139 shorter events, 33.8 us)
Async XLA Ops:
  8.3 4.1 %copy-start.15 = (s32[12]{0:T(128)S(1)}, s32[12]{0:T(128)}, u32[]{:S(2)}) copy-start(s32[12]{0:T(128)} %param.29) | copy-start | bytes 148
  8.3 4.1 %copy-start.12 = (s32[12,2]{0,1:T(2,128)S(1)}, s32[12,2]{0,1:T(2,128)}, u32[]{:S(2)}) copy-start(s32[12,2]{0,1:T(2,128)} %param.26) | copy-start | bytes 292
  8.3 4.3 %copy-start.14 = (s32[12]{0:T(128)S(1)}, s32[12]{0:T(128)}, u32[]{:S(2)}) copy-start(s32[12]{0:T(128)} %param.28) | copy-start | bytes 148
  8.3 4.3 %copy-start.16 = (s32[12]{0:T(128)S(1)}, s32[12]{0:T(128)}, u32[]{:S(2)}) copy-start(s32[12]{0:T(128)} %param.27) | copy-start | bytes 148
  8.4 19.7 %copy-start.10 = (bf16[2,12,3072]{2,0,1:T(2,128)(2,1)S(1)}, bf16[2,12,3072]{2,0,1:T(2,128)(2,1)}, u32[]{:S(2)}) copy-start(bf16[2,12,3072]{2,0,1:T(2,128)(2,1)} %param.17) | copy-start | bytes 442372
  11.6 153.1 %copy-start.3 = (bf16[12,512,128]{2,1,0:T(8,128)(2,1)}, bf16[12,512,128]{2,1,0:T(8,128)(2,1)S(1)}, u32[]{:S(2)}) copy-start(bf16[12,512,128]{2,1,0:T(8,128)(2,1)S(1)} %get-tuple-element.66.rest_0_) | copy-start | bytes 4718596
  11.6 221.5 %copy-start = (bf16[12,512,128]{2,1,0:T(8,128)(2,1)}, bf16[12,512,128]{2,1,0:T(8,128)(2,1)S(1)}, u32[]{:S(2)}) copy-start(bf16[12,512,128]{2,1,0:T(8,128)(2,1)S(1)} %get-tuple-element.76.rest_0_) | copy-start | bytes 4718596
  11.6 30.3 %collective-permute-start = (bf16[12,512,128]{2,1,0:T(8,128)(2,1)S(1)}, bf16[12,512,128]{2,1,0:T(8,128)(2,1)}, u32[]{:S(2)}, u32[]{:S(2)}) collective-permute-start(bf16[12,512,128]{2,1,0:T(8,128)(2,1)S(1)} %get-tuple-element.66.rest_0_), channel_id=1, source_target_pairs={{0,1},{1,0},{2,3},{3,2},{4,5},{5,4},{6,7},{7,6},{8,9},{9,8},{10,11... | collective-permute-start | bytes 4718600 | tf_op jit(solution)/shard_map/ppermute | solution.py:688
  12.4 68.7 %collective-permute-start.4 = (bf16[12,512,128]{2,1,0:T(8,128)(2,1)S(1)}, bf16[12,512,128]{2,1,0:T(8,128)(2,1)}, u32[]{:S(2)}, u32[]{:S(2)}) collective-permute-start(bf16[12,512,128]{2,1,0:T(8,128)(2,1)S(1)} %get-tuple-element.76.rest_0_), channel_id=1, source_target_pairs={{0,1},{1,0},{2,3},{3,2},{4,5},{5,4},{6,7},{7,6},{8,9},{9,8},{10,11... | collective-permute-start | bytes 4718600 | tf_op jit(solution)/shard_map/ppermute | solution.py:688
  46.9 15.4 %slice-start = ((s8[12582912]{0:T(1024)(128)(4,1)}), s8[4194304]{0:T(1024)(128)(4,1)S(1)}, s32[]{:S(2)}) async-start(s8[12582912]{0:T(1024)(128)(4,1)} %bitcast.154), calls=%async_computation.2 | async-start | bytes 8388608
  50.8 11.5 %slice-start.1 = ((s8[12582912]{0:T(1024)(128)(4,1)}), s8[4194304]{0:T(1024)(128)(4,1)S(1)}, s32[]{:S(2)}) async-start(s8[12582912]{0:T(1024)(128)(4,1)} %bitcast.154), calls=%async_computation.3 | async-start | bytes 8388608
  50.8 11.5 %slice-start.2 = ((s8[12582912]{0:T(1024)(128)(4,1)}), s8[4194304]{0:T(1024)(128)(4,1)S(1)}, s32[]{:S(2)}) async-start(s8[12582912]{0:T(1024)(128)(4,1)} %bitcast.154), calls=%async_computation.4 | async-start | bytes 8388608
  50.9 45.9 %collective-permute-start.1 = (bf16[6,512,128]{2,1,0:T(8,128)(2,1)}, bf16[6,512,128]{2,1,0:T(8,128)(2,1)}, u32[]{:S(2)}, u32[]{:S(2)}) collective-permute-start(bf16[6,512,128]{2,1,0:T(8,128)(2,1)} %get-tuple-element.70), channel_id=1, source_target_pairs={{0,4},{4,8},{8,12},{12,0},{1,5},{5,9},{9,13},{13,1},{2,6},{6,10},{... | collective-permute-start | bytes 2359304 | tf_op jit(solution)/shard_map/ppermute | solution.py:644
  52.3 67.1 %collective-permute-start.2 = (bf16[6,512,128]{2,1,0:T(8,128)(2,1)}, bf16[6,512,128]{2,1,0:T(8,128)(2,1)}, u32[]{:S(2)}, u32[]{:S(2)}) collective-permute-start(bf16[6,512,128]{2,1,0:T(8,128)(2,1)} %get-tuple-element.71), channel_id=1, source_target_pairs={{0,8},{4,12},{8,0},{12,4},{1,9},{5,13},{9,1},{13,5},{2,10},{6,14},... | collective-permute-start | bytes 2359304 | tf_op jit(solution)/shard_map/ppermute | solution.py:644
  53.6 68.7 %collective-permute-start.3 = (bf16[6,512,128]{2,1,0:T(8,128)(2,1)}, bf16[6,512,128]{2,1,0:T(8,128)(2,1)}, u32[]{:S(2)}, u32[]{:S(2)}) collective-permute-start(bf16[6,512,128]{2,1,0:T(8,128)(2,1)} %get-tuple-element.72), channel_id=1, source_target_pairs={{0,12},{4,0},{8,4},{12,8},{1,13},{5,1},{9,5},{13,9},{2,14},{6,2},{... | collective-permute-start | bytes 2359304 | tf_op jit(solution)/shard_map/ppermute | solution.py:644
  122.4 2.8 collective-permute-start.8
  123.0 3.4 collective-permute-start.9
  123.0 4.5 %collective-permute-start.10 = (bf16[6,512,128]{2,1,0:T(8,128)(2,1)}, bf16[6,512,128]{2,1,0:T(8,128)(2,1)}, u32[]{:S(2)}, u32[]{:S(2)}) collective-permute-start(bf16[6,512,128]{2,1,0:T(8,128)(2,1)} %collective-permute-done.3.rest_4_), channel_id=1, source_target_pairs={{0,1},{1,0},{2,3},{3,2},{4,5},{5,4},{6,7},{7,6},{8,9},{9,8},{10,11... | collective-permute-start | bytes 2359304 | tf_op jit(solution)/shard_map/ppermute | solution.py:648
  130.6 30.2 %collective-permute-start.11 = (bf16[10,512,128]{2,1,0:T(8,128)(2,1)}, bf16[10,512,128]{2,1,0:T(8,128)(2,1)}, u32[]{:S(2)}, u32[]{:S(2)}) collective-permute-start(bf16[10,512,128]{2,1,0:T(8,128)(2,1)} %shard_map.151), channel_id=1, source_target_pairs={{0,2},{1,3},{2,0},{3,1},{4,6},{5,7},{6,4},{7,5},{8,10},{9,11},{10,... | collective-permute-start | bytes 3932168 | tf_op jit(solution)/shard_map/ppermute | solution.py:653
  160.8 4.4 %collective-permute-start.12 = (bf16[10,512,128]{2,1,0:T(8,128)(2,1)}, bf16[10,512,128]{2,1,0:T(8,128)(2,1)}, u32[]{:S(2)}, u32[]{:S(2)}) collective-permute-start(bf16[10,512,128]{2,1,0:T(8,128)(2,1)} %collective-permute-done.11.rest_8_), channel_id=1, source_target_pairs={{0,1},{1,0},{2,3},{3,2},{4,5},{5,4},{6,7},{7,6},{8,9},{9,8},{10,11... | collective-permute-start | bytes 3932168 | tf_op jit(solution)/shard_map/ppermute | solution.py:654
  162.1 38.3 %collective-permute-start.5 = (bf16[6,512,128]{2,1,0:T(8,128)(2,1)}, bf16[6,512,128]{2,1,0:T(8,128)(2,1)}, u32[]{:S(2)}, u32[]{:S(2)}) collective-permute-start(bf16[6,512,128]{2,1,0:T(8,128)(2,1)} %get-tuple-element.80), channel_id=1, source_target_pairs={{0,4},{4,8},{8,12},{12,0},{1,5},{5,9},{9,13},{13,1},{2,6},{6,10},{... | collective-permute-start | bytes 2359304 | tf_op jit(solution)/shard_map/ppermute | solution.py:644
  162.1 68.0 %collective-permute-start.6 = (bf16[6,512,128]{2,1,0:T(8,128)(2,1)}, bf16[6,512,128]{2,1,0:T(8,128)(2,1)}, u32[]{:S(2)}, u32[]{:S(2)}) collective-permute-start(bf16[6,512,128]{2,1,0:T(8,128)(2,1)} %get-tuple-element.81), channel_id=1, source_target_pairs={{0,8},{4,12},{8,0},{12,4},{1,9},{5,13},{9,1},{13,5},{2,10},{6,14},... | collective-permute-start | bytes 2359304 | tf_op jit(solution)/shard_map/ppermute | solution.py:644
  163.2 68.9 %collective-permute-start.7 = (bf16[6,512,128]{2,1,0:T(8,128)(2,1)}, bf16[6,512,128]{2,1,0:T(8,128)(2,1)}, u32[]{:S(2)}, u32[]{:S(2)}) collective-permute-start(bf16[6,512,128]{2,1,0:T(8,128)(2,1)} %get-tuple-element.82), channel_id=1, source_target_pairs={{0,12},{4,0},{8,4},{12,8},{1,13},{5,1},{9,5},{13,9},{2,14},{6,2},{... | collective-permute-start | bytes 2359304 | tf_op jit(solution)/shard_map/ppermute | solution.py:644
  232.1 2.8 collective-permute-start.13
  232.6 3.2 collective-permute-start.14
  232.7 4.5 %collective-permute-start.15 = (bf16[6,512,128]{2,1,0:T(8,128)(2,1)}, bf16[6,512,128]{2,1,0:T(8,128)(2,1)}, u32[]{:S(2)}, u32[]{:S(2)}) collective-permute-start(bf16[6,512,128]{2,1,0:T(8,128)(2,1)} %collective-permute-done.7.rest_4_), channel_id=1, source_target_pairs={{0,1},{1,0},{2,3},{3,2},{4,5},{5,4},{6,7},{7,6},{8,9},{9,8},{10,11... | collective-permute-start | bytes 2359304 | tf_op jit(solution)/shard_map/ppermute | solution.py:648
  240.4 33.3 %collective-permute-start.16 = (bf16[10,512,128]{2,1,0:T(8,128)(2,1)}, bf16[10,512,128]{2,1,0:T(8,128)(2,1)S(1)}, u32[]{:S(2)}, u32[]{:S(2)}) collective-permute-start(bf16[10,512,128]{2,1,0:T(8,128)(2,1)} %shard_map.154), channel_id=1, source_target_pairs={{0,2},{1,3},{2,0},{3,1},{4,6},{5,7},{6,4},{7,5},{8,10},{9,11},{10,... | collective-permute-start | bytes 3932168 | tf_op jit(solution)/shard_map/ppermute | solution.py:653
  264.6 9.3 %copy-start.8 = (bf16[32,3072]{1,0:T(8,128)(2,1)S(1)}, bf16[32,3072]{1,0:T(8,128)(2,1)}, u32[]{:S(2)}) copy-start(bf16[32,3072]{1,0:T(8,128)(2,1)} %shard_map.153) | copy-start | bytes 589828
  273.7 23.7 %copy-start.7 = (bf16[10,512,128]{2,1,0:T(8,128)(2,1)}, bf16[10,512,128]{2,1,0:T(8,128)(2,1)S(1)}, u32[]{:S(2)}) copy-start(bf16[10,512,128]{2,1,0:T(8,128)(2,1)S(1)} %collective-permute-done.16.rest_8_) | copy-start | bytes 3932164
  273.7 35.2 %collective-permute-start.17 = (bf16[10,512,128]{2,1,0:T(8,128)(2,1)S(1)}, bf16[10,512,128]{2,1,0:T(8,128)(2,1)}, u32[]{:S(2)}, u32[]{:S(2)}) collective-permute-start(bf16[10,512,128]{2,1,0:T(8,128)(2,1)S(1)} %collective-permute-done.16.rest_8_), channel_id=1, source_target_pairs={{0,1},{1,0},{2,3},{3,2},{4,5},{5,4},{6,7},{7,6},{8,9},{9,8},{10,11... | collective-permute-start | bytes 3932168 | tf_op jit(solution)/shard_map/ppermute | solution.py:654
  297.4 10.7 %copy-start.13 = (pred[32]{0:T(512)(128)(4,1)S(1)}, pred[32]{0:T(512)(128)(4,1)}, u32[]{:S(2)}) copy-start(pred[32]{0:T(512)(128)(4,1)} %constant.146.clone.1) | copy-start | bytes 100
  297.4 11.5 %copy-start.1 = (bf16[12,512,128]{2,1,0:T(8,128)(2,1)S(1)}, bf16[12,512,128]{2,1,0:T(8,128)(2,1)}, u32[]{:S(2)}) copy-start(bf16[12,512,128]{2,1,0:T(8,128)(2,1)} %copy-done) | copy-start | bytes 4718596
  (4 other events, 7.6 us)

commit v3 on v2

--- a/solution.py
+++ b/solution.py
@@ -139,18 +139,56 @@
     )(x)
 
 
+def route_z(own, pair, pos):
+    n_mig = own.shape[0]
+
+    def body(own_ref, pair_ref, pos_ref, z_ref, cnt):
+        row, core = pos_ref[0], pos_ref[1] & 1
+
+        @pl.loop(0, 3 * Z_CORE)
+        def _(i):
+            z_ref[i] = 0
+
+        for i in range(4):
+            cnt[i] = 0
+
+        @pl.loop(0, 2 * n_mig)
+        def _(i):
+            second = (i >= n_mig).astype(jnp.int32)
+            e = i - second * n_mig
+            mine = second == core
+            dd = jnp.where(mine, own_ref[e], pair_ref[e])
+            di = dd >> 2
+            k = cnt[di]
+            cnt[di] = k + 1
+            shift = (di - row) & 3
+
+            @pl.when((shift != 0) & ((k & 1) == core) & (k < 2 * Z_CORE))
+            def _():
+                z_ref[(shift - 1) * Z_CORE + (k >> 1)] = jnp.where(mine, e, n_mig + e)
+
+    smem = pl.BlockSpec(memory_space=pltpu.SMEM)
+    return pl.pallas_call(
+        body,
+        out_shape=jax.ShapeDtypeStruct((64,), jnp.int32),
+        in_specs=[smem] * 3,
+        out_specs=smem,
+        scratch_shapes=[pltpu.SMEM((4,), jnp.int32)],
+        name="route_z",
+    )(own, pair, pos)
+
+
 def route(dst, dev, pos, n_mig, n_slots):
     n_dev = dev.shape[0] // n_mig
     z_at, y_at = 2 * n_mig, 2 * n_mig + 2 * 3 * Z_CORE
 
-    def body(dst_ref, dev_ref, pos_ref, z_ref, y_ref, s_ref, cnt, cnt2):
+    def body(dst_ref, dev_ref, pos_ref, y_ref, s_ref, cnt, cnt2):
         row, colm = pos_ref[0], pos_ref[1]
         half, core = colm >> 1, colm & 1
         me = row * 4 + colm
 
         @pl.loop(0, 64)
         def _(i):
-            z_ref[i] = 0
             y_ref[i] = 0
             s_ref[i] = -1
             cnt[i] = 0
@@ -174,30 +212,29 @@
                 c2 = di * 2 + sy
                 k2 = cnt2[c2]
                 cnt2[c2] = k2 + cross
-                shift = (di - si) & 3
-                at = jnp.where(sc == core, e, n_mig + e)
-                z_slot = (shift - 1) * Z_CORE + (k >> 1)
-                here = jnp.where(shift == 0, at, z_at + z_slot + jnp.where((k & 1) == core, 0, 3 * Z_CORE))
-
-                @pl.when((si == row) & (sy == half) & (shift != 0) & ((k & 1) == core) & (k < 2 * Z_CORE))
+
+                @pl.when(di == row)
                 def _():
-                    z_ref[z_slot] = at
-
-                @pl.when((di == row) & (sy == half) & (cross == 1) & ((k2 & 1) == core) & (k2 < 2 * Y_CORE))
-                def _():
-                    y_ref[k2 >> 1] = jnp.minimum(here, y_at - 1)
-
-                @pl.when(dd == me)
-                def _():
-                    by_y = y_at + (k2 >> 1) + jnp.where((k2 & 1) == core, 0, Y_CORE)
-                    s_ref[dst_ref[d * n_mig + e] - me * n_slots] = jnp.where(cross == 1, by_y, here)
+                    shift = (di - si) & 3
+                    at = jnp.where(sc == core, e, n_mig + e)
+                    z_slot = (shift - 1) * Z_CORE + (k >> 1)
+                    here = jnp.where(shift == 0, at, z_at + z_slot + jnp.where((k & 1) == core, 0, 3 * Z_CORE))
+
+                    @pl.when((sy == half) & (cross == 1) & ((k2 & 1) == core) & (k2 < 2 * Y_CORE))
+                    def _():
+                        y_ref[k2 >> 1] = jnp.minimum(here, y_at - 1)
+
+                    @pl.when(dd == me)
+                    def _():
+                        by_y = y_at + (k2 >> 1) + jnp.where((k2 & 1) == core, 0, Y_CORE)
+                        s_ref[dst_ref[d * n_mig + e] - me * n_slots] = jnp.where(cross == 1, by_y, here)
 
     smem = pl.BlockSpec(memory_space=pltpu.SMEM)
     return pl.pallas_call(
         body,
-        out_shape=[jax.ShapeDtypeStruct((64,), jnp.int32)] * 3,
+        out_shape=[jax.ShapeDtypeStruct((64,), jnp.int32)] * 2,
         in_specs=[smem] * 3,
-        out_specs=[smem] * 3,
+        out_specs=[smem] * 2,
         scratch_shapes=[pltpu.SMEM((64,), jnp.int32), pltpu.SMEM((8,), jnp.int32)],
         cost_estimate=pl.CostEstimate(flops=100_000_000, bytes_accessed=1_000_000, transcendentals=0),
         name="route",
@@ -403,7 +440,9 @@
     return out[:rows]
 
 
-def attend(info, counts, qkv, sources, prev_pools, state, layer, part, n_slots, layers, page, kvh, q_group, hd):
+def attend(info, counts, qkv, pools_in, unit_srcs, first_unit, prev_pools, state, layer, part, n_slots, layers, page, kvh, q_group, hd):
+    sources = list(pools_in) + list(unit_srcs)
+    n_pool = len(pools_in)
     prow = page * kvh
     qr = 2 * kvh * q_group
     n_seq = qkv.shape[0]
@@ -427,19 +466,23 @@
             return (pltpu.make_async_copy(k_page, kbuf.at[i], isem.at[0, i]),
                     pltpu.make_async_copy(v_page, vbuf.at[i], isem.at[1, i]))
 
-        def loads(i):
-            if part:
-                return load_from(ins[0].at[0, pl.ds(0, prow)], ins[0].at[0, pl.ds(prow, prow)], i)
+        def from_pool(i):
             at = info_ref[0, i] * layers + layer
             return load_from(ins[0].at[at], ins[1].at[at], i)
 
+        def loads(i):
+            if n_pool:
+                return from_pool(i)
+            return load_from(ins[0].at[0, pl.ds(0, prow)], ins[0].at[0, pl.ds(prow, prow)], i)
+
         def start_loads(i):
-            if not part:
-                for cp in loads(i):
+            at, first = info_ref[3, i], first_unit
+            if n_pool and unit_srcs:
+                pl.when(at < 0)(lambda: [cp.start() for cp in from_pool(i)] and None)
+            elif n_pool:
+                for cp in from_pool(i):
                     cp.start()
-                return
-            at, first = info_ref[3, i], 0
-            for ref in ins:
+            for ref in ins[n_pool:]:
                 last = first + ref.shape[0]
 
                 @pl.when((at >= first) & (at < last))
@@ -603,6 +646,17 @@
         me = me_row * n_cols + me_col
         base = me * n_slots
 
+        k_rows = k_pool.reshape(n_slots * layers, prow, head_dim)
+        v_rows = v_pool.reshape(n_slots * layers, prow, head_dim)
+        pair = [(c, c ^ 1) for c in range(n_cols)]
+        over = [(c, c ^ 2) for c in range(n_cols)]
+        z_hops = [[(r, (r + s) % n_rows) for r in range(n_rows)] for s in range(1, n_rows)]
+        pos = jnp.stack([me_row, me_col]).astype(jnp.int32)
+        dev_own = dst_slot // n_slots
+        leaving = take_pages((src_slot - base) * layers, k_rows, v_rows, layers)
+        units = [[leaving[0], lax.ppermute(leaving[0], 'kv', pair)]]
+        dev_pair = lax.ppermute(dev_own, 'kv', pair)
+
         n_rep = mesh.shape['rep']
         words = [src_slot, dst_slot, dst_slot // n_slots, old_table.reshape(-1), seq_len]
         cuts = [0]
@@ -610,6 +664,14 @@
             cuts.append(cuts[-1] + w.shape[0])
         meta = jnp.pad(jnp.concatenate(words), (0, 128 - cuts[-1])).reshape(1, 128)
         meta_all = share_plan(meta, (n_rep, n_rows, n_cols), 2).reshape(n_rep, n_dev, 128)
+
+        meta_all, pos = lax.optimization_barrier((meta_all, pos))
+        z_list = route_z(dev_own, dev_pair, pos)
+        hops = pick(z_list, units[0], [Z_CORE] * (n_rows - 1))
+        hops, z_list, hidden, meta_all, later = lax.optimization_barrier(
+            (hops, z_list, x_embed.reshape(2 * seq_dev, width), meta_all, leaving[1:]))
+        units += [[own, lax.ppermute(own, 'kv', pair)] for own in later]
+
         meta = lax.dynamic_index_in_dim(meta_all, lax.axis_index('rep'), 0, keepdims=False)
         src_all, dst_all, dev_all = (meta[:, cuts[t]:cuts[t + 1]].reshape(-1) for t in range(3))
         row_meta = lax.dynamic_slice_in_dim(meta, me_row * n_cols, n_cols, axis=0)
@@ -629,14 +691,7 @@
         y_full = (per_side.reshape(n_rep, n_rows, n_cols // 2, 2, n_rows).sum(axis=(1, 3)) > 2 * Y_CORE).any()
         full = z_full | y_full
 
-        k_rows = k_pool.reshape(n_slots * layers, prow, head_dim)
-        v_rows = v_pool.reshape(n_slots * layers, prow, head_dim)
-        leaving = take_pages((src_slot - base) * layers, k_rows, v_rows, layers)
-        pos = jnp.stack([me_row, me_col]).astype(jnp.int32)
-        z_list, y_list, unit_of = route(dst_all, dev_all, pos, n_mig, n_slots)
-        pair = [(c, c ^ 1) for c in range(n_cols)]
-        over = [(c, c ^ 2) for c in range(n_cols)]
-        z_hops = [[(r, (r + s) % n_rows) for r in range(n_rows)] for s in range(1, n_rows)]
+        y_list, unit_of = route(dst_all, dev_all, pos, n_mig, n_slots)
 
         def along_z(hops):
             got = []
@@ -644,14 +699,12 @@
                 got.append(lax.ppermute(h, 'kv2', z))
             return got
 
-        def to_y(units, got):
-            units = units + got + [lax.ppermute(g, 'kv', pair) for g in got]
-            hop, = pick(y_list, units, [Y_CORE])
-            return units, hop
-
-        def along_y(units, hop):
+        def swap(units, got):
+            return units + got + [lax.ppermute(g, 'kv', pair) for g in got]
+
+        def along_y(hop):
             got = lax.ppermute(hop, 'kv', over)
-            return units + [got, lax.ppermute(got, 'kv', pair)]
+            return [got, lax.ppermute(got, 'kv', pair)]
 
         same = row_table[:, None] == src_all[None, :]
         new_table = jnp.where(same.any(axis=1), jnp.sum(jnp.where(same, dst_all[None, :], 0), axis=1), row_table)
@@ -667,14 +720,20 @@
         len_of = jnp.sum(jnp.where(seq_one, row_len[None, :], 0), axis=1)
         off_of = len_of - (slot_cell % n_pages) * page
         off_of = jnp.where(used & (off_of >= 0) & (off_of < page), off_of, 2 * page)
-        key = is_mig.astype(jnp.int32) * 2 + (~used).astype(jnp.int32)
-        order = key * n_slots + slots
-        pos = jnp.sum((order[None, :] < order[:, None]).astype(jnp.int32), axis=1)
-        place = pos[None, :] == jnp.arange(64, dtype=jnp.int32)[:, None]
-        fast_units = 2 * n_mig + 2 * (n_rows - 1) * Z_CORE + 2 * Y_CORE
-        unit = jnp.where(full, slots + fast_units, unit_of[:n_slots])
-        info = jnp.stack([jnp.sum(jnp.where(place, t[None, :], 0), axis=1) for t in (slots, seq_of, off_of, unit)])
-        counts = jnp.sum((key[None, :] <= jnp.arange(4, dtype=jnp.int32)[:, None]).astype(jnp.int32), axis=1)
+        y_at = 2 * n_mig + 2 * (n_rows - 1) * Z_CORE
+        unit = jnp.where(is_mig, jnp.where(full, slots + y_at + 2 * Y_CORE, unit_of[:n_slots]), -1)
+
+        def lists(cls, n_cls):
+            key = cls * 2 + (~used).astype(jnp.int32)
+            order = key * n_slots + slots
+            at = jnp.sum((order[None, :] < order[:, None]).astype(jnp.int32), axis=1)
+            place = at[None, :] == jnp.arange(64, dtype=jnp.int32)[:, None]
+            info = jnp.stack([jnp.sum(jnp.where(place, t[None, :], 0), axis=1) for t in (slots, seq_of, off_of, unit)])
+            counts = jnp.sum((key[None, :] <= jnp.arange(2 * n_cls, dtype=jnp.int32)[:, None]).astype(jnp.int32), axis=1)
+            return info, counts
+
+        by_class = lists(is_mig.astype(jnp.int32) + (unit >= y_at).astype(jnp.int32), 3)
+        by_use = lists(jnp.zeros_like(slots), 1)
 
         def all_pages(layer):
             def collect():
@@ -683,11 +742,7 @@
 
             return lax.cond(full, collect, lambda: uninit((n_slots, 2 * prow, head_dim), jnp.bfloat16))
 
-        hidden = x_embed.reshape(2 * seq_dev, width)
         pools = None
-        units = [[own, lax.ppermute(own, 'kv', pair)] for own in leaving]
-        hops = pick(z_list, units[0], [Z_CORE] * (n_rows - 1))
-        *hops, z_list, hidden = lax.optimization_barrier((*hops, z_list, hidden))
         got = along_z(hops)
         for layer in range(layers):
             dot = lambda a, w: jnp.dot(a, w[layer], preferred_element_type=jnp.float32)
@@ -698,18 +753,25 @@
             qkv = jnp.concatenate([per_seq(query), per_seq(k_new), per_seq(v_new)], axis=1)
             qkv = gather_rows(qkv, 'kv', n_cols, 0).reshape(row_seqs, -1, head_dim)
             dims = dict(layer=layer, n_slots=n_slots, layers=layers, page=page, kvh=kv_heads, q_group=q_group, hd=head_dim)
-            *pools, acc, ml = attend(info, counts, qkv, [k_rows, v_rows], pools, None, part=0, **dims)
             if layer == 0:
+                *pools, acc, ml = attend(*by_class, qkv, [k_rows, v_rows], [], 0, pools, None, part=0, **dims)
                 next_hops = pick(z_list, units[1], [Z_CORE] * (n_rows - 1))
                 got, acc, next_hops = lax.optimization_barrier((got, acc, next_hops))
                 next_got = along_z(next_hops)
-                all_units, hop = to_y(units[0], got)
-            all_units = along_y(all_units, hop)
-            *pools, acc, ml = attend(info, counts, qkv, all_units + [all_pages(layer)], pools, (acc, ml), part=1, **dims)
+                all_units = swap(units[0], got)
+                hop, = pick(y_list, all_units, [Y_CORE])
+                last = along_y(hop) + [all_pages(0)]
+                *pools, acc, ml = attend(*by_class, qkv, [], all_units, 0, pools, (acc, ml), part=1, **dims)
+                *pools, acc, ml = attend(*by_class, qkv, [], last, y_at, pools, (acc, ml), part=2, **dims)
+            else:
+                srcs = all_units + along_y(hop) + [all_pages(layer)]
+                *pools, acc, ml = attend(*by_use, qkv, [k_rows, v_rows], srcs, 0, pools, None, part=0, **dims)
             o = combine(acc, ml, 'kv', n_cols, 1)
             if layer + 1 < layers:
                 next_got, o = lax.optimization_barrier((next_got, o))
-                all_units, hop = to_y(units[1], next_got)
+                all_units = swap(units[layer + 1], next_got)
+                hop, = pick(y_list, all_units, [Y_CORE])
+                hop, o = lax.optimization_barrier((hop, o))
             attn_out = jnp.swapaxes(o.reshape(seq_dev, 2, heads * head_dim), 0, 1).reshape(2 * seq_dev, heads * head_dim)
             hidden = mlp_pair(attn_out, hidden, w_out, w_up, w_down, layer, 3 + layer)
         k_out, v_out = (p.reshape(k_pool.shape) for p in pools)

time: 379 us -> 380 us (level)
  waiting for transfers between devices: 92.9 us -> 78 us
  other arithmetic: 10.9 us -> 17 us
    ppermute x6, waiting for transfers between devices: 57.3 us -> 43.4 us  [along_z(): got.append(lax.ppermute(h, 'kv2', z))]
  transfers between devices with their start and end apart: 18 -> 19, of which waited for: 11 -> 10; matrix products, arithmetic and copies ran while one was open for 12% -> 10% of each run, Pallas kernels for 37% -> 34%
where the time goes in v3:
time: 380 us; the launch traced here: 379 us
  Pallas kernels  208 us (55%)
  waiting for transfers between devices  78 us (21%)
  matrix products  32.9 us (9%)
  other arithmetic  17 us (4%)
  between operations  15.8 us (4%)
  starting transfers between devices  14.4 us (4%)
  local copies, waits for them, and re-layouts  12.9 us (3%)
    pallas_call x2, Pallas kernels, combine(): pl.pallas_call(body, out_shape=jax.ShapeDtypeStruct((b, r, hd), jnp.bfloa...  60.2 us
    pallas_call x2, Pallas kernels, mlp_pair(): pl.pallas_call(body, out_shape=jax.ShapeDtypeStruct((r, d), jnp.bfloat16)...  45.4 us
    ppermute x6, waiting for transfers between devices, along_z(): got.append(lax.ppermute(h, 'kv2', z))  43.4 us
    pallas_call x4, Pallas kernels, attend(): pl.pallas_call(body, out_shape=[pool, pool, jax.ShapeDtypeStruct((n_seq +...  33.3 us
    dot_general x6, matrix products, per_device(): dot = lambda a, w: jnp.dot(a, w[layer], preferred_element_type=jnp.float32)  32.9 us
    pallas_call x2, Pallas kernels, gather_rows(): pl.pallas_call(body, out_shape=jax.ShapeDtypeStruct((n,) + x.shape, x.dty...  31.2 us
    ppermute x2, waiting for transfers between devices, along_y(): got = lax.ppermute(hop, 'kv', over)  28.7 us
    pallas_call x4, Pallas kernels, pick(): pl.pallas_call(body, out_shape=[jax.ShapeDtypeStruct((size,) + tail, dtyp...  16.4 us
  transfers between devices with their start and end apart: 19, of which 10 were waited for; matrix products, arithmetic and copies ran while one was open for 10% of the time, Pallas kernels for 34%

profile of v3, /device:TPU:9, one launch (start us, length us, event | category | flops | bytes accessed | tf_op | source)
XLA Modules:
  0.0 378.5 jit_solution(12664320919203866337)
XLA Ops:
  8.4 3.2 take_pages.1
  13.3 9.3 %share_plan.1 = s32[32,1,128]{2,1,0:T(1,128)} custom-call(s32[1,128]{1,0:T(1,128)} %pad_bitcast_fusion.x_ref), custom_call_target="tpu_custom_call" | custom-call | tf_op jit(solution)/shard_map/share_plan/pallas_call | solution.py:131
  24.5 1.7 route_z.1.idx_ref
  26.2 5.0 %shard_map.148 = (bf16[6,512,128]{2,1,0:T(8,128)(2,1)}, bf16[6,512,128]{2,1,0:T(8,128)(2,1)}, bf16[6,512,128]{2,1,0:T(8,128)(2,1)}) custom-call(s32[64]{0:T(128)} %route_z.1.idx_ref, bf16[12,512,128]{2,1,0:T(8,128)(2,1)S(1)} %get-tuple-element.70.rest_0_, bf16[12,512,128]{2,1,0:T(8,128)(2,1)} %collective-permute-done.1.rest_1_), custom_call_target="tpu_custom_call" | custom-call | flops 100000000 | bytes 5000000 | tf_op jit(solution)/shard_map/pallas_call | solution.py:95
  31.2 3.7 fusion.51
  34.9 3.7 fusion.48
  38.7 8.4 %fusion.27 = bf16[3,8,24,128]{3,1,2,0:T(8,128)(2,1)} fusion(bf16[24,3072]{1,0:T(8,128)(2,1)S(1)} %reshape.243, bf16[2,3072,3072]{2,1,0:T(8,128)(2,1)} %param.18), kind=kOutput, calls=%fused_computation.23 | convolution fusion | flops 453058560 | bytes 19169280 | tf_op jit(solution)/shard_map/dot_general | solution.py:748
  64.8 16.1 %gather_rows.2 = bf16[4,12,80,128]{3,2,1,0:T(8,128)(2,1)} custom-call(bf16[12,80,128]{2,1,0:T(8,128)(2,1)} %pad_maximum_fusion.x_ref), custom_call_target="tpu_custom_call" | custom-call | tf_op jit(solution)/shard_map/gather_rows/pallas_call | solution.py:266
  83.4 6.9 %route.1 = (s32[64]{0:T(128)}, s32[64]{0:T(128)}) custom-call(s32[192]{0:T(256)} %copy-done.12, s32[192]{0:T(256)} %reshape.246.dev_ref, s32[2]{0:T(128)} %pad_add_fusion.2.pos_ref), custom_call_target="tpu_custom_call" | custom-call | flops 100000000 | bytes 1000000 | tf_op jit(solution)/shard_map/route/pallas_call | solution.py:233
  94.1 10.6 %shard_map.149 = (bf16[120,256,128]{2,1,0:T(8,128)(2,1)}, bf16[120,256,128]{2,1,0:T(8,128)(2,1)}, f32[49,48,128]{2,1,0:T(8,128)}, f32[2,48,128]{2,1,0:T(8,128)}) custom-call(s32[4,64]{1,0:T(4,128)} %pad_add_fusion.1.info_ref, s32[6]{0:T(128)} %convert_reduce_fusion.4.cnt_ref, bf16[48,80,128]{2,1,0:T(8,128)(2,1)} %bitcast.132, ...), custom_call_target="tpu_custom_call" | custom-call | flops 400000000 | bytes 16000000 | tf_op jit(solution)/shard_map/pallas_call | solution.py:606
  104.7 5.0 %shard_map.150 = (bf16[6,512,128]{2,1,0:T(8,128)(2,1)}, bf16[6,512,128]{2,1,0:T(8,128)(2,1)}, bf16[6,512,128]{2,1,0:T(8,128)(2,1)}) custom-call(s32[64]{0:T(128)} %route_z.1.idx_ref, bf16[12,512,128]{2,1,0:T(8,128)(2,1)S(1)} %get-tuple-element.79.rest_0_.rest_2_, bf16[12,512,128]{2,1,0:T(8,128)(2,1)} %collective-permute-done.2.rest_1_.rest_3_), custom_call_target="tpu_custom_call" | custom-call | flops 100000000 | bytes 5000000 | tf_op jit(solution)/shard_map/pallas_call | solution.py:95
  109.7 15.5 %collective-permute-done.4.rest_3_ = bf16[6,512,128]{2,1,0:T(8,128)(2,1)} collective-permute-done((bf16[6,512,128]{2,1,0:T(8,128)(2,1)}, bf16[6,512,128]{2,1,0:T(8,128)(2,1)}, u32[]{:S(2)}, u32[]{:S(2)}) %collective-permute-start.4) | collective-permute-done | bytes 786464 | tf_op jit(solution)/shard_map/ppermute | solution.py:699
  125.2 2.4 collective-permute-done.5.rest_4_
  128.6 1.7 collective-permute-done.10.rest_6_
  132.6 3.1 shard_map.151
  135.7 1.6 collective-permute-start.12
  137.2 28.7 %collective-permute-done.12.rest_0_ = bf16[10,512,128]{2,1,0:T(8,128)(2,1)} collective-permute-done((bf16[10,512,128]{2,1,0:T(8,128)(2,1)}, bf16[10,512,128]{2,1,0:T(8,128)(2,1)}, u32[]{:S(2)}, u32[]{:S(2)}) %collective-permute-start.12) | collective-permute-done | bytes 1310752 | tf_op jit(solution)/shard_map/ppermute | solution.py:706
  168.3 1.5 collective-permute-start.8
  169.8 4.9 %shard_map.152 = (bf16[120,256,128]{2,1,0:T(8,128)(2,1)}, bf16[120,256,128]{2,1,0:T(8,128)(2,1)}, f32[49,48,128]{2,1,0:T(8,128)}, f32[2,48,128]{2,1,0:T(8,128)}) custom-call(s32[4,64]{1,0:T(4,128)} %pad_add_fusion.1.info_ref, s32[6]{0:T(128)} %convert_reduce_fusion.4.cnt_ref, ...), custom_call_target="tpu_custom_call", output_to_operand_aliasing={{0}: (11, {}), {1}: (12, {})} | custom-call | flops 400000000 | bytes 16000000 | tf_op jit(solution)/shard_map/pallas_call | solution.py:606
  174.7 5.0 %shard_map.153 = (bf16[120,256,128]{2,1,0:T(8,128)(2,1)}, bf16[120,256,128]{2,1,0:T(8,128)(2,1)}, f32[49,48,128]{2,1,0:T(8,128)}, f32[2,48,128]{2,1,0:T(8,128)}) custom-call(s32[4,64]{1,0:T(4,128)} %pad_add_fusion.1.info_ref, s32[6]{0:T(128)} %convert_reduce_fusion.4.cnt_ref, ...), custom_call_target="tpu_custom_call", output_to_operand_aliasing={{0}: (6, {}), {1}: (7, {})} | custom-call | flops 400000000 | bytes 16000000 | tf_op jit(solution)/shard_map/pallas_call | solution.py:606
  179.7 32.0 %combine.2 = bf16[12,48,128]{2,1,0:T(8,128)(2,1)} custom-call(f32[49,48,128]{2,1,0:T(8,128)} %get-tuple-element.103.acc_ref, f32[2,48,128]{2,1,0:T(8,128)} %get-tuple-element.104.ml_ref), custom_call_target="tpu_custom_call" | custom-call | tf_op jit(solution)/shard_map/combine/pallas_call | solution.py:312
  211.8 23.6 %collective-permute-done.7.rest_3_.rest_5_ = bf16[6,512,128]{2,1,0:T(8,128)(2,1)} collective-permute-done((bf16[6,512,128]{2,1,0:T(8,128)(2,1)}, bf16[6,512,128]{2,1,0:T(8,128)(2,1)}, u32[]{:S(2)}, u32[]{:S(2)}) %collective-permute-start.7) | collective-permute-done | bytes 786464 | tf_op jit(solution)/shard_map/ppermute | solution.py:699
  235.3 1.9 collective-permute-done.8.rest_4_.rest_6_
  242.2 3.2 shard_map.154
  247.6 23.0 %shard_map.155 = bf16[32,3072]{1,0:T(8,128)(2,1)} custom-call(bf16[32,3072]{1,0:T(8,128)(2,1)} %pad.18.attn_ref, bf16[32,3072]{1,0:T(8,128)(2,1)} %pad.19.hid_ref, bf16[2,3072,3072]{2,1,0:T(8,128)(2,1)} %wo_ref.3, bf16[2,3072,8192]{2,1,0:T(8,128)(2,1)} %wu_ref.3, bf16[2,8192,3072]{2,1,0:T(8,128)(2,1)} %wd_ref.3), custom_call_target="tpu_custom_call" | custom-call | flops 6000000000 | bytes 60000000 | tf_op jit(solution)/shard_map/pallas_call | solution.py:425
  270.6 9.0 %fusion.24 = bf16[3,8,24,128]{3,1,2,0:T(8,128)(2,1)S(1)} fusion(bf16[2,3072,3072]{2,1,0:T(8,128)(2,1)} %param.18, bf16[32,3072]{1,0:T(8,128)(2,1)} %shard_map.155), kind=kOutput, calls=%fused_computation.22 | convolution fusion | flops 453058560 | bytes 19169280 | tf_op jit(solution)/shard_map/dot_general | solution.py:748
  279.9 4.3 %fusion.42 = bf16[3,8,8,128]{3,1,2,0:T(8,128)(2,1)S(1)} fusion(bf16[2,3072,1024]{2,1,0:T(8,128)(2,1)} %param.20, bf16[32,3072]{1,0:T(8,128)(2,1)S(1)} %copy-done.8), kind=kOutput, calls=%fused_computation.28 | convolution fusion | flops 151019520 | bytes 6488064 | tf_op jit(solution)/shard_map/dot_general | solution.py:748
  284.3 3.7 fusion.45
  288.8 15.1 %gather_rows.3 = bf16[4,12,80,128]{3,2,1,0:T(8,128)(2,1)} custom-call(bf16[12,80,128]{2,1,0:T(8,128)(2,1)} %pad_maximum_fusion.1.x_ref), custom_call_target="tpu_custom_call" | custom-call | tf_op jit(solution)/shard_map/gather_rows/pallas_call | solution.py:266
  304.7 12.8 %shard_map.156 = (bf16[120,256,128]{2,1,0:T(8,128)(2,1)}, bf16[120,256,128]{2,1,0:T(8,128)(2,1)}, f32[49,48,128]{2,1,0:T(8,128)}, f32[2,48,128]{2,1,0:T(8,128)}) custom-call(s32[4,64]{1,0:T(4,128)} %pad_add_fusion.info_ref, s32[2]{0:T(128)} %fusion.65.cnt_ref, bf16[48,80,128]{2,1,0:T(8,128)(2,1)} %bitcast.135, ...), custom_call_target="tpu_custom_call", output_to_operand_aliasing={{0}: (16, {}), {1}: (17, {})} | custom-call | flops 400000000 | bytes 16000000 | tf_op jit(solution)/shard_map/pallas_call | solution.py:606
  317.5 28.2 %combine.3 = bf16[12,48,128]{2,1,0:T(8,128)(2,1)} custom-call(f32[49,48,128]{2,1,0:T(8,128)} %get-tuple-element.113.acc_ref, f32[2,48,128]{2,1,0:T(8,128)} %get-tuple-element.114.ml_ref), custom_call_target="tpu_custom_call" | custom-call | tf_op jit(solution)/shard_map/combine/pallas_call | solution.py:312
  347.4 22.5 %shard_map.157 = bf16[32,3072]{1,0:T(8,128)(2,1)} custom-call(bf16[32,3072]{1,0:T(8,128)(2,1)} %pad.20.attn_ref, bf16[32,3072]{1,0:T(8,128)(2,1)} %broadcast_select_fusion.hid_ref, bf16[2,3072,3072]{2,1,0:T(8,128)(2,1)} %wo_ref.3, bf16[2,3072,8192]{2,1,0:T(8,128)(2,1)} %wu_ref.3, bf16[2,8192,3072]{2,1,0:T(8,128)(2,1)} %wd_ref.3), custom_call_target="tpu_custom_call" | custom-call | flops 6000000000 | bytes 60000000 | tf_op jit(solution)/shard_map/pallas_call | solution.py:425
  (150 shorter events, 45.4 us)
Async XLA Ops:
  8.3 4.3 %copy-start.18 = (s32[12]{0:T(128)S(1)}, s32[12]{0:T(128)}, u32[]{:S(2)}) copy-start(s32[12]{0:T(128)} %param.28) | copy-start | bytes 148
  8.3 4.3 %copy-start.20 = (s32[12]{0:T(128)S(1)}, s32[12]{0:T(128)}, u32[]{:S(2)}) copy-start(s32[12]{0:T(128)} %param.27) | copy-start | bytes 148
  8.4 14.9 %copy-start.11 = (bf16[2,12,3072]{2,0,1:T(2,128)(2,1)S(1)}, bf16[2,12,3072]{2,0,1:T(2,128)(2,1)}, u32[]{:S(2)}) copy-start(bf16[2,12,3072]{2,0,1:T(2,128)(2,1)} %param.17) | copy-start | bytes 442372
  11.6 158.2 %copy-start.3 = (bf16[12,512,128]{2,1,0:T(8,128)(2,1)}, bf16[12,512,128]{2,1,0:T(8,128)(2,1)S(1)}, u32[]{:S(2)}) copy-start(bf16[12,512,128]{2,1,0:T(8,128)(2,1)S(1)} %get-tuple-element.70.rest_0_) | copy-start | bytes 4718596
  11.6 227.3 %copy-start = (bf16[12,512,128]{2,1,0:T(8,128)(2,1)}, bf16[12,512,128]{2,1,0:T(8,128)(2,1)S(1)}, u32[]{:S(2)}) copy-start(bf16[12,512,128]{2,1,0:T(8,128)(2,1)S(1)} %get-tuple-element.79.rest_0_.rest_2_) | copy-start | bytes 4718596
  11.6 14.6 %collective-permute-start.1 = (bf16[12,512,128]{2,1,0:T(8,128)(2,1)S(1)}, bf16[12,512,128]{2,1,0:T(8,128)(2,1)}, u32[]{:S(2)}, u32[]{:S(2)}) collective-permute-start(bf16[12,512,128]{2,1,0:T(8,128)(2,1)S(1)} %get-tuple-element.70.rest_0_), channel_id=1, source_target_pairs={{0,1},{1,0},{2,3},{3,2},{4,5},{5,4},{6,7},{7,6},{8,9},{9,8},{10,11... | collective-permute-start | bytes 4718600 | tf_op jit(solution)/shard_map/ppermute | solution.py:657
  12.4 11.6 %copy-start.13 = (s32[12]{0:T(128)}, s32[12]{0:T(128)S(1)}, u32[]{:S(2)}) copy-start(s32[12]{0:T(128)S(1)} %and_select_fusion.5.own_ref) | copy-start | bytes 148
  12.4 11.6 %collective-permute-start = (s32[12]{0:T(128)S(1)}, s32[12]{0:T(128)S(1)}, u32[]{:S(2)}, u32[]{:S(2)}) collective-permute-start(s32[12]{0:T(128)S(1)} %and_select_fusion.5.own_ref), channel_id=1, source_target_pairs={{0,1},{1,0},{2,3},{3,2},{4,5},{5,4},{6,7},{7,6},{8,9},{9,8},{10,11... | collective-permute-start | bytes 152 | tf_op jit(solution)/shard_map/ppermute | solution.py:658
  23.4 25.1 %copy-start.21 = (s32[60]{0:T(128)}, s32[60]{0:T(128)S(1)}, u32[]{:S(2)}) copy-start(s32[60]{0:T(128)S(1)} %iota_add_fusion.2) | copy-start | bytes 724
  38.7 8.4 %copy-start.10 = (s32[32,1,128]{2,1,0:T(1,128)S(1)}, s32[32,1,128]{2,1,0:T(1,128)}, u32[]{:S(2)}) copy-start(s32[32,1,128]{2,1,0:T(1,128)} %share_plan.1) | copy-start | bytes 49156
  50.2 54.4 %collective-permute-start.2 = (bf16[12,512,128]{2,1,0:T(8,128)(2,1)S(1)}, bf16[12,512,128]{2,1,0:T(8,128)(2,1)}, u32[]{:S(2)}, u32[]{:S(2)}) collective-permute-start(bf16[12,512,128]{2,1,0:T(8,128)(2,1)S(1)} %get-tuple-element.79.rest_0_.rest_2_), channel_id=1, source_target_pairs={{0,1},{1,0},{2,3},{3,2},{4,5},{5,4},{6,7},{7,6},{8,9},{9,8},{10,11... | collective-permute-start | bytes 4718600 | tf_op jit(solution)/shard_map/ppermute | solution.py:673
  56.1 53.6 %collective-permute-start.3 = (bf16[6,512,128]{2,1,0:T(8,128)(2,1)}, bf16[6,512,128]{2,1,0:T(8,128)(2,1)}, u32[]{:S(2)}, u32[]{:S(2)}) collective-permute-start(bf16[6,512,128]{2,1,0:T(8,128)(2,1)} %get-tuple-element.80), channel_id=1, source_target_pairs={{0,4},{4,8},{8,12},{12,0},{1,5},{5,9},{9,13},{13,1},{2,6},{6,10},{... | collective-permute-start | bytes 2359304 | tf_op jit(solution)/shard_map/ppermute | solution.py:699
  57.5 67.8 %collective-permute-start.4 = (bf16[6,512,128]{2,1,0:T(8,128)(2,1)}, bf16[6,512,128]{2,1,0:T(8,128)(2,1)}, u32[]{:S(2)}, u32[]{:S(2)}) collective-permute-start(bf16[6,512,128]{2,1,0:T(8,128)(2,1)} %get-tuple-element.81), channel_id=1, source_target_pairs={{0,8},{4,12},{8,0},{12,4},{1,9},{5,13},{9,1},{13,5},{2,10},{6,14},... | collective-permute-start | bytes 2359304 | tf_op jit(solution)/shard_map/ppermute | solution.py:699
  58.7 68.9 %collective-permute-start.5 = (bf16[6,512,128]{2,1,0:T(8,128)(2,1)}, bf16[6,512,128]{2,1,0:T(8,128)(2,1)}, u32[]{:S(2)}, u32[]{:S(2)}) collective-permute-start(bf16[6,512,128]{2,1,0:T(8,128)(2,1)} %get-tuple-element.82), channel_id=1, source_target_pairs={{0,12},{4,0},{8,4},{12,8},{1,13},{5,1},{9,5},{13,9},{2,14},{6,2},{... | collective-permute-start | bytes 2359304 | tf_op jit(solution)/shard_map/ppermute | solution.py:699
  127.6 2.7 collective-permute-start.10
  128.1 3.4 collective-permute-start.11
  128.1 4.5 %collective-permute-start.9 = (bf16[6,512,128]{2,1,0:T(8,128)(2,1)}, bf16[6,512,128]{2,1,0:T(8,128)(2,1)}, u32[]{:S(2)}, u32[]{:S(2)}) collective-permute-start(bf16[6,512,128]{2,1,0:T(8,128)(2,1)} %collective-permute-done.3.rest_2_), channel_id=1, source_target_pairs={{0,1},{1,0},{2,3},{3,2},{4,5},{5,4},{6,7},{7,6},{8,9},{9,8},{10,11... | collective-permute-start | bytes 2359304 | tf_op jit(solution)/shard_map/ppermute | solution.py:703
  135.7 30.3 %collective-permute-start.12 = (bf16[10,512,128]{2,1,0:T(8,128)(2,1)}, bf16[10,512,128]{2,1,0:T(8,128)(2,1)}, u32[]{:S(2)}, u32[]{:S(2)}) collective-permute-start(bf16[10,512,128]{2,1,0:T(8,128)(2,1)} %shard_map.151), channel_id=1, source_target_pairs={{0,2},{1,3},{2,0},{3,1},{4,6},{5,7},{6,4},{7,5},{8,10},{9,11},{10,... | collective-permute-start | bytes 3932168 | tf_op jit(solution)/shard_map/ppermute | solution.py:706
  166.0 8.7 %collective-permute-start.13 = (bf16[10,512,128]{2,1,0:T(8,128)(2,1)}, bf16[10,512,128]{2,1,0:T(8,128)(2,1)}, u32[]{:S(2)}, u32[]{:S(2)}) collective-permute-start(bf16[10,512,128]{2,1,0:T(8,128)(2,1)} %collective-permute-done.12.rest_0_), channel_id=1, source_target_pairs={{0,1},{1,0},{2,3},{3,2},{4,5},{5,4},{6,7},{7,6},{8,9},{9,8},{10,11... | collective-permute-start | bytes 3932168 | tf_op jit(solution)/shard_map/ppermute | solution.py:707
  167.3 44.5 %collective-permute-start.6 = (bf16[6,512,128]{2,1,0:T(8,128)(2,1)}, bf16[6,512,128]{2,1,0:T(8,128)(2,1)}, u32[]{:S(2)}, u32[]{:S(2)}) collective-permute-start(bf16[6,512,128]{2,1,0:T(8,128)(2,1)} %get-tuple-element.89), channel_id=1, source_target_pairs={{0,4},{4,8},{8,12},{12,0},{1,5},{5,9},{9,13},{13,1},{2,6},{6,10},{... | collective-permute-start | bytes 2359304 | tf_op jit(solution)/shard_map/ppermute | solution.py:699
  167.3 68.0 %collective-permute-start.7 = (bf16[6,512,128]{2,1,0:T(8,128)(2,1)}, bf16[6,512,128]{2,1,0:T(8,128)(2,1)}, u32[]{:S(2)}, u32[]{:S(2)}) collective-permute-start(bf16[6,512,128]{2,1,0:T(8,128)(2,1)} %get-tuple-element.90), channel_id=1, source_target_pairs={{0,8},{4,12},{8,0},{12,4},{1,9},{5,13},{9,1},{13,5},{2,10},{6,14},... | collective-permute-start | bytes 2359304 | tf_op jit(solution)/shard_map/ppermute | solution.py:699
  168.3 68.9 %collective-permute-start.8 = (bf16[6,512,128]{2,1,0:T(8,128)(2,1)}, bf16[6,512,128]{2,1,0:T(8,128)(2,1)}, u32[]{:S(2)}, u32[]{:S(2)}) collective-permute-start(bf16[6,512,128]{2,1,0:T(8,128)(2,1)} %get-tuple-element.91), channel_id=1, source_target_pairs={{0,12},{4,0},{8,4},{12,8},{1,13},{5,1},{9,5},{13,9},{2,14},{6,2},{... | collective-permute-start | bytes 2359304 | tf_op jit(solution)/shard_map/ppermute | solution.py:699
  237.3 3.1 collective-permute-start.14
  237.7 3.2 collective-permute-start.15
  237.8 4.5 %collective-permute-start.16 = (bf16[6,512,128]{2,1,0:T(8,128)(2,1)}, bf16[6,512,128]{2,1,0:T(8,128)(2,1)}, u32[]{:S(2)}, u32[]{:S(2)}) collective-permute-start(bf16[6,512,128]{2,1,0:T(8,128)(2,1)} %collective-permute-done.8.rest_4_.rest_6_), channel_id=1, source_target_pairs={{0,1},{1,0},{2,3},{3,2},{4,5},{5,4},{6,7},{7,6},{8,9},{9,8},{10,11... | collective-permute-start | bytes 2359304 | tf_op jit(solution)/shard_map/ppermute | solution.py:703
  238.9 6.5 %copy-start.9 = (bf16[12,48,128]{2,1,0:T(8,128)(2,1)S(1)}, bf16[12,48,128]{2,1,0:T(8,128)(2,1)}, u32[]{:S(2)}) copy-start(bf16[12,48,128]{2,1,0:T(8,128)(2,1)} %combine.2) | copy-start | bytes 442372
  246.3 33.4 %collective-permute-start.17 = (bf16[10,512,128]{2,1,0:T(8,128)(2,1)}, bf16[10,512,128]{2,1,0:T(8,128)(2,1)S(1)}, u32[]{:S(2)}, u32[]{:S(2)}) collective-permute-start(bf16[10,512,128]{2,1,0:T(8,128)(2,1)} %shard_map.154), channel_id=1, source_target_pairs={{0,2},{1,3},{2,0},{3,1},{4,6},{5,7},{6,4},{7,5},{8,10},{9,11},{10,... | collective-permute-start | bytes 3932168 | tf_op jit(solution)/shard_map/ppermute | solution.py:706
  270.6 9.3 %copy-start.8 = (bf16[32,3072]{1,0:T(8,128)(2,1)S(1)}, bf16[32,3072]{1,0:T(8,128)(2,1)}, u32[]{:S(2)}) copy-start(bf16[32,3072]{1,0:T(8,128)(2,1)} %shard_map.155) | copy-start | bytes 589828
  279.7 24.2 %copy-start.15 = (pred[32]{0:T(512)(128)(4,1)S(1)}, pred[32]{0:T(512)(128)(4,1)}, u32[]{:S(2)}) copy-start(pred[32]{0:T(512)(128)(4,1)} %constant.149.clone.1) | copy-start | bytes 100
  279.7 25.0 %copy-start.1 = (bf16[12,512,128]{2,1,0:T(8,128)(2,1)S(1)}, bf16[12,512,128]{2,1,0:T(8,128)(2,1)}, u32[]{:S(2)}) copy-start(bf16[12,512,128]{2,1,0:T(8,128)(2,1)} %copy-done) | copy-start | bytes 4718596
  279.7 24.2 %copy-start.7 = (bf16[10,512,128]{2,1,0:T(8,128)(2,1)}, bf16[10,512,128]{2,1,0:T(8,128)(2,1)S(1)}, u32[]{:S(2)}) copy-start(bf16[10,512,128]{2,1,0:T(8,128)(2,1)S(1)} %collective-permute-done.17.rest_10_) | copy-start | bytes 3932164
  279.7 25.0 %collective-permute-start.18 = (bf16[10,512,128]{2,1,0:T(8,128)(2,1)S(1)}, bf16[10,512,128]{2,1,0:T(8,128)(2,1)}, u32[]{:S(2)}, u32[]{:S(2)}) collective-permute-start(bf16[10,512,128]{2,1,0:T(8,128)(2,1)S(1)} %collective-permute-done.17.rest_10_), channel_id=1, source_target_pairs={{0,1},{1,0},{2,3},{3,2},{4,5},{5,4},{6,7},{7,6},{8,9},{9,8},{10,11... | collective-permute-start | bytes 3932168 | tf_op jit(solution)/shard_map/ppermute | solution.py:707
  (8 other events, 15.0 us)

commit v4 on v3

--- a/solution.py
+++ b/solution.py
@@ -1,5 +1,3 @@
-import functools
-
 import jax
 import jax.numpy as jnp
 from jax import lax
@@ -241,35 +239,48 @@
     )(dst, dev, pos)
 
 
-def enter(axis, n, me):
+def around(me):
+    sib = me + 1 - 2 * lax.rem(me, 2)
+    over = lax.rem(me + 2, 4)
+    return sib, over, lax.rem(sib + 2, 4)
+
+
+def enter(axis, peers):
     barrier = pltpu.get_barrier_semaphore()
-    for d in range(1, n):
-        pl.semaphore_signal(barrier, inc=1, device_id={axis: lax.rem(me + d, n)}, device_id_type=MESH_ID)
-    pl.semaphore_wait(barrier, n - 1)
+    for p in peers:
+        pl.semaphore_signal(barrier, inc=1, device_id={axis: p}, device_id_type=MESH_ID)
+    pl.semaphore_wait(barrier, len(peers))
 
 
 def gather_rows(x, axis, n, cid):
     def body(x_ref, o_ref, send_sem, recv_sem):
         me = lax.axis_index(axis)
-        enter(axis, n, me)
-        copies = []
-        for d in range(1, n):
-            cp = pltpu.make_async_remote_copy(
-                src_ref=x_ref, dst_ref=o_ref.at[me], send_sem=send_sem.at[d], recv_sem=recv_sem.at[d],
-                device_id={axis: lax.rem(me + d, n)}, device_id_type=MESH_ID)
-            cp.start()
-            copies.append(cp)
+        sib, over, _ = around(me)
+        enter(axis, (sib, over))
+
+        def send(src, at, peer, i):
+            return pltpu.make_async_remote_copy(
+                src_ref=src, dst_ref=o_ref.at[at], send_sem=send_sem.at[i], recv_sem=recv_sem.at[i],
+                device_id={axis: peer}, device_id_type=MESH_ID)
+
+        cross, near = send(x_ref, me, over, 0), send(x_ref, me, sib, 1)
+        cross.start()
+        near.start()
         o_ref[me] = x_ref[...]
-        for cp in copies:
-            cp.wait()
+        cross.wait()
+        hand = send(o_ref.at[over], over, sib, 2)
+        hand.start()
+        near.wait()
+        hand.wait()
 
     return pl.pallas_call(
         body,
         out_shape=jax.ShapeDtypeStruct((n,) + x.shape, x.dtype),
         in_specs=[pl.BlockSpec(memory_space=pltpu.VMEM)],
         out_specs=pl.BlockSpec(memory_space=pltpu.VMEM),
-        scratch_shapes=[pltpu.SemaphoreType.DMA((n,)), pltpu.SemaphoreType.DMA((n,))],
+        scratch_shapes=[pltpu.SemaphoreType.DMA((3,)), pltpu.SemaphoreType.DMA((3,))],
         compiler_params=pltpu.CompilerParams(collective_id=cid, has_side_effects=True),
+        cost_estimate=pl.CostEstimate(flops=1_000_000_000, bytes_accessed=2_000_000, transcendentals=0),
         name="gather_rows",
     )(x)
 
@@ -278,49 +289,63 @@
     rows, r, hd = acc.shape
     b = rows // n
 
-    def body(acc_ref, ml_ref, o_ref, acc_in, ml_in, send_sem, recv_sem, send_ml, recv_ml):
+    def body(acc_ref, ml_ref, o_ref, sib_me, sib_over, ml_sib, to_over, ml_to, y_acc, ml_y, send_sem, recv_sem):
         me = lax.axis_index(axis)
-        enter(axis, n, me)
-        copies = []
-        for d in range(1, n):
-            peer = lax.rem(me + d, n)
-            for src, dst, ss, rs in (
-                (acc_ref.at[pl.ds(peer * b, b)], acc_in.at[d], send_sem, recv_sem),
-                (ml_ref, ml_in.at[d], send_ml, recv_ml),
-            ):
-                cp = pltpu.make_async_remote_copy(
-                    src_ref=src, dst_ref=dst, send_sem=ss.at[d], recv_sem=rs.at[d],
-                    device_id={axis: peer}, device_id_type=MESH_ID)
-                cp.start()
-                copies.append(cp)
-        for cp in copies:
-            cp.wait()
+        sib, over, diag = around(me)
+        enter(axis, (sib, over))
+
+        def send(src, dst, peer, i):
+            return pltpu.make_async_remote_copy(
+                src_ref=src, dst_ref=dst, send_sem=send_sem.at[i], recv_sem=recv_sem.at[i],
+                device_id={axis: peer}, device_id_type=MESH_ID)
+
+        near = [send(acc_ref.at[pl.ds(diag * b, b)], sib_over, sib, 0), send(ml_ref, ml_sib, sib, 1),
+                send(acc_ref.at[pl.ds(sib * b, b)], sib_me, sib, 2)]
+        for cp in near:
+            cp.start()
+        near[0].wait()
+        near[1].wait()
         lane = lax.broadcasted_iota(jnp.int32, (r, ml_ref.shape[2]), 1)
+
+        def pick(t, s):
+            return jnp.sum(jnp.where(lane == s, t, 0.0), axis=1, keepdims=True)
+
+        top = jnp.maximum(ml_ref[0], ml_sib[0])
+        w_own, w_sib = jnp.exp(ml_ref[0] - top), jnp.exp(ml_sib[0] - top)
+        tot = w_own * ml_ref[1] + w_sib * ml_sib[1]
+        ml_to[0] = top
+        ml_to[1] = tot
         for i in range(b):
-            sel = lane == me * b + i
-            pick = lambda t: jnp.sum(jnp.where(sel, t, 0.0), axis=1, keepdims=True)
-            ms = [pick(ml_ref[0])] + [pick(ml_in[d, 0]) for d in range(1, n)]
-            ls = [pick(ml_ref[1])] + [pick(ml_in[d, 1]) for d in range(1, n)]
-            top = functools.reduce(jnp.maximum, ms)
-            ws = [jnp.exp(m - top) for m in ms]
-            den = sum(w * l for w, l in zip(ws, ls))
-            num = ws[0] * acc_ref[me * b + i]
-            for d in range(1, n):
-                num += ws[d] * acc_in[d, i]
-            o_ref[i] = (num / den).astype(o_ref.dtype)
-
+            s = over * b + i
+            to_over[i] = pick(w_own, s) * acc_ref[s] + pick(w_sib, s) * sib_over[i]
+        far = [send(to_over, y_acc, over, 3), send(ml_to, ml_y, over, 4)]
+        for cp in far:
+            cp.start()
+        near[2].wait()
+        far[1].wait()
+        last = jnp.maximum(top, ml_y[0])
+        f, g = jnp.exp(top - last), jnp.exp(ml_y[0] - last)
+        den = f * tot + g * ml_y[1]
+        f, g = f / den, g / den
+        w_own, w_sib = f * w_own, f * w_sib
+        for i in range(b):
+            s = me * b + i
+            sib_me[i] = pick(w_own, s) * acc_ref[s] + pick(w_sib, s) * sib_me[i]
+        far[0].wait()
+        for i in range(b):
+            o_ref[i] = (sib_me[i] + pick(g, me * b + i) * y_acc[i]).astype(o_ref.dtype)
+
+    block = pltpu.VMEM((b, r, hd), jnp.float32)
+    stats = pltpu.VMEM(ml.shape, jnp.float32)
     return pl.pallas_call(
         body,
         out_shape=jax.ShapeDtypeStruct((b, r, hd), jnp.bfloat16),
         in_specs=[pl.BlockSpec(memory_space=pltpu.VMEM)] * 2,
         out_specs=pl.BlockSpec(memory_space=pltpu.VMEM),
-        scratch_shapes=[
-            pltpu.VMEM((n, b, r, hd), jnp.float32),
-            pltpu.VMEM((n,) + ml.shape, jnp.float32),
-            pltpu.SemaphoreType.DMA((n,)), pltpu.SemaphoreType.DMA((n,)),
-            pltpu.SemaphoreType.DMA((n,)), pltpu.SemaphoreType.DMA((n,)),
-        ],
+        scratch_shapes=[block, block, stats, block, stats, block, stats,
+                        pltpu.SemaphoreType.DMA((5,)), pltpu.SemaphoreType.DMA((5,))],
         compiler_params=pltpu.CompilerParams(collective_id=cid, has_side_effects=True),
+        cost_estimate=pl.CostEstimate(flops=1_000_000_000, bytes_accessed=2_000_000, transcendentals=0),
         name="combine",
     )(acc, ml)
 
@@ -536,19 +561,18 @@
                     for cp in loads(j):
                         cp.wait()
 
-                    @pl.when(info_ref[2, j] < page)
-                    def _():
-                        off = info_ref[2, j]
-                        w = jnp.minimum(off // 2, page // 2 - 2)
-                        at = pl.ds(pl.multiple_of(w * (2 * kvh), 2 * kvh), 4 * kvh)
-                        for buf, r0 in ((kbuf, qr), (vbuf, qr + 2 * kvh)):
-                            new = qkv_ref[info_ref[1, j], r0:r0 + 2 * kvh, :].astype(jnp.float32)
-                            first = jnp.concatenate([new[:kvh]] * 4, axis=0)
-                            second = jnp.concatenate([new[kvh:]] * 4, axis=0)
-                            old = buf[j, at, :].astype(jnp.float32)
-                            tok = wrow + 2 * w
-                            old = jnp.where(tok == off, first, jnp.where(tok == off + 1, second, old))
-                            buf[j, at, :] = old.astype(jnp.bfloat16)
+            for j, seq, off in zip(idx, seqs, offs):
+                w = jnp.minimum(off // 2, page // 2 - 2)
+                at = pl.ds(pl.multiple_of(w * (2 * kvh), 2 * kvh), 4 * kvh)
+                tok = wrow + 2 * w
+                seq = jnp.minimum(info_ref[1, j], n_seq - 1)
+                for buf, r0 in ((kbuf, qr), (vbuf, qr + 2 * kvh)):
+                    new = qkv_ref[seq, r0:r0 + 2 * kvh, :].astype(jnp.float32)
+                    first = jnp.concatenate([new[:kvh]] * 4, axis=0)
+                    second = jnp.concatenate([new[kvh:]] * 4, axis=0)
+                    old = buf[j, at, :].astype(jnp.float32)
+                    old = jnp.where(tok == off, first, jnp.where(tok == off + 1, second, old))
+                    buf[j, at, :] = old.astype(jnp.bfloat16)
 
             res = []
             for u in range(UNROLL):

time: 380 us -> 377 us (level)
  Pallas kernels: 208 us -> 189 us
  waiting for transfers between devices: 78 us -> 95.7 us
    ppermute x6, waiting for transfers between devices: 43.4 us -> 61 us  [along_z(): got.append(lax.ppermute(h, 'kv2', z))]
    pallas_call x2, Pallas kernels: 60.2 us -> 49.3 us  [combine(): pl.pallas_call(body, out_shape=jax.ShapeDtypeStruct((b, r, hd), jnp.bfloa...]
    pallas_call x2, Pallas kernels: 31.2 us -> 23.2 us  [gather_rows(): pl.pallas_call(body, out_shape=jax.ShapeDtypeStruct((n,) + x.shape, x.dty...]
  transfers between devices with their start and end apart: 19 -> 19, of which waited for: 10 -> 10; matrix products, arithmetic and copies ran while one was open for 10% -> 9% of each run, Pallas kernels for 34% -> 29%
where the time goes in v4:
time: 377 us; the launch traced here: 376 us
  Pallas kernels  189 us (50%)
  waiting for transfers between devices  95.7 us (25%)
  matrix products  32 us (8%)
  other arithmetic  16.7 us (4%)
  between operations  15.9 us (4%)
  starting transfers between devices  14.3 us (4%)
  local copies, waits for them, and re-layouts  12 us (3%)
    ppermute x6, waiting for transfers between devices, along_z(): got.append(lax.ppermute(h, 'kv2', z))  61 us
    pallas_call x2, Pallas kernels, combine(): pl.pallas_call(body, out_shape=jax.ShapeDtypeStruct((b, r, hd), jnp.bfloa...  49.3 us
    pallas_call x2, Pallas kernels, mlp_pair(): pl.pallas_call(body, out_shape=jax.ShapeDtypeStruct((r, d), jnp.bfloat16)...  46 us
    pallas_call x4, Pallas kernels, attend(): pl.pallas_call(body, out_shape=[pool, pool, jax.ShapeDtypeStruct((n_seq +...  33.4 us
    dot_general x6, matrix products, per_device(): dot = lambda a, w: jnp.dot(a, w[layer], preferred_element_type=jnp.float32)  32 us
    ppermute x2, waiting for transfers between devices, along_y(): got = lax.ppermute(hop, 'kv', over)  28.7 us
    pallas_call x2, Pallas kernels, gather_rows(): pl.pallas_call(body, out_shape=jax.ShapeDtypeStruct((n,) + x.shape, x.dty...  23.2 us
    pallas_call x4, Pallas kernels, pick(): pl.pallas_call(body, out_shape=[jax.ShapeDtypeStruct((size,) + tail, dtyp...  16.4 us
  transfers between devices with their start and end apart: 19, of which 10 were waited for; matrix products, arithmetic and copies ran while one was open for 9% of the time, Pallas kernels for 29%

profile of v4, /device:TPU:9, one launch (start us, length us, event | category | flops | bytes accessed | tf_op | source)
XLA Modules:
  0.0 375.9 jit_solution(17406240148574348619)
XLA Ops:
  8.4 3.2 take_pages.1
  13.3 9.3 %share_plan.1 = s32[32,1,128]{2,1,0:T(1,128)} custom-call(s32[1,128]{1,0:T(1,128)} %pad_bitcast_fusion.x_ref), custom_call_target="tpu_custom_call" | custom-call | tf_op jit(solution)/shard_map/share_plan/pallas_call | solution.py:129
  25.4 1.7 route_z.1.idx_ref
  27.1 5.0 %shard_map.148 = (bf16[6,512,128]{2,1,0:T(8,128)(2,1)}, bf16[6,512,128]{2,1,0:T(8,128)(2,1)}, bf16[6,512,128]{2,1,0:T(8,128)(2,1)}) custom-call(s32[64]{0:T(128)} %route_z.1.idx_ref, bf16[12,512,128]{2,1,0:T(8,128)(2,1)S(1)} %get-tuple-element.70.rest_0_, bf16[12,512,128]{2,1,0:T(8,128)(2,1)} %collective-permute-done.1.rest_1_), custom_call_target="tpu_custom_call" | custom-call | flops 100000000 | bytes 5000000 | tf_op jit(solution)/shard_map/pallas_call | solution.py:93
  33.7 3.7 fusion.51
  37.4 3.7 fusion.48
  41.7 7.7 %fusion.27 = bf16[3,8,24,128]{3,1,2,0:T(8,128)(2,1)S(1)} fusion(bf16[24,3072]{1,0:T(8,128)(2,1)S(1)} %reshape.243, bf16[2,3072,3072]{2,1,0:T(8,128)(2,1)} %param.18), kind=kOutput, calls=%fused_computation.23 | convolution fusion | flops 453058560 | bytes 19169280 | tf_op jit(solution)/shard_map/dot_general | solution.py:772
  54.1 6.9 %route.1 = (s32[64]{0:T(128)}, s32[64]{0:T(128)}) custom-call(s32[192]{0:T(256)} %copy-done.12, s32[192]{0:T(256)} %reshape.246.dev_ref, s32[2]{0:T(128)} %pad_add_fusion.2.pos_ref), custom_call_target="tpu_custom_call" | custom-call | flops 100000000 | bytes 1000000 | tf_op jit(solution)/shard_map/route/pallas_call | solution.py:231
  73.2 11.8 %gather_rows.2 = bf16[4,12,80,128]{3,2,1,0:T(8,128)(2,1)} custom-call(bf16[12,80,128]{2,1,0:T(8,128)(2,1)} %pad_maximum_fusion.x_ref), custom_call_target="tpu_custom_call" | custom-call | flops 1000000000 | bytes 2000000 | tf_op jit(solution)/shard_map/gather_rows/pallas_call | solution.py:276
  88.1 10.6 %shard_map.149 = (bf16[120,256,128]{2,1,0:T(8,128)(2,1)}, bf16[120,256,128]{2,1,0:T(8,128)(2,1)}, f32[49,48,128]{2,1,0:T(8,128)}, f32[2,48,128]{2,1,0:T(8,128)}) custom-call(s32[4,64]{1,0:T(4,128)} %pad_add_fusion.1.info_ref, s32[6]{0:T(128)} %convert_reduce_fusion.4.cnt_ref, bf16[48,80,128]{2,1,0:T(8,128)(2,1)} %bitcast.132, ...), custom_call_target="tpu_custom_call" | custom-call | flops 400000000 | bytes 16000000 | tf_op jit(solution)/shard_map/pallas_call | solution.py:630
  98.7 5.0 %shard_map.150 = (bf16[6,512,128]{2,1,0:T(8,128)(2,1)}, bf16[6,512,128]{2,1,0:T(8,128)(2,1)}, bf16[6,512,128]{2,1,0:T(8,128)(2,1)}) custom-call(s32[64]{0:T(128)} %route_z.1.idx_ref, bf16[12,512,128]{2,1,0:T(8,128)(2,1)S(1)} %get-tuple-element.79.rest_0_.rest_2_, bf16[12,512,128]{2,1,0:T(8,128)(2,1)} %collective-permute-done.2.rest_1_.rest_3_), custom_call_target="tpu_custom_call" | custom-call | flops 100000000 | bytes 5000000 | tf_op jit(solution)/shard_map/pallas_call | solution.py:93
  103.8 27.0 %collective-permute-done.4.rest_3_ = bf16[6,512,128]{2,1,0:T(8,128)(2,1)} collective-permute-done((bf16[6,512,128]{2,1,0:T(8,128)(2,1)}, bf16[6,512,128]{2,1,0:T(8,128)(2,1)}, u32[]{:S(2)}, u32[]{:S(2)}) %collective-permute-start.4) | collective-permute-done | bytes 786464 | tf_op jit(solution)/shard_map/ppermute | solution.py:723
  130.8 2.5 collective-permute-done.5.rest_4_
  134.2 1.7 collective-permute-done.10.rest_6_
  138.2 3.1 shard_map.151
  141.3 1.6 collective-permute-start.12
  142.9 28.7 %collective-permute-done.12.rest_0_ = bf16[10,512,128]{2,1,0:T(8,128)(2,1)} collective-permute-done((bf16[10,512,128]{2,1,0:T(8,128)(2,1)}, bf16[10,512,128]{2,1,0:T(8,128)(2,1)}, u32[]{:S(2)}, u32[]{:S(2)}) %collective-permute-start.12) | collective-permute-done | bytes 1310752 | tf_op jit(solution)/shard_map/ppermute | solution.py:730
  174.0 1.5 collective-permute-start.8
  175.4 4.9 %shard_map.152 = (bf16[120,256,128]{2,1,0:T(8,128)(2,1)}, bf16[120,256,128]{2,1,0:T(8,128)(2,1)}, f32[49,48,128]{2,1,0:T(8,128)}, f32[2,48,128]{2,1,0:T(8,128)}) custom-call(s32[4,64]{1,0:T(4,128)} %pad_add_fusion.1.info_ref, s32[6]{0:T(128)} %convert_reduce_fusion.4.cnt_ref, ...), custom_call_target="tpu_custom_call", output_to_operand_aliasing={{0}: (11, {}), {1}: (12, {})} | custom-call | flops 400000000 | bytes 16000000 | tf_op jit(solution)/shard_map/pallas_call | solution.py:630
  180.3 5.0 %shard_map.153 = (bf16[120,256,128]{2,1,0:T(8,128)(2,1)}, bf16[120,256,128]{2,1,0:T(8,128)(2,1)}, f32[49,48,128]{2,1,0:T(8,128)}, f32[2,48,128]{2,1,0:T(8,128)}) custom-call(s32[4,64]{1,0:T(4,128)} %pad_add_fusion.1.info_ref, s32[6]{0:T(128)} %convert_reduce_fusion.4.cnt_ref, ...), custom_call_target="tpu_custom_call", output_to_operand_aliasing={{0}: (6, {}), {1}: (7, {})} | custom-call | flops 400000000 | bytes 16000000 | tf_op jit(solution)/shard_map/pallas_call | solution.py:630
  185.4 26.0 %combine.2 = bf16[12,48,128]{2,1,0:T(8,128)(2,1)} custom-call(f32[49,48,128]{2,1,0:T(8,128)} %get-tuple-element.103.acc_ref, f32[2,48,128]{2,1,0:T(8,128)} %get-tuple-element.104.ml_ref), custom_call_target="tpu_custom_call" | custom-call | flops 1000000000 | bytes 2000000 | tf_op jit(solution)/shard_map/combine/pallas_call | solution.py:340
  211.4 29.6 %collective-permute-done.7.rest_3_.rest_5_ = bf16[6,512,128]{2,1,0:T(8,128)(2,1)} collective-permute-done((bf16[6,512,128]{2,1,0:T(8,128)(2,1)}, bf16[6,512,128]{2,1,0:T(8,128)(2,1)}, u32[]{:S(2)}, u32[]{:S(2)}) %collective-permute-start.7) | collective-permute-done | bytes 786464 | tf_op jit(solution)/shard_map/ppermute | solution.py:723
  241.0 1.9 collective-permute-done.8.rest_4_.rest_6_
  247.9 3.2 shard_map.154
  253.3 23.0 %shard_map.155 = bf16[32,3072]{1,0:T(8,128)(2,1)} custom-call(bf16[32,3072]{1,0:T(8,128)(2,1)} %pad.18.attn_ref, bf16[32,3072]{1,0:T(8,128)(2,1)} %pad.19.hid_ref, bf16[2,3072,3072]{2,1,0:T(8,128)(2,1)} %wo_ref.3, bf16[2,3072,8192]{2,1,0:T(8,128)(2,1)} %wu_ref.3, bf16[2,8192,3072]{2,1,0:T(8,128)(2,1)} %wd_ref.3), custom_call_target="tpu_custom_call" | custom-call | flops 6000000000 | bytes 60000000 | tf_op jit(solution)/shard_map/pallas_call | solution.py:450
  276.3 9.0 %fusion.24 = bf16[3,8,24,128]{3,1,2,0:T(8,128)(2,1)S(1)} fusion(bf16[2,3072,3072]{2,1,0:T(8,128)(2,1)} %param.18, bf16[32,3072]{1,0:T(8,128)(2,1)} %shard_map.155), kind=kOutput, calls=%fused_computation.22 | convolution fusion | flops 453058560 | bytes 19169280 | tf_op jit(solution)/shard_map/dot_general | solution.py:772
  285.4 3.8 %fusion.42 = bf16[3,8,8,128]{3,1,2,0:T(8,128)(2,1)S(1)} fusion(bf16[2,3072,1024]{2,1,0:T(8,128)(2,1)} %param.20, bf16[32,3072]{1,0:T(8,128)(2,1)S(1)} %copy-done.8), kind=kOutput, calls=%fused_computation.28 | convolution fusion | flops 151019520 | bytes 6488064 | tf_op jit(solution)/shard_map/dot_general | solution.py:772
  289.5 4.0 %fusion.45 = bf16[3,8,8,128]{3,1,2,0:T(8,128)(2,1)S(1)} fusion(bf16[2,3072,1024]{2,1,0:T(8,128)(2,1)} %param.19, bf16[32,3072]{1,0:T(8,128)(2,1)S(1)} %copy-done.8), kind=kOutput, calls=%fused_computation.29 | convolution fusion | flops 151019520 | bytes 6488064 | tf_op jit(solution)/shard_map/dot_general | solution.py:772
  294.3 11.3 %gather_rows.3 = bf16[4,12,80,128]{3,2,1,0:T(8,128)(2,1)} custom-call(bf16[12,80,128]{2,1,0:T(8,128)(2,1)} %pad_maximum_fusion.1.x_ref), custom_call_target="tpu_custom_call" | custom-call | flops 1000000000 | bytes 2000000 | tf_op jit(solution)/shard_map/gather_rows/pallas_call | solution.py:276
  306.4 12.8 %shard_map.156 = (bf16[120,256,128]{2,1,0:T(8,128)(2,1)}, bf16[120,256,128]{2,1,0:T(8,128)(2,1)}, f32[49,48,128]{2,1,0:T(8,128)}, f32[2,48,128]{2,1,0:T(8,128)}) custom-call(s32[4,64]{1,0:T(4,128)} %pad_add_fusion.info_ref, s32[2]{0:T(128)} %fusion.65.cnt_ref, bf16[48,80,128]{2,1,0:T(8,128)(2,1)} %bitcast.135, ...), custom_call_target="tpu_custom_call", output_to_operand_aliasing={{0}: (16, {}), {1}: (17, {})} | custom-call | flops 400000000 | bytes 16000000 | tf_op jit(solution)/shard_map/pallas_call | solution.py:630
  319.2 23.3 %combine.3 = bf16[12,48,128]{2,1,0:T(8,128)(2,1)} custom-call(f32[49,48,128]{2,1,0:T(8,128)} %get-tuple-element.113.acc_ref, f32[2,48,128]{2,1,0:T(8,128)} %get-tuple-element.114.ml_ref), custom_call_target="tpu_custom_call" | custom-call | flops 1000000000 | bytes 2000000 | tf_op jit(solution)/shard_map/combine/pallas_call | solution.py:340
  344.3 23.0 %shard_map.157 = bf16[32,3072]{1,0:T(8,128)(2,1)} custom-call(bf16[32,3072]{1,0:T(8,128)(2,1)} %pad.20.attn_ref, bf16[32,3072]{1,0:T(8,128)(2,1)} %broadcast_select_fusion.hid_ref, bf16[2,3072,3072]{2,1,0:T(8,128)(2,1)} %wo_ref.3, bf16[2,3072,8192]{2,1,0:T(8,128)(2,1)} %wu_ref.3, bf16[2,8192,3072]{2,1,0:T(8,128)(2,1)} %wd_ref.3), custom_call_target="tpu_custom_call" | custom-call | flops 6000000000 | bytes 60000000 | tf_op jit(solution)/shard_map/pallas_call | solution.py:450
  (146 shorter events, 44.2 us)
Async XLA Ops:
  8.3 4.3 %copy-start.16 = (s32[12]{0:T(128)S(1)}, s32[12]{0:T(128)}, u32[]{:S(2)}) copy-start(s32[12]{0:T(128)} %param.28) | copy-start | bytes 148
  8.3 4.3 %copy-start.18 = (s32[12]{0:T(128)S(1)}, s32[12]{0:T(128)}, u32[]{:S(2)}) copy-start(s32[12]{0:T(128)} %param.27) | copy-start | bytes 148
  8.4 14.8 %copy-start.11 = (bf16[2,12,3072]{2,0,1:T(2,128)(2,1)S(1)}, bf16[2,12,3072]{2,0,1:T(2,128)(2,1)}, u32[]{:S(2)}) copy-start(bf16[2,12,3072]{2,0,1:T(2,128)(2,1)} %param.17) | copy-start | bytes 442372
  11.6 163.8 %copy-start.3 = (bf16[12,512,128]{2,1,0:T(8,128)(2,1)}, bf16[12,512,128]{2,1,0:T(8,128)(2,1)S(1)}, u32[]{:S(2)}) copy-start(bf16[12,512,128]{2,1,0:T(8,128)(2,1)S(1)} %get-tuple-element.70.rest_0_) | copy-start | bytes 4718596
  11.6 233.0 %copy-start = (bf16[12,512,128]{2,1,0:T(8,128)(2,1)}, bf16[12,512,128]{2,1,0:T(8,128)(2,1)S(1)}, u32[]{:S(2)}) copy-start(bf16[12,512,128]{2,1,0:T(8,128)(2,1)S(1)} %get-tuple-element.79.rest_0_.rest_2_) | copy-start | bytes 4718596
  11.6 15.5 %collective-permute-start.1 = (bf16[12,512,128]{2,1,0:T(8,128)(2,1)S(1)}, bf16[12,512,128]{2,1,0:T(8,128)(2,1)}, u32[]{:S(2)}, u32[]{:S(2)}) collective-permute-start(bf16[12,512,128]{2,1,0:T(8,128)(2,1)S(1)} %get-tuple-element.70.rest_0_), channel_id=1, source_target_pairs={{0,1},{1,0},{2,3},{3,2},{4,5},{5,4},{6,7},{7,6},{8,9},{9,8},{10,11... | collective-permute-start | bytes 4718600 | tf_op jit(solution)/shard_map/ppermute | solution.py:681
  12.4 12.5 %copy-start.13 = (s32[12]{0:T(128)}, s32[12]{0:T(128)S(1)}, u32[]{:S(2)}) copy-start(s32[12]{0:T(128)S(1)} %and_select_fusion.5.own_ref) | copy-start | bytes 148
  12.4 12.5 %collective-permute-start = (s32[12]{0:T(128)S(1)}, s32[12]{0:T(128)S(1)}, u32[]{:S(2)}, u32[]{:S(2)}) collective-permute-start(s32[12]{0:T(128)S(1)} %and_select_fusion.5.own_ref), channel_id=1, source_target_pairs={{0,1},{1,0},{2,3},{3,2},{4,5},{5,4},{6,7},{7,6},{8,9},{9,8},{10,11... | collective-permute-start | bytes 152 | tf_op jit(solution)/shard_map/ppermute | solution.py:682
  41.7 9.7 %copy-start.9 = (s32[32,1,128]{2,1,0:T(1,128)S(1)}, s32[32,1,128]{2,1,0:T(1,128)}, u32[]{:S(2)}) copy-start(s32[32,1,128]{2,1,0:T(1,128)} %share_plan.1) | copy-start | bytes 49156
  49.8 4.3 %copy-start.12 = (s32[192]{0:T(256)}, s32[192]{0:T(256)S(1)}, u32[]{:S(2)}) copy-start(s32[192]{0:T(256)S(1)} %broadcast_in_dim.144.dst_ref) | copy-start | bytes 2308
  60.9 37.8 %collective-permute-start.2 = (bf16[12,512,128]{2,1,0:T(8,128)(2,1)S(1)}, bf16[12,512,128]{2,1,0:T(8,128)(2,1)}, u32[]{:S(2)}, u32[]{:S(2)}) collective-permute-start(bf16[12,512,128]{2,1,0:T(8,128)(2,1)S(1)} %get-tuple-element.79.rest_0_.rest_2_), channel_id=1, source_target_pairs={{0,1},{1,0},{2,3},{3,2},{4,5},{5,4},{6,7},{7,6},{8,9},{9,8},{10,11... | collective-permute-start | bytes 4718600 | tf_op jit(solution)/shard_map/ppermute | solution.py:697
  61.8 42.0 %collective-permute-start.3 = (bf16[6,512,128]{2,1,0:T(8,128)(2,1)}, bf16[6,512,128]{2,1,0:T(8,128)(2,1)}, u32[]{:S(2)}, u32[]{:S(2)}) collective-permute-start(bf16[6,512,128]{2,1,0:T(8,128)(2,1)} %get-tuple-element.80), channel_id=1, source_target_pairs={{0,4},{4,8},{8,12},{12,0},{1,5},{5,9},{9,13},{13,1},{2,6},{6,10},{... | collective-permute-start | bytes 2359304 | tf_op jit(solution)/shard_map/ppermute | solution.py:723
  63.1 67.7 %collective-permute-start.4 = (bf16[6,512,128]{2,1,0:T(8,128)(2,1)}, bf16[6,512,128]{2,1,0:T(8,128)(2,1)}, u32[]{:S(2)}, u32[]{:S(2)}) collective-permute-start(bf16[6,512,128]{2,1,0:T(8,128)(2,1)} %get-tuple-element.81), channel_id=1, source_target_pairs={{0,8},{4,12},{8,0},{12,4},{1,9},{5,13},{9,1},{13,5},{2,10},{6,14},... | collective-permute-start | bytes 2359304 | tf_op jit(solution)/shard_map/ppermute | solution.py:723
  64.3 68.9 %collective-permute-start.5 = (bf16[6,512,128]{2,1,0:T(8,128)(2,1)}, bf16[6,512,128]{2,1,0:T(8,128)(2,1)}, u32[]{:S(2)}, u32[]{:S(2)}) collective-permute-start(bf16[6,512,128]{2,1,0:T(8,128)(2,1)} %get-tuple-element.82), channel_id=1, source_target_pairs={{0,12},{4,0},{8,4},{12,8},{1,13},{5,1},{9,5},{13,9},{2,14},{6,2},{... | collective-permute-start | bytes 2359304 | tf_op jit(solution)/shard_map/ppermute | solution.py:723
  133.3 2.7 collective-permute-start.10
  133.7 3.4 collective-permute-start.11
  133.8 4.5 %collective-permute-start.9 = (bf16[6,512,128]{2,1,0:T(8,128)(2,1)}, bf16[6,512,128]{2,1,0:T(8,128)(2,1)}, u32[]{:S(2)}, u32[]{:S(2)}) collective-permute-start(bf16[6,512,128]{2,1,0:T(8,128)(2,1)} %collective-permute-done.3.rest_2_), channel_id=1, source_target_pairs={{0,1},{1,0},{2,3},{3,2},{4,5},{5,4},{6,7},{7,6},{8,9},{9,8},{10,11... | collective-permute-start | bytes 2359304 | tf_op jit(solution)/shard_map/ppermute | solution.py:727
  141.3 30.3 %collective-permute-start.12 = (bf16[10,512,128]{2,1,0:T(8,128)(2,1)}, bf16[10,512,128]{2,1,0:T(8,128)(2,1)}, u32[]{:S(2)}, u32[]{:S(2)}) collective-permute-start(bf16[10,512,128]{2,1,0:T(8,128)(2,1)} %shard_map.151), channel_id=1, source_target_pairs={{0,2},{1,3},{2,0},{3,1},{4,6},{5,7},{6,4},{7,5},{8,10},{9,11},{10,... | collective-permute-start | bytes 3932168 | tf_op jit(solution)/shard_map/ppermute | solution.py:730
  171.6 8.7 %collective-permute-start.13 = (bf16[10,512,128]{2,1,0:T(8,128)(2,1)}, bf16[10,512,128]{2,1,0:T(8,128)(2,1)}, u32[]{:S(2)}, u32[]{:S(2)}) collective-permute-start(bf16[10,512,128]{2,1,0:T(8,128)(2,1)} %collective-permute-done.12.rest_0_), channel_id=1, source_target_pairs={{0,1},{1,0},{2,3},{3,2},{4,5},{5,4},{6,7},{7,6},{8,9},{9,8},{10,11... | collective-permute-start | bytes 3932168 | tf_op jit(solution)/shard_map/ppermute | solution.py:731
  173.0 38.5 %collective-permute-start.6 = (bf16[6,512,128]{2,1,0:T(8,128)(2,1)}, bf16[6,512,128]{2,1,0:T(8,128)(2,1)}, u32[]{:S(2)}, u32[]{:S(2)}) collective-permute-start(bf16[6,512,128]{2,1,0:T(8,128)(2,1)} %get-tuple-element.89), channel_id=1, source_target_pairs={{0,4},{4,8},{8,12},{12,0},{1,5},{5,9},{9,13},{13,1},{2,6},{6,10},{... | collective-permute-start | bytes 2359304 | tf_op jit(solution)/shard_map/ppermute | solution.py:723
  173.0 68.0 %collective-permute-start.7 = (bf16[6,512,128]{2,1,0:T(8,128)(2,1)}, bf16[6,512,128]{2,1,0:T(8,128)(2,1)}, u32[]{:S(2)}, u32[]{:S(2)}) collective-permute-start(bf16[6,512,128]{2,1,0:T(8,128)(2,1)} %get-tuple-element.90), channel_id=1, source_target_pairs={{0,8},{4,12},{8,0},{12,4},{1,9},{5,13},{9,1},{13,5},{2,10},{6,14},... | collective-permute-start | bytes 2359304 | tf_op jit(solution)/shard_map/ppermute | solution.py:723
  174.0 68.9 %collective-permute-start.8 = (bf16[6,512,128]{2,1,0:T(8,128)(2,1)}, bf16[6,512,128]{2,1,0:T(8,128)(2,1)}, u32[]{:S(2)}, u32[]{:S(2)}) collective-permute-start(bf16[6,512,128]{2,1,0:T(8,128)(2,1)} %get-tuple-element.91), channel_id=1, source_target_pairs={{0,12},{4,0},{8,4},{12,8},{1,13},{5,1},{9,5},{13,9},{2,14},{6,2},{... | collective-permute-start | bytes 2359304 | tf_op jit(solution)/shard_map/ppermute | solution.py:723
  242.9 3.0 collective-permute-start.14
  243.4 3.2 collective-permute-start.15
  243.4 4.5 %collective-permute-start.16 = (bf16[6,512,128]{2,1,0:T(8,128)(2,1)}, bf16[6,512,128]{2,1,0:T(8,128)(2,1)}, u32[]{:S(2)}, u32[]{:S(2)}) collective-permute-start(bf16[6,512,128]{2,1,0:T(8,128)(2,1)} %collective-permute-done.8.rest_4_.rest_6_), channel_id=1, source_target_pairs={{0,1},{1,0},{2,3},{3,2},{4,5},{5,4},{6,7},{7,6},{8,9},{9,8},{10,11... | collective-permute-start | bytes 2359304 | tf_op jit(solution)/shard_map/ppermute | solution.py:727
  244.6 6.5 %copy-start.10 = (bf16[12,48,128]{2,1,0:T(8,128)(2,1)S(1)}, bf16[12,48,128]{2,1,0:T(8,128)(2,1)}, u32[]{:S(2)}) copy-start(bf16[12,48,128]{2,1,0:T(8,128)(2,1)} %combine.2) | copy-start | bytes 442372
  251.9 37.3 %collective-permute-start.17 = (bf16[10,512,128]{2,1,0:T(8,128)(2,1)}, bf16[10,512,128]{2,1,0:T(8,128)(2,1)S(1)}, u32[]{:S(2)}, u32[]{:S(2)}) collective-permute-start(bf16[10,512,128]{2,1,0:T(8,128)(2,1)} %shard_map.154), channel_id=1, source_target_pairs={{0,2},{1,3},{2,0},{3,1},{4,6},{5,7},{6,4},{7,5},{8,10},{9,11},{10,... | collective-permute-start | bytes 3932168 | tf_op jit(solution)/shard_map/ppermute | solution.py:730
  276.3 9.1 %copy-start.8 = (bf16[32,3072]{1,0:T(8,128)(2,1)S(1)}, bf16[32,3072]{1,0:T(8,128)(2,1)}, u32[]{:S(2)}) copy-start(bf16[32,3072]{1,0:T(8,128)(2,1)} %shard_map.155) | copy-start | bytes 589828
  285.4 20.2 %copy-start.15 = (pred[32]{0:T(512)(128)(4,1)S(1)}, pred[32]{0:T(512)(128)(4,1)}, u32[]{:S(2)}) copy-start(pred[32]{0:T(512)(128)(4,1)} %constant.149.clone.1) | copy-start | bytes 100
  285.4 21.0 %copy-start.1 = (bf16[12,512,128]{2,1,0:T(8,128)(2,1)S(1)}, bf16[12,512,128]{2,1,0:T(8,128)(2,1)}, u32[]{:S(2)}) copy-start(bf16[12,512,128]{2,1,0:T(8,128)(2,1)} %copy-done) | copy-start | bytes 4718596
  289.3 17.1 %copy-start.7 = (bf16[10,512,128]{2,1,0:T(8,128)(2,1)}, bf16[10,512,128]{2,1,0:T(8,128)(2,1)S(1)}, u32[]{:S(2)}) copy-start(bf16[10,512,128]{2,1,0:T(8,128)(2,1)S(1)} %collective-permute-done.17.rest_10_) | copy-start | bytes 3932164
  289.3 17.1 %collective-permute-start.18 = (bf16[10,512,128]{2,1,0:T(8,128)(2,1)S(1)}, bf16[10,512,128]{2,1,0:T(8,128)(2,1)}, u32[]{:S(2)}, u32[]{:S(2)}) collective-permute-start(bf16[10,512,128]{2,1,0:T(8,128)(2,1)S(1)} %collective-permute-done.17.rest_10_), channel_id=1, source_target_pairs={{0,1},{1,0},{2,3},{3,2},{4,5},{5,4},{6,7},{7,6},{8,9},{9,8},{10,11... | collective-permute-start | bytes 3932168 | tf_op jit(solution)/shard_map/ppermute | solution.py:731
  (6 other events, 12.4 us)

commit v5 on v4

--- a/solution.py
+++ b/solution.py
@@ -350,17 +350,25 @@
     )(acc, ml)
 
 
-def mlp_pair(attn, hidden, w_out, w_up, w_down, layer, cid):
+def mlp_pair(attn, hidden, w_out, w_up, w_down, w_next, layer, cid):
     rows, d = attn.shape
     ff = w_up.shape[2]
     r = -(-rows // 32) * 32
     tile = 512
     d_half, f_half = d // 2, ff // 2
     n_o, n_f = d_half // tile, f_half // tile
-    ring_c, ring_r = min(8, n_o + n_f), min(6, n_f)
+    ring_c, ring_r = 8, 6
+    halves = [w.shape[2] // 2 for w in w_next]
+    parts = [(w, t * tile) for w, h in enumerate(halves) for t in range(h // tile)]
+    n_p, p_half = len(parts), sum(halves)
     attn, hidden = (jnp.pad(t, ((0, r - rows), (0, 0))) for t in (attn, hidden))
 
-    def body(attn_ref, hid_ref, wo_ref, wu_ref, wd_ref, o_ref, x_all, h_all, hm, act, acc, rx, wc, wr, csem, rsem, ssem, qsem):
+    def body(attn_ref, hid_ref, wo_ref, wu_ref, wd_ref, *rest):
+        wn_refs, rest = rest[:len(w_next)], rest[len(w_next):]
+        o_ref, rest = rest[0], rest[1:]
+        if n_p:
+            p_ref, p_to, p_in, rest = rest[0], rest[1], rest[2], rest[3:]
+        x_all, h_all, hm, act, acc, rx, wc, wr, csem, rsem, ssem, qsem = rest
         me = lax.axis_index('kv')
         core = lax.rem(me, 2)
         peer = me + 1 - 2 * core
@@ -374,6 +382,12 @@
             slot = lax.rem(c, ring_c)
             return pltpu.make_async_copy(src, wc.at[slot], csem.at[slot])
 
+        def proj(p):
+            w, lo = parts[p]
+            src = wn_refs[w].at[layer + 1, :, pl.ds(pl.multiple_of(core * halves[w] + lo, tile), tile)]
+            slot = (n_o + n_f + p) % ring_c
+            return pltpu.make_async_copy(src, wc.at[slot], csem.at[slot])
+
         def row(j):
             slot = lax.rem(j, ring_r)
             src = wd_ref.at[layer, pl.ds(pl.multiple_of(core * f_half + j * tile, tile), tile), :]
@@ -427,6 +441,11 @@
             def _():
                 col(c + ring_c, False).start()
 
+            for p in range(n_p):
+                @pl.when(c + ring_c == n_o + n_f + p)
+                def _():
+                    proj(p).start()
+
             @pl.when(j < ring_r)
             def _():
                 row(j).start()
@@ -445,24 +464,62 @@
         cp.start()
         cp.wait()
         o_ref[...] = (hm[mine].astype(jnp.float32) + (acc[mine] + rx[...])).astype(o_ref.dtype)
+        if not n_p:
+            return
+        cp = send(o_ref, x_all.at[mine], 4)
+        cp.start()
+        x_all[mine] = o_ref[...]
+        cp.wait()
+        at = 0
+        for p in range(n_p):
+            w, lo = parts[p]
+            proj(p).wait()
+            res = jnp.dot(x_all[...], wc[(n_o + n_f + p) % ring_c], preferred_element_type=jnp.float32).astype(jnp.bfloat16)
+            first = 2 * sum(halves[:w])
+            acc_at = pl.ds(pl.multiple_of(first + core * halves[w] + lo, tile), tile)
+
+            @pl.when(core == 0)
+            def _():
+                p_ref[:, acc_at] = res[:r]
+                p_to[:, at:at + tile] = res[r:]
+
+            @pl.when(core == 1)
+            def _():
+                p_ref[:, acc_at] = res[r:]
+                p_to[:, at:at + tile] = res[:r]
+
+            at += tile
+        cp = send(p_to, p_in, 5)
+        cp.start()
+        cp.wait()
+        at = 0
+        for w, lo in parts:
+            first = 2 * sum(halves[:w])
+            p_ref[:, pl.ds(pl.multiple_of(first + (1 - core) * halves[w] + lo, tile), tile)] = p_in[:, at:at + tile]
+            at += tile
 
     vmem, any_spec = pl.BlockSpec(memory_space=pltpu.VMEM), pl.BlockSpec(memory_space=pl.ANY)
+    out_shape = [jax.ShapeDtypeStruct((r, d), jnp.bfloat16)]
+    extra = []
+    if n_p:
+        out_shape.append(jax.ShapeDtypeStruct((r, 2 * p_half), jnp.bfloat16))
+        extra = [pltpu.VMEM((r, p_half), jnp.bfloat16)] * 2
     out = pl.pallas_call(
         body,
-        out_shape=jax.ShapeDtypeStruct((r, d), jnp.bfloat16),
-        in_specs=[vmem, vmem, any_spec, any_spec, any_spec],
-        out_specs=vmem,
-        scratch_shapes=[
+        out_shape=out_shape,
+        in_specs=[vmem, vmem] + [any_spec] * (3 + len(w_next)),
+        out_specs=[vmem] * len(out_shape),
+        scratch_shapes=extra + [
             pltpu.VMEM((2 * r, d), jnp.bfloat16), pltpu.VMEM((2 * r, d), jnp.bfloat16), pltpu.VMEM((2 * r, d), jnp.bfloat16),
             pltpu.VMEM((2 * r, f_half), jnp.bfloat16), pltpu.VMEM((2 * r, d), jnp.float32), pltpu.VMEM((r, d), jnp.float32),
             pltpu.VMEM((ring_c, d, tile), jnp.bfloat16), pltpu.VMEM((ring_r, tile, d), jnp.bfloat16),
             pltpu.SemaphoreType.DMA((ring_c,)), pltpu.SemaphoreType.DMA((ring_r,)),
-            pltpu.SemaphoreType.DMA((4,)), pltpu.SemaphoreType.DMA((4,)),
+            pltpu.SemaphoreType.DMA((6,)), pltpu.SemaphoreType.DMA((6,)),
         ],
         compiler_params=pltpu.CompilerParams(collective_id=cid, has_side_effects=True, vmem_limit_bytes=58 * 1024 * 1024),
         cost_estimate=pl.CostEstimate(flops=6_000_000_000, bytes_accessed=60_000_000, transcendentals=0),
-    )(attn, hidden, w_out, w_up, w_down)
-    return out[:rows]
+    )(attn, hidden, w_out, w_up, w_down, *w_next)
+    return [t[:rows] for t in out]
 
 
 def attend(info, counts, qkv, pools_in, unit_srcs, first_unit, prev_pools, state, layer, part, n_slots, layers, page, kvh, q_group, hd):
@@ -770,9 +827,11 @@
         got = along_z(hops)
         for layer in range(layers):
             dot = lambda a, w: jnp.dot(a, w[layer], preferred_element_type=jnp.float32)
-            query = dot(hidden, w_query).astype(jnp.bfloat16).reshape(2, seq_dev, heads, head_dim)
-            k_new = dot(hidden, w_key).astype(jnp.bfloat16).reshape(2, seq_dev, kv_heads, head_dim)
-            v_new = dot(hidden, w_value).astype(jnp.bfloat16).reshape(2, seq_dev, kv_heads, head_dim)
+            if layer == 0:
+                parts = [dot(hidden, w).astype(jnp.bfloat16) for w in (w_query, w_key, w_value)]
+            else:
+                parts = jnp.split(ahead, [heads * head_dim, (heads + kv_heads) * head_dim], axis=1)
+            query, k_new, v_new = (t.reshape(2, seq_dev, -1, head_dim) for t in parts)
             per_seq = lambda t: jnp.swapaxes(t, 0, 1).reshape(seq_dev, -1, head_dim)
             qkv = jnp.concatenate([per_seq(query), per_seq(k_new), per_seq(v_new)], axis=1)
             qkv = gather_rows(qkv, 'kv', n_cols, 0).reshape(row_seqs, -1, head_dim)
@@ -780,7 +839,7 @@
             if layer == 0:
                 *pools, acc, ml = attend(*by_class, qkv, [k_rows, v_rows], [], 0, pools, None, part=0, **dims)
                 next_hops = pick(z_list, units[1], [Z_CORE] * (n_rows - 1))
-                got, acc, next_hops = lax.optimization_barrier((got, acc, next_hops))
+                got, acc, next_hops, by_use = lax.optimization_barrier((got, acc, next_hops, by_use))
                 next_got = along_z(next_hops)
                 all_units = swap(units[0], got)
                 hop, = pick(y_list, all_units, [Y_CORE])
@@ -797,7 +856,9 @@
                 hop, = pick(y_list, all_units, [Y_CORE])
                 hop, o = lax.optimization_barrier((hop, o))
             attn_out = jnp.swapaxes(o.reshape(seq_dev, 2, heads * head_dim), 0, 1).reshape(2 * seq_dev, heads * head_dim)
-            hidden = mlp_pair(attn_out, hidden, w_out, w_up, w_down, layer, 3 + layer)
+            w_next = (w_query, w_key, w_value) if layer + 1 < layers else ()
+            hidden, *ahead = mlp_pair(attn_out, hidden, w_out, w_up, w_down, w_next, layer, 3 + layer)
+            ahead = ahead[0] if ahead else None
         k_out, v_out = (p.reshape(k_pool.shape) for p in pools)
         return hidden.reshape(2, seq_dev, width), k_out, v_out
 

time: 377 us -> 375 us (level)
  matrix products: 32 us -> 15.2 us
  Pallas kernels: 189 us -> 200 us
    dot_general x6 -> x3, matrix products: 32 us -> 15.2 us  [per_device(): dot = lambda a, w: jnp.dot(a, w[layer], preferred_element_type=jnp.float32)]
    pallas_call x2, Pallas kernels: 46 us -> 56.5 us  [mlp_pair(): pl.pallas_call(body, out_shape=out_shape, in_specs=[vmem, vmem] + [any_sp...]
  transfers between devices with their start and end apart: 19 -> 19, of which waited for: 10 -> 11; matrix products, arithmetic and copies ran while one was open for 9% -> 4% of each run, Pallas kernels for 29% -> 32%
where the time goes in v5:
time: 375 us; the launch traced here: 374 us
  Pallas kernels  200 us (53%)
  waiting for transfers between devices  98.2 us (26%)
  other arithmetic  17.4 us (5%)
  between operations  15.9 us (4%)
  matrix products  15.2 us (4%)
  starting transfers between devices  14.6 us (4%)
  local copies, waits for them, and re-layouts  12.9 us (3%)
    ppermute x6, waiting for transfers between devices, along_z(): got.append(lax.ppermute(h, 'kv2', z))  61.4 us
    pallas_call x2, Pallas kernels, mlp_pair(): pl.pallas_call(body, out_shape=out_shape, in_specs=[vmem, vmem] + [any_sp...  56.5 us
    pallas_call x2, Pallas kernels, combine(): pl.pallas_call(body, out_shape=jax.ShapeDtypeStruct((b, r, hd), jnp.bfloa...  49.3 us
    pallas_call x4, Pallas kernels, attend(): pl.pallas_call(body, out_shape=[pool, pool, jax.ShapeDtypeStruct((n_seq +...  33.4 us
    ppermute x2, waiting for transfers between devices, along_y(): got = lax.ppermute(hop, 'kv', over)  28.7 us
    pallas_call x2, Pallas kernels, gather_rows(): pl.pallas_call(body, out_shape=jax.ShapeDtypeStruct((n,) + x.shape, x.dty...  23.2 us
    pallas_call x4, Pallas kernels, pick(): pl.pallas_call(body, out_shape=[jax.ShapeDtypeStruct((size,) + tail, dtyp...  16.2 us
    dot_general x3, matrix products, per_device(): dot = lambda a, w: jnp.dot(a, w[layer], preferred_element_type=jnp.float32)  15.2 us
  transfers between devices with their start and end apart: 19, of which 11 were waited for; matrix products, arithmetic and copies ran while one was open for 4% of the time, Pallas kernels for 32%

profile of v5, /device:TPU:9, one launch (start us, length us, event | category | flops | bytes accessed | tf_op | source)
XLA Modules:
  0.0 373.9 jit_solution(14444179637381405660)
XLA Ops:
  8.4 3.2 take_pages.1
  13.3 9.3 %share_plan.1 = s32[32,1,128]{2,1,0:T(1,128)} custom-call(s32[1,128]{1,0:T(1,128)} %pad_bitcast_fusion.x_ref), custom_call_target="tpu_custom_call" | custom-call | tf_op jit(solution)/shard_map/share_plan/pallas_call | solution.py:129
  23.9 1.7 route_z.1.idx_ref
  25.6 5.0 %shard_map.148 = (bf16[6,512,128]{2,1,0:T(8,128)(2,1)}, bf16[6,512,128]{2,1,0:T(8,128)(2,1)}, bf16[6,512,128]{2,1,0:T(8,128)(2,1)}) custom-call(s32[64]{0:T(128)} %route_z.1.idx_ref, bf16[12,512,128]{2,1,0:T(8,128)(2,1)S(1)} %get-tuple-element.74.rest_0_, bf16[12,512,128]{2,1,0:T(8,128)(2,1)} %collective-permute-done.1.rest_1_), custom_call_target="tpu_custom_call" | custom-call | flops 100000000 | bytes 5000000 | tf_op jit(solution)/shard_map/pallas_call | solution.py:93
  36.4 6.9 %route.1 = (s32[64]{0:T(128)}, s32[64]{0:T(128)}) custom-call(s32[192]{0:T(256)} %copy-done.10, s32[192]{0:T(256)} %reshape.246.dev_ref, s32[2]{0:T(128)} %pad_add_fusion.2.pos_ref), custom_call_target="tpu_custom_call" | custom-call | flops 100000000 | bytes 1000000 | tf_op jit(solution)/shard_map/route/pallas_call | solution.py:231
  45.4 3.7 fusion.24
  49.2 3.7 fusion.21
  52.9 7.7 %fusion.12 = bf16[3,8,24,128]{3,1,2,0:T(8,128)(2,1)S(1)} fusion(bf16[24,3072]{1,0:T(8,128)(2,1)S(1)} %reshape.243, bf16[2,3072,3072]{2,1,0:T(8,128)(2,1)} %rest_0_.1), kind=kOutput, calls=%fused_computation.12 | convolution fusion | flops 453058560 | bytes 19169280 | tf_op jit(solution)/shard_map/dot_general | solution.py:829
  69.4 1.5 select_reduce_fusion.4
  71.6 11.9 %gather_rows.2 = bf16[4,12,80,128]{3,2,1,0:T(8,128)(2,1)} custom-call(bf16[12,80,128]{2,1,0:T(8,128)(2,1)} %pad_maximum_fusion.x_ref), custom_call_target="tpu_custom_call" | custom-call | flops 1000000000 | bytes 2000000 | tf_op jit(solution)/shard_map/gather_rows/pallas_call | solution.py:276
  86.1 10.6 %shard_map.149 = (bf16[120,256,128]{2,1,0:T(8,128)(2,1)}, bf16[120,256,128]{2,1,0:T(8,128)(2,1)}, f32[49,48,128]{2,1,0:T(8,128)}, f32[2,48,128]{2,1,0:T(8,128)}) custom-call(s32[4,64]{1,0:T(4,128)} %pad_add_fusion.info_ref, s32[6]{0:T(128)} %convert_reduce_fusion.4.cnt_ref, bf16[48,80,128]{2,1,0:T(8,128)(2,1)} %bitcast.111, ...), custom_call_target="tpu_custom_call" | custom-call | flops 400000000 | bytes 16000000 | tf_op jit(solution)/shard_map/pallas_call | solution.py:687
  98.0 5.0 %shard_map.150 = (bf16[6,512,128]{2,1,0:T(8,128)(2,1)}, bf16[6,512,128]{2,1,0:T(8,128)(2,1)}, bf16[6,512,128]{2,1,0:T(8,128)(2,1)}) custom-call(s32[64]{0:T(128)} %route_z.1.idx_ref, bf16[12,512,128]{2,1,0:T(8,128)(2,1)S(1)} %get-tuple-element.88.rest_0_.rest_2_, bf16[12,512,128]{2,1,0:T(8,128)(2,1)} %collective-permute-done.5.rest_1_.rest_3_), custom_call_target="tpu_custom_call" | custom-call | flops 100000000 | bytes 5000000 | tf_op jit(solution)/shard_map/pallas_call | solution.py:93
  103.1 27.5 %collective-permute-done.3.rest_3_ = bf16[6,512,128]{2,1,0:T(8,128)(2,1)} collective-permute-done((bf16[6,512,128]{2,1,0:T(8,128)(2,1)}, bf16[6,512,128]{2,1,0:T(8,128)(2,1)}, u32[]{:S(2)}, u32[]{:S(2)}) %collective-permute-start.3) | collective-permute-done | bytes 786464 | tf_op jit(solution)/shard_map/ppermute | solution.py:780
  130.6 2.5 collective-permute-done.4.rest_4_
  134.0 1.7 collective-permute-done.10.rest_6_
  138.0 3.1 shard_map.151
  141.1 1.6 collective-permute-start.12
  142.7 28.7 %collective-permute-done.12.rest_0_ = bf16[10,512,128]{2,1,0:T(8,128)(2,1)} collective-permute-done((bf16[10,512,128]{2,1,0:T(8,128)(2,1)}, bf16[10,512,128]{2,1,0:T(8,128)(2,1)}, u32[]{:S(2)}, u32[]{:S(2)}) %collective-permute-start.12) | collective-permute-done | bytes 1310752 | tf_op jit(solution)/shard_map/ppermute | solution.py:787
  175.2 4.9 %shard_map.152 = (bf16[120,256,128]{2,1,0:T(8,128)(2,1)}, bf16[120,256,128]{2,1,0:T(8,128)(2,1)}, f32[49,48,128]{2,1,0:T(8,128)}, f32[2,48,128]{2,1,0:T(8,128)}) custom-call(s32[4,64]{1,0:T(4,128)} %pad_add_fusion.info_ref, s32[6]{0:T(128)} %convert_reduce_fusion.4.cnt_ref, ...), custom_call_target="tpu_custom_call", output_to_operand_aliasing={{0}: (11, {}), {1}: (12, {})} | custom-call | flops 400000000 | bytes 16000000 | tf_op jit(solution)/shard_map/pallas_call | solution.py:687
  180.1 5.1 %shard_map.153 = (bf16[120,256,128]{2,1,0:T(8,128)(2,1)}, bf16[120,256,128]{2,1,0:T(8,128)(2,1)}, f32[49,48,128]{2,1,0:T(8,128)}, f32[2,48,128]{2,1,0:T(8,128)}) custom-call(s32[4,64]{1,0:T(4,128)} %pad_add_fusion.info_ref, s32[6]{0:T(128)} %convert_reduce_fusion.4.cnt_ref, ...), custom_call_target="tpu_custom_call", output_to_operand_aliasing={{0}: (6, {}), {1}: (7, {})} | custom-call | flops 400000000 | bytes 16000000 | tf_op jit(solution)/shard_map/pallas_call | solution.py:687
  185.2 26.0 %combine.2 = bf16[12,48,128]{2,1,0:T(8,128)(2,1)} custom-call(f32[49,48,128]{2,1,0:T(8,128)} %get-tuple-element.109.acc_ref, f32[2,48,128]{2,1,0:T(8,128)} %get-tuple-element.110.ml_ref), custom_call_target="tpu_custom_call" | custom-call | flops 1000000000 | bytes 2000000 | tf_op jit(solution)/shard_map/combine/pallas_call | solution.py:340
  211.2 29.5 %collective-permute-done.7.rest_3_.rest_5_ = bf16[6,512,128]{2,1,0:T(8,128)(2,1)} collective-permute-done((bf16[6,512,128]{2,1,0:T(8,128)(2,1)}, bf16[6,512,128]{2,1,0:T(8,128)(2,1)}, u32[]{:S(2)}, u32[]{:S(2)}) %collective-permute-start.7) | collective-permute-done | bytes 786464 | tf_op jit(solution)/shard_map/ppermute | solution.py:780
  240.8 1.9 collective-permute-done.8.rest_4_.rest_6_
  243.7 1.6 collective-permute-done.14.rest_5_.rest_7_
  247.7 3.1 shard_map.154
  250.8 1.5 collective-permute-start.17
  254.8 33.4 %shard_map.155 = (bf16[32,3072]{1,0:T(8,128)(2,1)}, bf16[32,5120]{1,0:T(8,128)(2,1)}) custom-call(bf16[32,3072]{1,0:T(8,128)(2,1)} %pad.18.attn_ref, bf16[32,3072]{1,0:T(8,128)(2,1)} %pad.19.hid_ref, bf16[2,3072,3072]{2,1,0:T(8,128)(2,1)} %wo_ref.3, bf16[2,3072,8192]{2,1,0:T(8,128)(2,1)} %wu_ref.3, bf16[2,8192,3072]{2,1,0:T(8,128)(2,1)} %wd_ref.3, ...), custom_call_target="tpu_custom_call" | custom-call | flops 6000000000 | bytes 60000000 | tf_op jit(solution)/shard_map/pallas_call | solution.py:507
  291.2 11.3 %gather_rows.3 = bf16[4,12,80,128]{3,2,1,0:T(8,128)(2,1)} custom-call(bf16[12,80,128]{2,1,0:T(8,128)(2,1)} %pad_maximum_fusion.1.x_ref), custom_call_target="tpu_custom_call" | custom-call | flops 1000000000 | bytes 2000000 | tf_op jit(solution)/shard_map/gather_rows/pallas_call | solution.py:276
  302.6 1.7 broadcast_select_fusion.hid_ref
  304.3 12.8 %shard_map.156 = (bf16[120,256,128]{2,1,0:T(8,128)(2,1)}, bf16[120,256,128]{2,1,0:T(8,128)(2,1)}, f32[49,48,128]{2,1,0:T(8,128)}, f32[2,48,128]{2,1,0:T(8,128)}) custom-call(s32[4,64]{1,0:T(4,128)} %pad_add_fusion.1.info_ref, s32[2]{0:T(128)} %fusion.35.cnt_ref, bf16[48,80,128]{2,1,0:T(8,128)(2,1)} %bitcast.114, ...), custom_call_target="tpu_custom_call", output_to_operand_aliasing={{0}: (16, {}), {1}: (17, {})} | custom-call | flops 400000000 | bytes 16000000 | tf_op jit(solution)/shard_map/pallas_call | solution.py:687
  317.1 23.3 %combine.3 = bf16[12,48,128]{2,1,0:T(8,128)(2,1)} custom-call(f32[49,48,128]{2,1,0:T(8,128)} %get-tuple-element.120.acc_ref, f32[2,48,128]{2,1,0:T(8,128)} %get-tuple-element.121.ml_ref), custom_call_target="tpu_custom_call" | custom-call | flops 1000000000 | bytes 2000000 | tf_op jit(solution)/shard_map/combine/pallas_call | solution.py:340
  342.2 23.1 %shard_map.157 = bf16[32,3072]{1,0:T(8,128)(2,1)} custom-call(bf16[32,3072]{1,0:T(8,128)(2,1)} %pad.20.attn_ref, bf16[32,3072]{1,0:T(8,128)(2,1)} %broadcast_select_fusion.hid_ref, bf16[2,3072,3072]{2,1,0:T(8,128)(2,1)} %wo_ref.3, bf16[2,3072,8192]{2,1,0:T(8,128)(2,1)} %wu_ref.3, bf16[2,8192,3072]{2,1,0:T(8,128)(2,1)} %wd_ref.3), custom_call_target="tpu_custom_call" | custom-call | flops 6000000000 | bytes 60000000 | tf_op jit(solution)/shard_map/pallas_call | solution.py:507
  (149 shorter events, 43.2 us)
Async XLA Ops:
  8.3 4.3 %copy-start.21 = (s32[12]{0:T(128)S(1)}, s32[12]{0:T(128)}, u32[]{:S(2)}) copy-start(s32[12]{0:T(128)} %param.27) | copy-start | bytes 148
  8.4 14.9 %copy-start.9 = (bf16[2,12,3072]{2,0,1:T(2,128)(2,1)S(1)}, bf16[2,12,3072]{2,0,1:T(2,128)(2,1)}, u32[]{:S(2)}) copy-start(bf16[2,12,3072]{2,0,1:T(2,128)(2,1)} %param.17) | copy-start | bytes 442372
  11.6 163.6 %copy-start.3 = (bf16[12,512,128]{2,1,0:T(8,128)(2,1)}, bf16[12,512,128]{2,1,0:T(8,128)(2,1)S(1)}, u32[]{:S(2)}) copy-start(bf16[12,512,128]{2,1,0:T(8,128)(2,1)S(1)} %get-tuple-element.74.rest_0_) | copy-start | bytes 4718596
  11.6 241.4 %copy-start = (bf16[12,512,128]{2,1,0:T(8,128)(2,1)}, bf16[12,512,128]{2,1,0:T(8,128)(2,1)S(1)}, u32[]{:S(2)}) copy-start(bf16[12,512,128]{2,1,0:T(8,128)(2,1)S(1)} %get-tuple-element.88.rest_0_.rest_2_) | copy-start | bytes 4718596
  11.6 14.0 %collective-permute-start.1 = (bf16[12,512,128]{2,1,0:T(8,128)(2,1)S(1)}, bf16[12,512,128]{2,1,0:T(8,128)(2,1)}, u32[]{:S(2)}, u32[]{:S(2)}) collective-permute-start(bf16[12,512,128]{2,1,0:T(8,128)(2,1)S(1)} %get-tuple-element.74.rest_0_), channel_id=1, source_target_pairs={{0,1},{1,0},{2,3},{3,2},{4,5},{5,4},{6,7},{7,6},{8,9},{9,8},{10,11... | collective-permute-start | bytes 4718600 | tf_op jit(solution)/shard_map/ppermute | solution.py:738
  12.4 11.0 %copy-start.11 = (s32[12]{0:T(128)}, s32[12]{0:T(128)S(1)}, u32[]{:S(2)}) copy-start(s32[12]{0:T(128)S(1)} %and_select_fusion.5.own_ref) | copy-start | bytes 148
  12.4 11.0 %collective-permute-start = (s32[12]{0:T(128)S(1)}, s32[12]{0:T(128)S(1)}, u32[]{:S(2)}, u32[]{:S(2)}) collective-permute-start(s32[12]{0:T(128)S(1)} %and_select_fusion.5.own_ref), channel_id=1, source_target_pairs={{0,1},{1,0},{2,3},{3,2},{4,5},{5,4},{6,7},{7,6},{8,9},{9,8},{10,11... | collective-permute-start | bytes 152 | tf_op jit(solution)/shard_map/ppermute | solution.py:739
  44.3 4.9 %copy-start.17 = (s32[60]{0:T(128)}, s32[60]{0:T(128)S(1)}, u32[]{:S(2)}) copy-start(s32[60]{0:T(128)S(1)} %select_reduce_fusion.9) | copy-start | bytes 724
  60.7 37.3 %collective-permute-start.5 = (bf16[12,512,128]{2,1,0:T(8,128)(2,1)S(1)}, bf16[12,512,128]{2,1,0:T(8,128)(2,1)}, u32[]{:S(2)}, u32[]{:S(2)}) collective-permute-start(bf16[12,512,128]{2,1,0:T(8,128)(2,1)S(1)} %get-tuple-element.88.rest_0_.rest_2_), channel_id=1, source_target_pairs={{0,1},{1,0},{2,3},{3,2},{4,5},{5,4},{6,7},{7,6},{8,9},{9,8},{10,11... | collective-permute-start | bytes 4718600 | tf_op jit(solution)/shard_map/ppermute | solution.py:754
  61.6 41.5 %collective-permute-start.2 = (bf16[6,512,128]{2,1,0:T(8,128)(2,1)}, bf16[6,512,128]{2,1,0:T(8,128)(2,1)}, u32[]{:S(2)}, u32[]{:S(2)}) collective-permute-start(bf16[6,512,128]{2,1,0:T(8,128)(2,1)} %get-tuple-element.80), channel_id=1, source_target_pairs={{0,4},{4,8},{8,12},{12,0},{1,5},{5,9},{9,13},{13,1},{2,6},{6,10},{... | collective-permute-start | bytes 2359304 | tf_op jit(solution)/shard_map/ppermute | solution.py:780
  62.9 67.7 %collective-permute-start.3 = (bf16[6,512,128]{2,1,0:T(8,128)(2,1)}, bf16[6,512,128]{2,1,0:T(8,128)(2,1)}, u32[]{:S(2)}, u32[]{:S(2)}) collective-permute-start(bf16[6,512,128]{2,1,0:T(8,128)(2,1)} %get-tuple-element.81), channel_id=1, source_target_pairs={{0,8},{4,12},{8,0},{12,4},{1,9},{5,13},{9,1},{13,5},{2,10},{6,14},... | collective-permute-start | bytes 2359304 | tf_op jit(solution)/shard_map/ppermute | solution.py:780
  64.1 68.9 %collective-permute-start.4 = (bf16[6,512,128]{2,1,0:T(8,128)(2,1)}, bf16[6,512,128]{2,1,0:T(8,128)(2,1)}, u32[]{:S(2)}, u32[]{:S(2)}) collective-permute-start(bf16[6,512,128]{2,1,0:T(8,128)(2,1)} %get-tuple-element.82), channel_id=1, source_target_pairs={{0,12},{4,0},{8,4},{12,8},{1,13},{5,1},{9,5},{13,9},{2,14},{6,2},{... | collective-permute-start | bytes 2359304 | tf_op jit(solution)/shard_map/ppermute | solution.py:780
  86.1 10.7 %copy-start.12 = (s32[64]{0:T(128)S(1)}, s32[64]{0:T(128)}, u32[]{:S(2)}) copy-start(s32[64]{0:T(128)} %get-tuple-element.143) | copy-start | bytes 772
  86.1 10.7 %copy-start.13 = (s32[64]{0:T(128)S(1)}, s32[64]{0:T(128)}, u32[]{:S(2)}) copy-start(s32[64]{0:T(128)} %get-tuple-element.147) | copy-start | bytes 772
  86.1 10.7 %copy-start.14 = (s32[64]{0:T(128)S(1)}, s32[64]{0:T(128)}, u32[]{:S(2)}) copy-start(s32[64]{0:T(128)} %get-tuple-element.149) | copy-start | bytes 772
  86.1 11.3 %copy-start.18 = (s32[60]{0:T(128)S(1)}, s32[60]{0:T(128)}, u32[]{:S(2)}) copy-start(s32[60]{0:T(128)} %copy-done.17) | copy-start | bytes 724
  133.0 2.7 collective-permute-start.10
  133.5 3.4 collective-permute-start.11
  133.5 4.5 %collective-permute-start.9 = (bf16[6,512,128]{2,1,0:T(8,128)(2,1)}, bf16[6,512,128]{2,1,0:T(8,128)(2,1)}, u32[]{:S(2)}, u32[]{:S(2)}) collective-permute-start(bf16[6,512,128]{2,1,0:T(8,128)(2,1)} %collective-permute-done.2.rest_2_), channel_id=1, source_target_pairs={{0,1},{1,0},{2,3},{3,2},{4,5},{5,4},{6,7},{7,6},{8,9},{9,8},{10,11... | collective-permute-start | bytes 2359304 | tf_op jit(solution)/shard_map/ppermute | solution.py:784
  141.1 30.3 %collective-permute-start.12 = (bf16[10,512,128]{2,1,0:T(8,128)(2,1)}, bf16[10,512,128]{2,1,0:T(8,128)(2,1)}, u32[]{:S(2)}, u32[]{:S(2)}) collective-permute-start(bf16[10,512,128]{2,1,0:T(8,128)(2,1)} %shard_map.151), channel_id=1, source_target_pairs={{0,2},{1,3},{2,0},{3,1},{4,6},{5,7},{6,4},{7,5},{8,10},{9,11},{10,... | collective-permute-start | bytes 3932168 | tf_op jit(solution)/shard_map/ppermute | solution.py:787
  171.4 8.7 %collective-permute-start.13 = (bf16[10,512,128]{2,1,0:T(8,128)(2,1)}, bf16[10,512,128]{2,1,0:T(8,128)(2,1)}, u32[]{:S(2)}, u32[]{:S(2)}) collective-permute-start(bf16[10,512,128]{2,1,0:T(8,128)(2,1)} %collective-permute-done.12.rest_0_), channel_id=1, source_target_pairs={{0,1},{1,0},{2,3},{3,2},{4,5},{5,4},{6,7},{7,6},{8,9},{9,8},{10,11... | collective-permute-start | bytes 3932168 | tf_op jit(solution)/shard_map/ppermute | solution.py:788
  172.7 38.5 %collective-permute-start.6 = (bf16[6,512,128]{2,1,0:T(8,128)(2,1)}, bf16[6,512,128]{2,1,0:T(8,128)(2,1)}, u32[]{:S(2)}, u32[]{:S(2)}) collective-permute-start(bf16[6,512,128]{2,1,0:T(8,128)(2,1)} %get-tuple-element.95), channel_id=1, source_target_pairs={{0,4},{4,8},{8,12},{12,0},{1,5},{5,9},{9,13},{13,1},{2,6},{6,10},{... | collective-permute-start | bytes 2359304 | tf_op jit(solution)/shard_map/ppermute | solution.py:780
  172.7 68.0 %collective-permute-start.7 = (bf16[6,512,128]{2,1,0:T(8,128)(2,1)}, bf16[6,512,128]{2,1,0:T(8,128)(2,1)}, u32[]{:S(2)}, u32[]{:S(2)}) collective-permute-start(bf16[6,512,128]{2,1,0:T(8,128)(2,1)} %get-tuple-element.96), channel_id=1, source_target_pairs={{0,8},{4,12},{8,0},{12,4},{1,9},{5,13},{9,1},{13,5},{2,10},{6,14},... | collective-permute-start | bytes 2359304 | tf_op jit(solution)/shard_map/ppermute | solution.py:780
  173.8 68.9 %collective-permute-start.8 = (bf16[6,512,128]{2,1,0:T(8,128)(2,1)}, bf16[6,512,128]{2,1,0:T(8,128)(2,1)}, u32[]{:S(2)}, u32[]{:S(2)}) collective-permute-start(bf16[6,512,128]{2,1,0:T(8,128)(2,1)} %get-tuple-element.97), channel_id=1, source_target_pairs={{0,12},{4,0},{8,4},{12,8},{1,13},{5,1},{9,5},{13,9},{2,14},{6,2},{... | collective-permute-start | bytes 2359304 | tf_op jit(solution)/shard_map/ppermute | solution.py:780
  242.7 2.6 collective-permute-start.14
  243.2 3.2 collective-permute-start.15
  243.2 4.5 %collective-permute-start.16 = (bf16[6,512,128]{2,1,0:T(8,128)(2,1)}, bf16[6,512,128]{2,1,0:T(8,128)(2,1)}, u32[]{:S(2)}, u32[]{:S(2)}) collective-permute-start(bf16[6,512,128]{2,1,0:T(8,128)(2,1)} %collective-permute-done.8.rest_4_.rest_6_), channel_id=1, source_target_pairs={{0,1},{1,0},{2,3},{3,2},{4,5},{5,4},{6,7},{7,6},{8,9},{9,8},{10,11... | collective-permute-start | bytes 2359304 | tf_op jit(solution)/shard_map/ppermute | solution.py:784
  250.8 37.5 %collective-permute-start.17 = (bf16[10,512,128]{2,1,0:T(8,128)(2,1)}, bf16[10,512,128]{2,1,0:T(8,128)(2,1)S(1)}, u32[]{:S(2)}, u32[]{:S(2)}) collective-permute-start(bf16[10,512,128]{2,1,0:T(8,128)(2,1)} %shard_map.154), channel_id=1, source_target_pairs={{0,2},{1,3},{2,0},{3,1},{4,6},{5,7},{6,4},{7,5},{8,10},{9,11},{10,... | collective-permute-start | bytes 3932168 | tf_op jit(solution)/shard_map/ppermute | solution.py:787
  254.8 47.8 %copy-start.16 = (pred[32]{0:T(512)(128)(4,1)S(1)}, pred[32]{0:T(512)(128)(4,1)}, u32[]{:S(2)}) copy-start(pred[32]{0:T(512)(128)(4,1)} %constant.149.clone.1) | copy-start | bytes 100
  254.8 49.6 %copy-start.1 = (bf16[12,512,128]{2,1,0:T(8,128)(2,1)S(1)}, bf16[12,512,128]{2,1,0:T(8,128)(2,1)}, u32[]{:S(2)}) copy-start(bf16[12,512,128]{2,1,0:T(8,128)(2,1)} %copy-done) | copy-start | bytes 4718596
  288.2 16.1 %copy-start.7 = (bf16[10,512,128]{2,1,0:T(8,128)(2,1)}, bf16[10,512,128]{2,1,0:T(8,128)(2,1)S(1)}, u32[]{:S(2)}) copy-start(bf16[10,512,128]{2,1,0:T(8,128)(2,1)S(1)} %collective-permute-done.17.rest_10_) | copy-start | bytes 3932164
  288.2 16.1 %collective-permute-start.18 = (bf16[10,512,128]{2,1,0:T(8,128)(2,1)S(1)}, bf16[10,512,128]{2,1,0:T(8,128)(2,1)}, u32[]{:S(2)}, u32[]{:S(2)}) collective-permute-start(bf16[10,512,128]{2,1,0:T(8,128)(2,1)S(1)} %collective-permute-done.17.rest_10_), channel_id=1, source_target_pairs={{0,1},{1,0},{2,3},{3,2},{4,5},{5,4},{6,7},{7,6},{8,9},{9,8},{10,11... | collective-permute-start | bytes 3932168 | tf_op jit(solution)/shard_map/ppermute | solution.py:788
  (8 other events, 18.7 us)

commit v6 on v5

--- a/solution.py
+++ b/solution.py
@@ -11,6 +11,19 @@
 UNROLL = 4
 Z_CORE = 6
 Y_CORE = 10
+
+
+def cost(flops, size):
+    return pl.CostEstimate(flops=flops, bytes_accessed=size, transcendentals=0)
+
+
+SMALL = cost(100_000_000, 4_000_000)
+
+
+def around(me):
+    sib = me + 1 - 2 * lax.rem(me, 2)
+    over = lax.rem(me + 2, 4)
+    return sib, over, lax.rem(sib + 2, 4)
 
 
 def uninit(shape, dtype):
@@ -52,7 +65,7 @@
         out_specs=[any_spec] * layers,
         scratch_shapes=[pltpu.VMEM((layers, m, 2 * prow, hd), k_rows.dtype),
                         pltpu.SemaphoreType.DMA((layers, 2 * m)), pltpu.SemaphoreType.DMA((layers,))],
-        cost_estimate=pl.CostEstimate(flops=100_000_000, bytes_accessed=12_000_000, transcendentals=0),
+        cost_estimate=SMALL,
         name="take_pages",
     )(rows, k_rows, v_rows)
 
@@ -96,7 +109,7 @@
         in_specs=[pl.BlockSpec(memory_space=pltpu.SMEM)] + [any_spec] * len(sources),
         out_specs=[any_spec] * len(splits),
         scratch_shapes=[pltpu.VMEM((n,) + tail, dtype), pltpu.SemaphoreType.DMA((n,)), pltpu.SemaphoreType.DMA((len(splits),))],
-        cost_estimate=pl.CostEstimate(flops=100_000_000, bytes_accessed=5_000_000, transcendentals=0),
+        cost_estimate=SMALL,
     )(lists, *sources)
 
 
@@ -234,15 +247,9 @@
         in_specs=[smem] * 3,
         out_specs=[smem] * 2,
         scratch_shapes=[pltpu.SMEM((64,), jnp.int32), pltpu.SMEM((8,), jnp.int32)],
-        cost_estimate=pl.CostEstimate(flops=100_000_000, bytes_accessed=1_000_000, transcendentals=0),
+        cost_estimate=SMALL,
         name="route",
     )(dst, dev, pos)
-
-
-def around(me):
-    sib = me + 1 - 2 * lax.rem(me, 2)
-    over = lax.rem(me + 2, 4)
-    return sib, over, lax.rem(sib + 2, 4)
 
 
 def enter(axis, peers):
@@ -280,78 +287,92 @@
         out_specs=pl.BlockSpec(memory_space=pltpu.VMEM),
         scratch_shapes=[pltpu.SemaphoreType.DMA((3,)), pltpu.SemaphoreType.DMA((3,))],
         compiler_params=pltpu.CompilerParams(collective_id=cid, has_side_effects=True),
-        cost_estimate=pl.CostEstimate(flops=1_000_000_000, bytes_accessed=2_000_000, transcendentals=0),
+        cost_estimate=SMALL,
         name="gather_rows",
     )(x)
+
+
+def merge_scratch(b, r, hd, ml_shape):
+    block, stats = pltpu.VMEM((b, r, hd), jnp.float32), pltpu.VMEM(ml_shape, jnp.float32)
+    return [block, block, stats, block, stats, block, stats, pltpu.SemaphoreType.DMA((5,)), pltpu.SemaphoreType.DMA((5,))]
+
+
+def merge(acc_ref, ml_ref, scratch, axis, b, emit):
+    sib_me, sib_over, ml_sib, to_over, ml_to, y_acc, ml_y, send_sem, recv_sem = scratch
+    r = acc_ref.shape[1]
+    me = lax.axis_index(axis)
+    sib, over, diag = around(me)
+
+    def send(src, dst, peer, i):
+        return pltpu.make_async_remote_copy(
+            src_ref=src, dst_ref=dst, send_sem=send_sem.at[i], recv_sem=recv_sem.at[i],
+            device_id={axis: peer}, device_id_type=MESH_ID)
+
+    near = [send(acc_ref.at[pl.ds(diag * b, b)], sib_over, sib, 0), send(ml_ref, ml_sib, sib, 1),
+            send(acc_ref.at[pl.ds(sib * b, b)], sib_me, sib, 2)]
+    for cp in near:
+        cp.start()
+    near[0].wait()
+    near[1].wait()
+    lane = lax.broadcasted_iota(jnp.int32, (r, ml_ref.shape[2]), 1)
+
+    def pick(t, s):
+        return jnp.sum(jnp.where(lane == s, t, 0.0), axis=1, keepdims=True)
+
+    top = jnp.maximum(ml_ref[0], ml_sib[0])
+    w_own, w_sib = jnp.exp(ml_ref[0] - top), jnp.exp(ml_sib[0] - top)
+    tot = w_own * ml_ref[1] + w_sib * ml_sib[1]
+    ml_to[0] = top
+    ml_to[1] = tot
+    for i in range(b):
+        s = over * b + i
+        to_over[i] = pick(w_own, s) * acc_ref[s] + pick(w_sib, s) * sib_over[i]
+    far = [send(to_over, y_acc, over, 3), send(ml_to, ml_y, over, 4)]
+    for cp in far:
+        cp.start()
+    near[2].wait()
+    far[1].wait()
+    last = jnp.maximum(top, ml_y[0])
+    f, g = jnp.exp(top - last), jnp.exp(ml_y[0] - last)
+    den = f * tot + g * ml_y[1]
+    f, g = f / den, g / den
+    w_own, w_sib = f * w_own, f * w_sib
+    for i in range(b):
+        s = me * b + i
+        sib_me[i] = pick(w_own, s) * acc_ref[s] + pick(w_sib, s) * sib_me[i]
+    far[0].wait()
+    for i in range(b):
+        emit(i, sib_me[i] + pick(g, me * b + i) * y_acc[i])
 
 
 def combine(acc, ml, axis, n, cid):
     rows, r, hd = acc.shape
     b = rows // n
 
-    def body(acc_ref, ml_ref, o_ref, sib_me, sib_over, ml_sib, to_over, ml_to, y_acc, ml_y, send_sem, recv_sem):
-        me = lax.axis_index(axis)
-        sib, over, diag = around(me)
+    def body(acc_ref, ml_ref, o_ref, *scratch):
+        sib, over, _ = around(lax.axis_index(axis))
         enter(axis, (sib, over))
 
-        def send(src, dst, peer, i):
-            return pltpu.make_async_remote_copy(
-                src_ref=src, dst_ref=dst, send_sem=send_sem.at[i], recv_sem=recv_sem.at[i],
-                device_id={axis: peer}, device_id_type=MESH_ID)
-
-        near = [send(acc_ref.at[pl.ds(diag * b, b)], sib_over, sib, 0), send(ml_ref, ml_sib, sib, 1),
-                send(acc_ref.at[pl.ds(sib * b, b)], sib_me, sib, 2)]
-        for cp in near:
-            cp.start()
-        near[0].wait()
-        near[1].wait()
-        lane = lax.broadcasted_iota(jnp.int32, (r, ml_ref.shape[2]), 1)
-
-        def pick(t, s):
-            return jnp.sum(jnp.where(lane == s, t, 0.0), axis=1, keepdims=True)
-
-        top = jnp.maximum(ml_ref[0], ml_sib[0])
-        w_own, w_sib = jnp.exp(ml_ref[0] - top), jnp.exp(ml_sib[0] - top)
-        tot = w_own * ml_ref[1] + w_sib * ml_sib[1]
-        ml_to[0] = top
-        ml_to[1] = tot
-        for i in range(b):
-            s = over * b + i
-            to_over[i] = pick(w_own, s) * acc_ref[s] + pick(w_sib, s) * sib_over[i]
-        far = [send(to_over, y_acc, over, 3), send(ml_to, ml_y, over, 4)]
-        for cp in far:
-            cp.start()
-        near[2].wait()
-        far[1].wait()
-        last = jnp.maximum(top, ml_y[0])
-        f, g = jnp.exp(top - last), jnp.exp(ml_y[0] - last)
-        den = f * tot + g * ml_y[1]
-        f, g = f / den, g / den
-        w_own, w_sib = f * w_own, f * w_sib
-        for i in range(b):
-            s = me * b + i
-            sib_me[i] = pick(w_own, s) * acc_ref[s] + pick(w_sib, s) * sib_me[i]
-        far[0].wait()
-        for i in range(b):
-            o_ref[i] = (sib_me[i] + pick(g, me * b + i) * y_acc[i]).astype(o_ref.dtype)
-
-    block = pltpu.VMEM((b, r, hd), jnp.float32)
-    stats = pltpu.VMEM(ml.shape, jnp.float32)
+        def emit(i, val):
+            o_ref[i] = val.astype(o_ref.dtype)
+
+        merge(acc_ref, ml_ref, scratch, axis, b, emit)
+
     return pl.pallas_call(
         body,
         out_shape=jax.ShapeDtypeStruct((b, r, hd), jnp.bfloat16),
         in_specs=[pl.BlockSpec(memory_space=pltpu.VMEM)] * 2,
         out_specs=pl.BlockSpec(memory_space=pltpu.VMEM),
-        scratch_shapes=[block, block, stats, block, stats, block, stats,
-                        pltpu.SemaphoreType.DMA((5,)), pltpu.SemaphoreType.DMA((5,))],
+        scratch_shapes=merge_scratch(b, r, hd, ml.shape),
         compiler_params=pltpu.CompilerParams(collective_id=cid, has_side_effects=True),
-        cost_estimate=pl.CostEstimate(flops=1_000_000_000, bytes_accessed=2_000_000, transcendentals=0),
+        cost_estimate=SMALL,
         name="combine",
     )(acc, ml)
 
 
 def mlp_pair(attn, hidden, w_out, w_up, w_down, w_next, layer, cid):
-    rows, d = attn.shape
+    rows, d = hidden.shape
+    fused = isinstance(attn, tuple)
     ff = w_up.shape[2]
     r = -(-rows // 32) * 32
     tile = 512
@@ -361,13 +382,28 @@
     halves = [w.shape[2] // 2 for w in w_next]
     parts = [(w, t * tile) for w, h in enumerate(halves) for t in range(h // tile)]
     n_p, p_half = len(parts), sum(halves)
-    attn, hidden = (jnp.pad(t, ((0, r - rows), (0, 0))) for t in (attn, hidden))
-
-    def body(attn_ref, hid_ref, wo_ref, wu_ref, wd_ref, *rest):
+    pad = lambda t: jnp.pad(t, ((0, r - rows), (0, 0)))
+    hidden = pad(hidden)
+    first_in = list(attn) if fused else [pad(attn)]
+    merge_in = []
+    if fused:
+        acc_rows, qr, hd = attn[0].shape
+        b = acc_rows // 4
+        merge_in = [pltpu.VMEM((r, d), jnp.float32), pltpu.VMEM((r, d), jnp.bfloat16)] + merge_scratch(b, qr, hd, attn[1].shape)
+
+    def body(*rest):
+        if fused:
+            (acc_ref, ml_ref), rest = rest[:2], rest[2:]
+        else:
+            attn_ref, rest = rest[0], rest[1:]
+        hid_ref, wo_ref, wu_ref, wd_ref = rest[:4]
+        rest = rest[4:]
         wn_refs, rest = rest[:len(w_next)], rest[len(w_next):]
         o_ref, rest = rest[0], rest[1:]
         if n_p:
             p_ref, p_to, p_in, rest = rest[0], rest[1], rest[2], rest[3:]
+        if fused:
+            x_f32, attn_ref, scratch, rest = rest[0], rest[1], rest[2:len(merge_in)], rest[len(merge_in):]
         x_all, h_all, hm, act, acc, rx, wc, wr, csem, rsem, ssem, qsem = rest
         me = lax.axis_index('kv')
         core = lax.rem(me, 2)
@@ -396,9 +432,18 @@
         for c in range(ring_c):
             col(c, c < n_o).start()
 
-        barrier = pltpu.get_barrier_semaphore()
-        pl.semaphore_signal(barrier, inc=1, device_id={'kv': peer}, device_id_type=MESH_ID)
-        pl.semaphore_wait(barrier, 1)
+        enter('kv', (peer, around(me)[1]) if fused else (peer,))
+        if fused:
+            x_f32[...] = jnp.zeros_like(x_f32)
+
+            def emit(i, val):
+                for t in range(2):
+                    for h in range(d // hd):
+                        k = t * (d // hd) + h
+                        x_f32[t * b + i:t * b + i + 1, h * hd:(h + 1) * hd] = val[k:k + 1]
+
+            merge(acc_ref, ml_ref, scratch, 'kv', b, emit)
+            attn_ref[...] = x_f32[...].astype(attn_ref.dtype)
 
         def send(src, dst, i):
             return pltpu.make_async_remote_copy(
@@ -507,9 +552,9 @@
     out = pl.pallas_call(
         body,
         out_shape=out_shape,
-        in_specs=[vmem, vmem] + [any_spec] * (3 + len(w_next)),
+        in_specs=[vmem] * (len(first_in) + 1) + [any_spec] * (3 + len(w_next)),
         out_specs=[vmem] * len(out_shape),
-        scratch_shapes=extra + [
+        scratch_shapes=extra + merge_in + [
             pltpu.VMEM((2 * r, d), jnp.bfloat16), pltpu.VMEM((2 * r, d), jnp.bfloat16), pltpu.VMEM((2 * r, d), jnp.bfloat16),
             pltpu.VMEM((2 * r, f_half), jnp.bfloat16), pltpu.VMEM((2 * r, d), jnp.float32), pltpu.VMEM((r, d), jnp.float32),
             pltpu.VMEM((ring_c, d, tile), jnp.bfloat16), pltpu.VMEM((ring_r, tile, d), jnp.bfloat16),
@@ -517,8 +562,8 @@
             pltpu.SemaphoreType.DMA((6,)), pltpu.SemaphoreType.DMA((6,)),
         ],
         compiler_params=pltpu.CompilerParams(collective_id=cid, has_side_effects=True, vmem_limit_bytes=58 * 1024 * 1024),
-        cost_estimate=pl.CostEstimate(flops=6_000_000_000, bytes_accessed=60_000_000, transcendentals=0),
-    )(attn, hidden, w_out, w_up, w_down, *w_next)
+        cost_estimate=cost(6_000_000_000, 60_000_000),
+    )(*first_in, hidden, w_out, w_up, w_down, *w_next)
     return [t[:rows] for t in out]
 
 
@@ -698,7 +743,7 @@
             pltpu.SemaphoreType.DMA((2, n_slots)),
         ],
         input_output_aliases=alias,
-        cost_estimate=pl.CostEstimate(flops=400_000_000, bytes_accessed=16_000_000, transcendentals=0),
+        cost_estimate=cost(400_000_000, 16_000_000),
     )(*operands)
 
 
@@ -849,13 +894,15 @@
             else:
                 srcs = all_units + along_y(hop) + [all_pages(layer)]
                 *pools, acc, ml = attend(*by_use, qkv, [k_rows, v_rows], srcs, 0, pools, None, part=0, **dims)
-            o = combine(acc, ml, 'kv', n_cols, 1)
             if layer + 1 < layers:
+                o = combine(acc, ml, 'kv', n_cols, 1)
                 next_got, o = lax.optimization_barrier((next_got, o))
                 all_units = swap(units[layer + 1], next_got)
                 hop, = pick(y_list, all_units, [Y_CORE])
                 hop, o = lax.optimization_barrier((hop, o))
-            attn_out = jnp.swapaxes(o.reshape(seq_dev, 2, heads * head_dim), 0, 1).reshape(2 * seq_dev, heads * head_dim)
+                attn_out = jnp.swapaxes(o.reshape(seq_dev, 2, heads * head_dim), 0, 1).reshape(2 * seq_dev, heads * head_dim)
+            else:
+                attn_out = (acc, ml)
             w_next = (w_query, w_key, w_value) if layer + 1 < layers else ()
             hidden, *ahead = mlp_pair(attn_out, hidden, w_out, w_up, w_down, w_next, layer, 3 + layer)
             ahead = ahead[0] if ahead else None

time: 375 us -> 404 us (1.077)
  waiting for transfers between devices: 98.2 us -> 142 us
  Pallas kernels: 200 us -> 194 us
  other arithmetic: 17.4 us -> 11.7 us
    ppermute x2, waiting for transfers between devices: 28.7 us -> 56 us  [along_y(): got = lax.ppermute(hop, 'kv', over)]
    pallas_call x2 -> x1, Pallas kernels: 49.3 us -> 26 us  [combine(): pl.pallas_call(body, out_shape=jax.ShapeDtypeStruct((b, r, hd), jnp.bfloa...]
    pallas_call x2, Pallas kernels: 56.5 us -> 74.3 us  [mlp_pair(): pl.pallas_call(body, out_shape=out_shape, in_specs=[vmem] * (len(first_in...]
    ppermute x6, waiting for transfers between devices: 61.4 us -> 78.4 us  [along_z(): got.append(lax.ppermute(h, 'kv2', z))]
  transfers between devices with their start and end apart: 19 -> 19, of which waited for: 11 -> 12; matrix products, arithmetic and copies ran while one was open for 4% -> 3% of each run, Pallas kernels for 32% -> 27%
where the time goes in v6:
time: 404 us; the launch traced here: 403 us
  Pallas kernels  194 us (48%)
  waiting for transfers between devices  142 us (35%)
  between operations  15.9 us (4%)
  matrix products  15.2 us (4%)
  starting transfers between devices  13.2 us (3%)
  other arithmetic  11.7 us (3%)
  local copies, waits for them, and re-layouts  10.5 us (3%)
    ppermute x6, waiting for transfers between devices, along_z(): got.append(lax.ppermute(h, 'kv2', z))  78.4 us
    pallas_call x2, Pallas kernels, mlp_pair(): pl.pallas_call(body, out_shape=out_shape, in_specs=[vmem] * (len(first_in...  74.3 us
    ppermute x2, waiting for transfers between devices, along_y(): got = lax.ppermute(hop, 'kv', over)  56 us
    pallas_call x4, Pallas kernels, attend(): pl.pallas_call(body, out_shape=[pool, pool, jax.ShapeDtypeStruct((n_seq +...  33.4 us
    pallas_call x1, Pallas kernels, combine(): pl.pallas_call(body, out_shape=jax.ShapeDtypeStruct((b, r, hd), jnp.bfloa...  26 us
    pallas_call x2, Pallas kernels, gather_rows(): pl.pallas_call(body, out_shape=jax.ShapeDtypeStruct((n,) + x.shape, x.dty...  23.5 us
    pallas_call x4, Pallas kernels, pick(): pl.pallas_call(body, out_shape=[jax.ShapeDtypeStruct((size,) + tail, dtyp...  16.2 us
    dot_general x3, matrix products, per_device(): dot = lambda a, w: jnp.dot(a, w[layer], preferred_element_type=jnp.float32)  15.2 us
  transfers between devices with their start and end apart: 19, of which 12 were waited for; matrix products, arithmetic and copies ran while one was open for 3% of the time, Pallas kernels for 27%

profile of v6, /device:TPU:9, one launch (start us, length us, event | category | flops | bytes accessed | tf_op | source)
XLA Modules:
  0.0 403.3 jit_solution(3100768843691921138)
XLA Ops:
  8.4 3.2 take_pages.1
  13.3 9.3 %share_plan.1 = s32[32,1,128]{2,1,0:T(1,128)} custom-call(s32[1,128]{1,0:T(1,128)} %pad_bitcast_fusion.x_ref), custom_call_target="tpu_custom_call" | custom-call | tf_op jit(solution)/shard_map/share_plan/pallas_call | solution.py:142
  23.9 1.7 route_z.1.idx_ref
  25.6 5.0 %shard_map.148 = (bf16[6,512,128]{2,1,0:T(8,128)(2,1)}, bf16[6,512,128]{2,1,0:T(8,128)(2,1)}, bf16[6,512,128]{2,1,0:T(8,128)(2,1)}) custom-call(s32[64]{0:T(128)} %route_z.1.idx_ref, bf16[12,512,128]{2,1,0:T(8,128)(2,1)S(1)} %get-tuple-element.74.rest_0_, bf16[12,512,128]{2,1,0:T(8,128)(2,1)} %collective-permute-done.1.rest_1_), custom_call_target="tpu_custom_call" | custom-call | flops 100000000 | bytes 4000000 | tf_op jit(solution)/shard_map/pallas_call | solution.py:106
  36.3 6.9 %route.1 = (s32[64]{0:T(128)}, s32[64]{0:T(128)}) custom-call(s32[192]{0:T(256)} %copy-done.10, s32[192]{0:T(256)} %reshape.240.dev_ref, s32[2]{0:T(128)} %pad_add_fusion.2.pos_ref), custom_call_target="tpu_custom_call" | custom-call | flops 100000000 | bytes 4000000 | tf_op jit(solution)/shard_map/route/pallas_call | solution.py:244
  43.3 3.7 fusion.24
  47.0 3.7 fusion.21
  50.7 7.7 %fusion.12 = bf16[3,8,24,128]{3,1,2,0:T(8,128)(2,1)S(1)} fusion(bf16[24,3072]{1,0:T(8,128)(2,1)S(1)} %reshape.237, bf16[2,3072,3072]{2,1,0:T(8,128)(2,1)} %rest_5_.2), kind=kOutput, calls=%fused_computation.12 | convolution fusion | flops 453058560 | bytes 19169280 | tf_op jit(solution)/shard_map/dot_general | solution.py:874
  59.3 12.1 %gather_rows.2 = bf16[4,12,80,128]{3,2,1,0:T(8,128)(2,1)} custom-call(bf16[12,80,128]{2,1,0:T(8,128)(2,1)} %pad_maximum_fusion.x_ref), custom_call_target="tpu_custom_call" | custom-call | flops 100000000 | bytes 4000000 | tf_op jit(solution)/shard_map/gather_rows/pallas_call | solution.py:283
  72.5 1.6 collective-permute-start.3
  79.2 10.6 %shard_map.149 = (bf16[120,256,128]{2,1,0:T(8,128)(2,1)}, bf16[120,256,128]{2,1,0:T(8,128)(2,1)}, f32[49,48,128]{2,1,0:T(8,128)}, f32[2,48,128]{2,1,0:T(8,128)}) custom-call(s32[4,64]{1,0:T(4,128)} %pad_add_fusion.info_ref, s32[6]{0:T(128)} %convert_reduce_fusion.4.cnt_ref, bf16[48,80,128]{2,1,0:T(8,128)(2,1)} %bitcast.108, ...), custom_call_target="tpu_custom_call" | custom-call | flops 400000000 | bytes 16000000 | tf_op jit(solution)/shard_map/pallas_call | solution.py:732
  91.0 5.0 %shard_map.150 = (bf16[6,512,128]{2,1,0:T(8,128)(2,1)}, bf16[6,512,128]{2,1,0:T(8,128)(2,1)}, bf16[6,512,128]{2,1,0:T(8,128)(2,1)}) custom-call(s32[64]{0:T(128)} %route_z.1.idx_ref, bf16[12,512,128]{2,1,0:T(8,128)(2,1)S(1)} %get-tuple-element.88.rest_0_.rest_2_, bf16[12,512,128]{2,1,0:T(8,128)(2,1)} %collective-permute-done.5.rest_1_.rest_3_), custom_call_target="tpu_custom_call" | custom-call | flops 100000000 | bytes 4000000 | tf_op jit(solution)/shard_map/pallas_call | solution.py:106
  96.1 43.8 %collective-permute-done.3.rest_3_ = bf16[6,512,128]{2,1,0:T(8,128)(2,1)} collective-permute-done((bf16[6,512,128]{2,1,0:T(8,128)(2,1)}, bf16[6,512,128]{2,1,0:T(8,128)(2,1)}, u32[]{:S(2)}, u32[]{:S(2)}) %collective-permute-start.3) | collective-permute-done | bytes 786464 | tf_op jit(solution)/shard_map/ppermute | solution.py:825
  139.9 3.1 collective-permute-done.4.rest_4_
  144.0 1.7 collective-permute-done.10.rest_6_
  148.0 3.1 shard_map.151
  151.8 29.5 %collective-permute-done.12.rest_0_ = bf16[10,512,128]{2,1,0:T(8,128)(2,1)} collective-permute-done((bf16[10,512,128]{2,1,0:T(8,128)(2,1)}, bf16[10,512,128]{2,1,0:T(8,128)(2,1)}, u32[]{:S(2)}, u32[]{:S(2)}) %collective-permute-start.12) | collective-permute-done | bytes 1310752 | tf_op jit(solution)/shard_map/ppermute | solution.py:832
  181.3 1.4 collective-permute-start.13
  183.4 1.5 collective-permute-start.8
  184.9 4.9 %shard_map.152 = (bf16[120,256,128]{2,1,0:T(8,128)(2,1)}, bf16[120,256,128]{2,1,0:T(8,128)(2,1)}, f32[49,48,128]{2,1,0:T(8,128)}, f32[2,48,128]{2,1,0:T(8,128)}) custom-call(s32[4,64]{1,0:T(4,128)} %pad_add_fusion.info_ref, s32[6]{0:T(128)} %convert_reduce_fusion.4.cnt_ref, ...), custom_call_target="tpu_custom_call", output_to_operand_aliasing={{0}: (11, {}), {1}: (12, {})} | custom-call | flops 400000000 | bytes 16000000 | tf_op jit(solution)/shard_map/pallas_call | solution.py:732
  189.8 5.0 %shard_map.153 = (bf16[120,256,128]{2,1,0:T(8,128)(2,1)}, bf16[120,256,128]{2,1,0:T(8,128)(2,1)}, f32[49,48,128]{2,1,0:T(8,128)}, f32[2,48,128]{2,1,0:T(8,128)}) custom-call(s32[4,64]{1,0:T(4,128)} %pad_add_fusion.info_ref, s32[6]{0:T(128)} %convert_reduce_fusion.4.cnt_ref, ...), custom_call_target="tpu_custom_call", output_to_operand_aliasing={{0}: (6, {}), {1}: (7, {})} | custom-call | flops 400000000 | bytes 16000000 | tf_op jit(solution)/shard_map/pallas_call | solution.py:732
  194.8 26.0 %combine.1 = bf16[12,48,128]{2,1,0:T(8,128)(2,1)} custom-call(f32[49,48,128]{2,1,0:T(8,128)} %get-tuple-element.109.acc_ref, f32[2,48,128]{2,1,0:T(8,128)} %get-tuple-element.110.ml_ref), custom_call_target="tpu_custom_call" | custom-call | flops 100000000 | bytes 4000000 | tf_op jit(solution)/shard_map/combine/pallas_call | solution.py:361
  220.9 29.8 %collective-permute-done.7.rest_3_.rest_5_ = bf16[6,512,128]{2,1,0:T(8,128)(2,1)} collective-permute-done((bf16[6,512,128]{2,1,0:T(8,128)(2,1)}, bf16[6,512,128]{2,1,0:T(8,128)(2,1)}, u32[]{:S(2)}, u32[]{:S(2)}) %collective-permute-start.7) | collective-permute-done | bytes 786464 | tf_op jit(solution)/shard_map/ppermute | solution.py:825
  250.7 1.6 collective-permute-done.8.rest_4_.rest_6_
  253.3 1.6 collective-permute-done.14.rest_5_.rest_7_
  257.3 3.1 shard_map.154
  264.0 26.5 %collective-permute-done.17.rest_10_ = bf16[10,512,128]{2,1,0:T(8,128)(2,1)S(1)} collective-permute-done((bf16[10,512,128]{2,1,0:T(8,128)(2,1)}, bf16[10,512,128]{2,1,0:T(8,128)(2,1)S(1)}, u32[]{:S(2)}, u32[]{:S(2)}) %collective-permute-start.17) | collective-permute-done | bytes 1310752 | tf_op jit(solution)/shard_map/ppermute | solution.py:832
  291.9 33.1 %shard_map.155 = (bf16[32,3072]{1,0:T(8,128)(2,1)}, bf16[32,5120]{1,0:T(8,128)(2,1)}) custom-call(bf16[32,3072]{1,0:T(8,128)(2,1)} %pad.15.rest_0_, bf16[32,3072]{1,0:T(8,128)(2,1)} %pad.16.rest_1_, bf16[2,3072,3072]{2,1,0:T(8,128)(2,1)} %rest_3_.3, bf16[2,3072,8192]{2,1,0:T(8,128)(2,1)} %rest_4_.3, bf16[2,8192,3072]{2,1,0:T(8,128)(2,1)} %rest_5_.3, ...), custom_call_target="tpu_custom_call" | custom-call | flops 6000000000 | bytes 60000000 | tf_op jit(solution)/shard_map/pallas_call | solution.py:552
  327.6 11.3 %gather_rows.3 = bf16[4,12,80,128]{3,2,1,0:T(8,128)(2,1)} custom-call(bf16[12,80,128]{2,1,0:T(8,128)(2,1)} %pad_maximum_fusion.1.x_ref), custom_call_target="tpu_custom_call" | custom-call | flops 100000000 | bytes 4000000 | tf_op jit(solution)/shard_map/gather_rows/pallas_call | solution.py:283
  338.9 1.7 broadcast_select_fusion.rest_2_
  340.6 12.8 %shard_map.156 = (bf16[120,256,128]{2,1,0:T(8,128)(2,1)}, bf16[120,256,128]{2,1,0:T(8,128)(2,1)}, f32[49,48,128]{2,1,0:T(8,128)}, f32[2,48,128]{2,1,0:T(8,128)}) custom-call(s32[4,64]{1,0:T(4,128)} %pad_add_fusion.1.info_ref, s32[2]{0:T(128)} %fusion.35.cnt_ref, bf16[48,80,128]{2,1,0:T(8,128)(2,1)} %bitcast.111, ...), custom_call_target="tpu_custom_call", output_to_operand_aliasing={{0}: (16, {}), {1}: (17, {})} | custom-call | flops 400000000 | bytes 16000000 | tf_op jit(solution)/shard_map/pallas_call | solution.py:732
  353.4 41.2 %shard_map.157 = bf16[32,3072]{1,0:T(8,128)(2,1)} custom-call(f32[49,48,128]{2,1,0:T(8,128)} %get-tuple-element.120.rest_0_, f32[2,48,128]{2,1,0:T(8,128)} %get-tuple-element.121.rest_1_, bf16[32,3072]{1,0:T(8,128)(2,1)} %broadcast_select_fusion.rest_2_, bf16[2,3072,3072]{2,1,0:T(8,128)(2,1)} %rest_3_.3, bf16[2,3072,8192]{2,1,0:T(8,128)(2,1)} %rest_4_.3, ...), custom_call_target="tpu_custom_call" | custom-call | flops 6000000000 | bytes 60000000 | tf_op jit(solution)/shard_map/pallas_call | solution.py:552
  (138 shorter events, 33.9 us)
Async XLA Ops:
  8.3 4.0 copy-start.17
  8.3 4.1 %copy-start.13 = (s32[12,2]{0,1:T(2,128)S(1)}, s32[12,2]{0,1:T(2,128)}, u32[]{:S(2)}) copy-start(s32[12,2]{0,1:T(2,128)} %param.26) | copy-start | bytes 292
  8.3 4.3 %copy-start.16 = (s32[12]{0:T(128)S(1)}, s32[12]{0:T(128)}, u32[]{:S(2)}) copy-start(s32[12]{0:T(128)} %param.28) | copy-start | bytes 148
  8.3 4.3 %copy-start.18 = (s32[12]{0:T(128)S(1)}, s32[12]{0:T(128)}, u32[]{:S(2)}) copy-start(s32[12]{0:T(128)} %param.27) | copy-start | bytes 148
  8.4 14.8 %copy-start.9 = (bf16[2,12,3072]{2,0,1:T(2,128)(2,1)S(1)}, bf16[2,12,3072]{2,0,1:T(2,128)(2,1)}, u32[]{:S(2)}) copy-start(bf16[2,12,3072]{2,0,1:T(2,128)(2,1)} %param.17) | copy-start | bytes 442372
  11.6 173.3 %copy-start.3 = (bf16[12,512,128]{2,1,0:T(8,128)(2,1)}, bf16[12,512,128]{2,1,0:T(8,128)(2,1)S(1)}, u32[]{:S(2)}) copy-start(bf16[12,512,128]{2,1,0:T(8,128)(2,1)S(1)} %get-tuple-element.74.rest_0_) | copy-start | bytes 4718596
  11.6 250.6 %copy-start = (bf16[12,512,128]{2,1,0:T(8,128)(2,1)}, bf16[12,512,128]{2,1,0:T(8,128)(2,1)S(1)}, u32[]{:S(2)}) copy-start(bf16[12,512,128]{2,1,0:T(8,128)(2,1)S(1)} %get-tuple-element.88.rest_0_.rest_2_) | copy-start | bytes 4718596
  11.6 14.0 %collective-permute-start.1 = (bf16[12,512,128]{2,1,0:T(8,128)(2,1)S(1)}, bf16[12,512,128]{2,1,0:T(8,128)(2,1)}, u32[]{:S(2)}, u32[]{:S(2)}) collective-permute-start(bf16[12,512,128]{2,1,0:T(8,128)(2,1)S(1)} %get-tuple-element.74.rest_0_), channel_id=1, source_target_pairs={{0,1},{1,0},{2,3},{3,2},{4,5},{5,4},{6,7},{7,6},{8,9},{9,8},{10,11... | collective-permute-start | bytes 4718600 | tf_op jit(solution)/shard_map/ppermute | solution.py:783
  12.4 11.0 %copy-start.12 = (s32[12]{0:T(128)}, s32[12]{0:T(128)S(1)}, u32[]{:S(2)}) copy-start(s32[12]{0:T(128)S(1)} %and_select_fusion.5.own_ref) | copy-start | bytes 148
  12.4 10.9 %collective-permute-start = (s32[12]{0:T(128)S(1)}, s32[12]{0:T(128)S(1)}, u32[]{:S(2)}, u32[]{:S(2)}) collective-permute-start(s32[12]{0:T(128)S(1)} %and_select_fusion.5.own_ref), channel_id=1, source_target_pairs={{0,1},{1,0},{2,3},{3,2},{4,5},{5,4},{6,7},{7,6},{8,9},{9,8},{10,11... | collective-permute-start | bytes 152 | tf_op jit(solution)/shard_map/ppermute | solution.py:784
  50.7 26.5 %copy-start.11 = (s32[192]{0:T(256)S(1)}, s32[192]{0:T(256)}, u32[]{:S(2)}) copy-start(s32[192]{0:T(256)} %copy-done.10) | copy-start | bytes 2308
  50.7 26.7 %copy-start.15 = (s32[64]{0:T(128)S(1)}, s32[64]{0:T(128)}, u32[]{:S(2)}) copy-start(s32[64]{0:T(128)} %get-tuple-element.84) | copy-start | bytes 772
  71.4 19.6 %collective-permute-start.5 = (bf16[12,512,128]{2,1,0:T(8,128)(2,1)S(1)}, bf16[12,512,128]{2,1,0:T(8,128)(2,1)}, u32[]{:S(2)}, u32[]{:S(2)}) collective-permute-start(bf16[12,512,128]{2,1,0:T(8,128)(2,1)S(1)} %get-tuple-element.88.rest_0_.rest_2_), channel_id=1, source_target_pairs={{0,1},{1,0},{2,3},{3,2},{4,5},{5,4},{6,7},{7,6},{8,9},{9,8},{10,11... | collective-permute-start | bytes 4718600 | tf_op jit(solution)/shard_map/ppermute | solution.py:799
  71.6 24.5 %collective-permute-start.2 = (bf16[6,512,128]{2,1,0:T(8,128)(2,1)}, bf16[6,512,128]{2,1,0:T(8,128)(2,1)}, u32[]{:S(2)}, u32[]{:S(2)}) collective-permute-start(bf16[6,512,128]{2,1,0:T(8,128)(2,1)} %get-tuple-element.80), channel_id=1, source_target_pairs={{0,4},{4,8},{8,12},{12,0},{1,5},{5,9},{9,13},{13,1},{2,6},{6,10},{... | collective-permute-start | bytes 2359304 | tf_op jit(solution)/shard_map/ppermute | solution.py:825
  72.5 67.4 %collective-permute-start.3 = (bf16[6,512,128]{2,1,0:T(8,128)(2,1)}, bf16[6,512,128]{2,1,0:T(8,128)(2,1)}, u32[]{:S(2)}, u32[]{:S(2)}) collective-permute-start(bf16[6,512,128]{2,1,0:T(8,128)(2,1)} %get-tuple-element.81), channel_id=1, source_target_pairs={{0,8},{4,12},{8,0},{12,4},{1,9},{5,13},{9,1},{13,5},{2,10},{6,14},... | collective-permute-start | bytes 2359304 | tf_op jit(solution)/shard_map/ppermute | solution.py:825
  74.1 68.9 %collective-permute-start.4 = (bf16[6,512,128]{2,1,0:T(8,128)(2,1)}, bf16[6,512,128]{2,1,0:T(8,128)(2,1)}, u32[]{:S(2)}, u32[]{:S(2)}) collective-permute-start(bf16[6,512,128]{2,1,0:T(8,128)(2,1)} %get-tuple-element.82), channel_id=1, source_target_pairs={{0,12},{4,0},{8,4},{12,8},{1,13},{5,1},{9,5},{13,9},{2,14},{6,2},{... | collective-permute-start | bytes 2359304 | tf_op jit(solution)/shard_map/ppermute | solution.py:825
  143.0 2.7 collective-permute-start.10
  143.5 3.4 collective-permute-start.11
  143.5 4.5 %collective-permute-start.9 = (bf16[6,512,128]{2,1,0:T(8,128)(2,1)}, bf16[6,512,128]{2,1,0:T(8,128)(2,1)}, u32[]{:S(2)}, u32[]{:S(2)}) collective-permute-start(bf16[6,512,128]{2,1,0:T(8,128)(2,1)} %collective-permute-done.2.rest_2_), channel_id=1, source_target_pairs={{0,1},{1,0},{2,3},{3,2},{4,5},{5,4},{6,7},{7,6},{8,9},{9,8},{10,11... | collective-permute-start | bytes 2359304 | tf_op jit(solution)/shard_map/ppermute | solution.py:829
  151.1 30.2 %collective-permute-start.12 = (bf16[10,512,128]{2,1,0:T(8,128)(2,1)}, bf16[10,512,128]{2,1,0:T(8,128)(2,1)}, u32[]{:S(2)}, u32[]{:S(2)}) collective-permute-start(bf16[10,512,128]{2,1,0:T(8,128)(2,1)} %shard_map.151), channel_id=1, source_target_pairs={{0,2},{1,3},{2,0},{3,1},{4,6},{5,7},{6,4},{7,5},{8,10},{9,11},{10,... | collective-permute-start | bytes 3932168 | tf_op jit(solution)/shard_map/ppermute | solution.py:832
  181.3 8.5 %collective-permute-start.13 = (bf16[10,512,128]{2,1,0:T(8,128)(2,1)}, bf16[10,512,128]{2,1,0:T(8,128)(2,1)}, u32[]{:S(2)}, u32[]{:S(2)}) collective-permute-start(bf16[10,512,128]{2,1,0:T(8,128)(2,1)} %collective-permute-done.12.rest_0_), channel_id=1, source_target_pairs={{0,1},{1,0},{2,3},{3,2},{4,5},{5,4},{6,7},{7,6},{8,9},{9,8},{10,11... | collective-permute-start | bytes 3932168 | tf_op jit(solution)/shard_map/ppermute | solution.py:833
  182.7 38.2 %collective-permute-start.6 = (bf16[6,512,128]{2,1,0:T(8,128)(2,1)}, bf16[6,512,128]{2,1,0:T(8,128)(2,1)}, u32[]{:S(2)}, u32[]{:S(2)}) collective-permute-start(bf16[6,512,128]{2,1,0:T(8,128)(2,1)} %get-tuple-element.95), channel_id=1, source_target_pairs={{0,4},{4,8},{8,12},{12,0},{1,5},{5,9},{9,13},{13,1},{2,6},{6,10},{... | collective-permute-start | bytes 2359304 | tf_op jit(solution)/shard_map/ppermute | solution.py:825
  182.7 68.0 %collective-permute-start.7 = (bf16[6,512,128]{2,1,0:T(8,128)(2,1)}, bf16[6,512,128]{2,1,0:T(8,128)(2,1)}, u32[]{:S(2)}, u32[]{:S(2)}) collective-permute-start(bf16[6,512,128]{2,1,0:T(8,128)(2,1)} %get-tuple-element.96), channel_id=1, source_target_pairs={{0,8},{4,12},{8,0},{12,4},{1,9},{5,13},{9,1},{13,5},{2,10},{6,14},... | collective-permute-start | bytes 2359304 | tf_op jit(solution)/shard_map/ppermute | solution.py:825
  183.4 68.9 %collective-permute-start.8 = (bf16[6,512,128]{2,1,0:T(8,128)(2,1)}, bf16[6,512,128]{2,1,0:T(8,128)(2,1)}, u32[]{:S(2)}, u32[]{:S(2)}) collective-permute-start(bf16[6,512,128]{2,1,0:T(8,128)(2,1)} %get-tuple-element.97), channel_id=1, source_target_pairs={{0,12},{4,0},{8,4},{12,8},{1,13},{5,1},{9,5},{13,9},{2,14},{6,2},{... | collective-permute-start | bytes 2359304 | tf_op jit(solution)/shard_map/ppermute | solution.py:825
  252.3 2.6 collective-permute-start.14
  252.8 3.2 collective-permute-start.15
  252.8 4.5 %collective-permute-start.16 = (bf16[6,512,128]{2,1,0:T(8,128)(2,1)}, bf16[6,512,128]{2,1,0:T(8,128)(2,1)}, u32[]{:S(2)}, u32[]{:S(2)}) collective-permute-start(bf16[6,512,128]{2,1,0:T(8,128)(2,1)} %collective-permute-done.8.rest_4_.rest_6_), channel_id=1, source_target_pairs={{0,1},{1,0},{2,3},{3,2},{4,5},{5,4},{6,7},{7,6},{8,9},{9,8},{10,11... | collective-permute-start | bytes 2359304 | tf_op jit(solution)/shard_map/ppermute | solution.py:829
  260.4 30.1 %collective-permute-start.17 = (bf16[10,512,128]{2,1,0:T(8,128)(2,1)}, bf16[10,512,128]{2,1,0:T(8,128)(2,1)S(1)}, u32[]{:S(2)}, u32[]{:S(2)}) collective-permute-start(bf16[10,512,128]{2,1,0:T(8,128)(2,1)} %shard_map.154), channel_id=1, source_target_pairs={{0,2},{1,3},{2,0},{3,1},{4,6},{5,7},{6,4},{7,5},{8,10},{9,11},{10,... | collective-permute-start | bytes 3932168 | tf_op jit(solution)/shard_map/ppermute | solution.py:832
  264.0 74.9 %copy-start.14 = (pred[32]{0:T(512)(128)(4,1)S(1)}, pred[32]{0:T(512)(128)(4,1)}, u32[]{:S(2)}) copy-start(pred[32]{0:T(512)(128)(4,1)} %constant.149.clone.1) | copy-start | bytes 100
  264.0 76.7 %copy-start.1 = (bf16[12,512,128]{2,1,0:T(8,128)(2,1)S(1)}, bf16[12,512,128]{2,1,0:T(8,128)(2,1)}, u32[]{:S(2)}) copy-start(bf16[12,512,128]{2,1,0:T(8,128)(2,1)} %copy-done) | copy-start | bytes 4718596
  290.5 34.4 %copy-start.7 = (bf16[10,512,128]{2,1,0:T(8,128)(2,1)}, bf16[10,512,128]{2,1,0:T(8,128)(2,1)S(1)}, u32[]{:S(2)}) copy-start(bf16[10,512,128]{2,1,0:T(8,128)(2,1)S(1)} %collective-permute-done.17.rest_10_) | copy-start | bytes 3932164
  290.5 50.1 %collective-permute-start.18 = (bf16[10,512,128]{2,1,0:T(8,128)(2,1)S(1)}, bf16[10,512,128]{2,1,0:T(8,128)(2,1)}, u32[]{:S(2)}, u32[]{:S(2)}) collective-permute-start(bf16[10,512,128]{2,1,0:T(8,128)(2,1)S(1)} %collective-permute-done.17.rest_10_), channel_id=1, source_target_pairs={{0,1},{1,0},{2,3},{3,2},{4,5},{5,4},{6,7},{7,6},{8,9},{9,8},{10,11... | collective-permute-start | bytes 3932168 | tf_op jit(solution)/shard_map/ppermute | solution.py:833
  (5 other events, 6.3 us)
